TPU v7x, 8 devices: a whole 2x2x1 slice. The times are simulated.
8 devices in a mesh: dp: 2 (over z, y), tp: 4 (over x, core).
Axes of the slice: x: 2, y: 2, z: 1, core: 2. Of those that a mesh axis runs over, the one named last changes fastest.
Arguments:
- hidden: bfloat16 [12, 1024, 2048], P('dp', 'tp'), parts along dimension 0
- grad_out: bfloat16 [12, 1024, 2048], P('dp', 'tp'), parts along dimension 0
- prefix_len: int32 [12], P('dp'), parts along dimension 0
- valid_len: int32 [12], P('dp'), parts along dimension 0
- attn_norm: bfloat16 [2048], replicated
- w_query: bfloat16 [2048, 2048], P(None, 'tp')
- w_key: bfloat16 [2048, 256], replicated
- w_value: bfloat16 [2048, 256], replicated
- w_out: bfloat16 [2048, 2048], P('tp')
- mlp_norm: bfloat16 [2048], replicated
- w_gate: bfloat16 [2048, 16384], P(None, 'tp')
- w_up: bfloat16 [2048, 16384], P(None, 'tp')
- w_down: bfloat16 [16384, 2048], P('tp')
Outputs:
- output 1: bfloat16 [12, 1024, 2048], P('dp', 'tp'), parts along dimension 0
- output 2: bfloat16 [12, 1024, 2048], P('dp', 'tp'), parts along dimension 0
- output 3: float32 [4096], P('dp'), parts along dimension 0
- output 4: float32 [4096, 2048], P('dp', 'tp'), parts along dimension 0
- output 5: float32 [4096, 256], P('dp'), parts along dimension 0
- output 6: float32 [4096, 256], P('dp'), parts along dimension 0
- output 7: float32 [4096, 2048], P(('dp', 'tp')), parts along dimension 0
- output 8: float32 [4096], P('dp'), parts along dimension 0
- output 9: float32 [4096, 16384], P('dp', 'tp'), parts along dimension 0
- output 10: float32 [4096, 16384], P('dp', 'tp'), parts along dimension 0
- output 11: float32 [32768, 2048], P(('dp', 'tp')), parts along dimension 0
There are 2 independent parts. A program takes and returns all parts, laid end to end along the dimension named above; an argument that names none is the same for every part.
All inputs are finite; a program needn't handle non-finite values.
Results may differ from a plain program's by a relative error of at most 0.02.
Values are sent between devices in bfloat16 or wider.
A program may use at most 1 GiB of HBM per device.

v0:
```python
import functools
import math

import jax
import jax.numpy as jnp
import numpy as np
from jax import lax
from jax.experimental import pallas as pl
from jax.experimental.pallas import tpu as pltpu
from jax.sharding import PartitionSpec as P


EPS = 1e-6
BF = jnp.bfloat16
F32 = jnp.float32
MIB = 1024 * 1024
ANY = pl.BlockSpec(memory_space=pl.ANY)


def dot_nn(a, b):
    return lax.dot_general(a, b, (((1,), (0,)), ((), ())), preferred_element_type=F32)


def dot_nt(a, b):
    return lax.dot_general(a, b, (((1,), (1,)), ((), ())), preferred_element_type=F32)


def dot_tn(a, b):
    return lax.dot_general(a, b, (((0,), (0,)), ((), ())), preferred_element_type=F32)


def const_spec(shape):
    zeros = (0,) * len(shape)
    return pl.BlockSpec(shape, lambda *_: zeros, pipeline_mode=pl.Buffered(1))


def run(kernel, grid, in_specs, out_specs, out_shape, args, scratch=(), prefetch=0, aliases=None, flops=0, nbytes=0, limit=60):
    spec = pltpu.PrefetchScalarGridSpec(num_scalar_prefetch=prefetch, grid=grid, in_specs=in_specs, out_specs=out_specs, scratch_shapes=scratch)
    return pl.pallas_call(
        kernel,
        grid_spec=spec,
        out_shape=out_shape,
        input_output_aliases=aliases or {},
        compiler_params=pltpu.CompilerParams(dimension_semantics=("arbitrary",) * len(grid), vmem_limit_bytes=limit * MIB),
        cost_estimate=pl.CostEstimate(flops=int(flops), bytes_accessed=int(nbytes), transcendentals=0),
    )(*args)


def rope_fwd(x, cos_t, sin_t):
    half = x.shape[-1] // 2
    a, b = x[:, :half], x[:, half:]
    return a * cos_t - b * sin_t, b * cos_t + a * sin_t


def rope_bwd(a, b, cos_t, sin_t):
    return a * cos_t + b * sin_t, b * cos_t - a * sin_t


def pre_kernel(me_ref, h_ref, gain_ref, wk_ref, wv_ref, cos_ref, sin_ref, u_ref, kv_ref):
    x = h_ref[0].astype(F32)
    inv = lax.rsqrt(jnp.mean(x * x, axis=-1, keepdims=True) + EPS)
    u = (x * inv * gain_ref[...]).astype(BF)
    u_ref[0] = u
    hd = wk_ref.shape[1]
    first, second = rope_fwd(dot_nn(u, wk_ref[...]), cos_ref[...], sin_ref[...])
    kv_ref[0, :, : hd // 2] = first.astype(BF)
    kv_ref[0, :, hd // 2 : hd] = second.astype(BF)
    kv_ref[0, :, hd:] = dot_nn(u, wv_ref[...]).astype(BF)


def attn_fwd_kernel(me_ref, pre_ref, val_ref, u_ref, wq_ref, kv_ref, cos_ref, sin_ref, token_ref, q_ref, pt_ref, mix_ref, vt_ref, s_ref):
    b = pl.program_id(0)
    tp_n, _, cols = wq_ref.shape
    hd = kv_ref.shape[-1] // 2
    seq = kv_ref.shape[0] * kv_ref.shape[2]
    sl = u_ref.shape[1]
    heads = tp_n * cols // hd
    u = u_ref[0]
    cos_t, sin_t = cos_ref[...], sin_ref[...]
    keys = kv_ref[:, 0, :, :hd].reshape(seq, hd)
    vt_ref[...] = kv_ref[:, 0, :, hd:].reshape(seq, hd).astype(F32).T.astype(BF)
    for s in range(tp_n):
        qs = dot_nn(u, wq_ref[s])
        for j in range(cols // hd):
            base = (s * (cols // hd) + j) * hd
            first, second = rope_fwd(qs[:, j * hd : (j + 1) * hd], cos_t, sin_t)
            q_ref[0, :, base : base + hd // 2] = first.astype(BF)
            q_ref[0, :, base + hd // 2 : base + hd] = second.astype(BF)
    prefix, valid = pre_ref[b], val_ref[b]
    q_end = lax.broadcasted_iota(jnp.int32, (1, sl), 1) + (me_ref[0] * sl + 1)
    limit = jnp.minimum(valid, jnp.maximum(prefix, q_end))
    visible = lax.broadcasted_iota(jnp.int32, (seq, sl), 0) < limit
    scale = (hd**-0.5) * math.log2(math.e)

    def scores(h):
        return dot_nt(keys, q_ref[0, :, h * hd : (h + 1) * hd])

    s_ref[0] = scores(0)
    for h in range(heads):
        if h + 1 < heads:
            s_ref[(h + 1) % 2] = scores(h + 1)
        sc = jnp.where(visible, s_ref[h % 2], -1e30)
        top = jnp.max(sc, axis=0, keepdims=True)
        e = jnp.exp2((sc - top) * scale)
        p = (e * (1.0 / jnp.sum(e, axis=0, keepdims=True))).astype(BF)
        pt_ref[0, :, h * sl : (h + 1) * sl] = p
        mix_ref[0, :, h * hd : (h + 1) * hd] = dot_nn(vt_ref[...], p).T.astype(BF)


def out_kernel(mix_ref, wo_ref, h_ref, gain_ref, *rest):
    resid_ref, z_ref = rest[-2:]
    x = (h_ref[0].astype(F32) + dot_nn(mix_ref[0], wo_ref[...])).astype(BF)
    resid_ref[0] = x
    x = x.astype(F32)
    inv = lax.rsqrt(jnp.mean(x * x, axis=-1, keepdims=True) + EPS)
    z_ref[0] = (x * inv * gain_ref[...]).astype(BF)


def place_copies(pieces, cats, sems):
    return [pltpu.make_async_copy(src, dst, sems.at[i]) for i, (src, dst) in enumerate(zip(pieces, cats))]


def start_at_first(copies):
    @pl.when(pl.program_id(0) == 0)
    def _():
        for c in copies:
            c.start()


def wait_at_last(copies):
    @pl.when(pl.program_id(0) == pl.num_programs(0) - 1)
    def _():
        for c in copies:
            c.wait()


def dact_near_kernel(me_ref, ga_ref, gb_ref, wd_ref, *rest):
    da_ref, cat0_ref, cat1_ref, own0_ref, own1_ref, sems = rest[-6:]
    half = ga_ref.shape[0] // 2
    rows, dim = half * ga_ref.shape[1], ga_ref.shape[2]
    chip, core = me_ref[0] // 2, me_ref[0] % 2
    src, dst = [], []
    for c, (cat, own) in enumerate(((cat0_ref, own0_ref), (cat1_ref, own1_ref))):
        mine = ga_ref.at[pl.ds(c * half, half)]
        src += [mine, gb_ref.at[pl.ds(c * half, half)], mine]
        dst += [cat.at[chip, core], cat.at[chip, 1 - core], own]
    copies = place_copies(src, dst, sems)
    start_at_first(copies)
    for c in range(2):
        for rel, ref in enumerate((ga_ref, gb_ref)):
            g = ref[c * half : (c + 1) * half].reshape(rows, dim)
            da_ref[c, rel] = dot_nt(g, wd_ref[...]).astype(BF)
    wait_at_last(copies)


def dact_far_kernel(me_ref, ga_ref, gb_ref, wd_ref, *rest):
    da_ref, cat_ref, sems = rest[-3:]
    rows, dim = ga_ref.shape[0] * ga_ref.shape[1], ga_ref.shape[2]
    chip, core = 1 - me_ref[0] // 2, me_ref[0] % 2
    copies = place_copies([ga_ref, gb_ref], [cat_ref.at[chip, core], cat_ref.at[chip, 1 - core]], sems)
    start_at_first(copies)
    for rel, ref in enumerate((ga_ref, gb_ref)):
        da_ref[0, rel] = dot_nt(ref[...].reshape(rows, dim), wd_ref[...]).astype(BF)
    wait_at_last(copies)


def gated(gate, up, da):
    c0 = math.sqrt(2.0 / math.pi)
    c1 = c0 * 0.044715
    x2 = gate * gate
    hh = 0.5 + 0.5 * jnp.tanh(gate * (c0 + c1 * x2))
    gelu = gate * hh
    slope = hh + gelu * ((1.0 - hh) * (2.0 * c0 + 6.0 * c1 * x2))
    return (gelu * up).astype(BF), (da * up * slope).astype(BF), (da * gelu).astype(BF)


def mlp_kernel(other, me_ref, za_ref, zb_ref, da_ref, wg_ref, wu_ref, *rest):
    act_ref, dg_ref, du_ref, cat_ref, sems = rest[-5:]
    rows, dim = za_ref.shape[0] * za_ref.shape[1], za_ref.shape[2]
    core = me_ref[0] % 2
    chip = abs(other - me_ref[0] // 2)
    copies = place_copies([za_ref, zb_ref], [cat_ref.at[chip, core], cat_ref.at[chip, 1 - core]], sems)
    start_at_first(copies)
    step = rows // 2
    for rel, ref in enumerate((za_ref, zb_ref)):
        place = core if rel == 0 else 1 - core
        z = ref[...].reshape(rows, dim)
        for r in range(0, rows, step):
            zr = z[r : r + step]
            out = gated(dot_nn(zr, wg_ref[...]), dot_nn(zr, wu_ref[...]), da_ref[0, rel, r : r + step, :].astype(F32))
            for o_ref, o in zip((act_ref, dg_ref, du_ref), out):
                o_ref[0, place, r : r + step, :] = o
    wait_at_last(copies)


def mlp_fused_kernel(other, me_ref, za_ref, zb_ref, ga_ref, gb_ref, wg_ref, wu_ref, wd_ref, *rest):
    act_ref, dg_ref, du_ref, zcat_ref, gcat_ref, sems = rest[-6:]
    rows, dim = za_ref.shape[0] * za_ref.shape[1], za_ref.shape[2]
    core = me_ref[0] % 2
    chip = abs(other - me_ref[0] // 2)
    here, there = (chip, core), (chip, 1 - core)
    copies = place_copies([za_ref, zb_ref, ga_ref, gb_ref], [zcat_ref.at[here], zcat_ref.at[there], gcat_ref.at[here], gcat_ref.at[there]], sems)
    start_at_first(copies)
    step = rows // 3
    for rel, (z_ref, g_ref) in enumerate(((za_ref, ga_ref), (zb_ref, gb_ref))):
        place = core if rel == 0 else 1 - core
        z, g = z_ref[...].reshape(rows, dim), g_ref[...].reshape(rows, dim)
        for r in range(0, rows, step):
            zr = z[r : r + step]
            out = gated(dot_nn(zr, wg_ref[...]), dot_nn(zr, wu_ref[...]), dot_nt(g[r : r + step], wd_ref[...]))
            for o_ref, o in zip((act_ref, dg_ref, du_ref), out):
                o_ref[0, place, r : r + step, :] = o
    wait_at_last(copies)


def attn_bwd_kernel(me_ref, dz0_ref, dz1_ref, res_ref, go_ref, gain_ref, wo_ref, kv_ref, q_ref, pt_ref, cos_ref, sin_ref, token0_ref, token1_ref, token2_ref,
                    dres_ref, dq_ref, dkv_ref, gn_ref, kt_ref, do_ref, qs_ref, ds_ref, dp_ref):
    b = pl.program_id(0)
    half = pl.num_programs(0) // 2
    hd = kv_ref.shape[-1] // 2
    seq = kv_ref.shape[0] * kv_ref.shape[2]
    sl = q_ref.shape[1]
    heads = q_ref.shape[2] // hd
    x = res_ref[0].astype(F32)
    dz = jnp.where(b < half, dz0_ref[0], dz1_ref[0]).astype(F32)
    inv = lax.rsqrt(jnp.mean(x * x, axis=-1, keepdims=True) + EPS)
    xn = x * inv
    part = jnp.sum(dz * xn, axis=0, keepdims=True)

    @pl.when(b == 0)
    def _():
        gn_ref[...] = part

    @pl.when(b > 0)
    def _():
        gn_ref[...] += part

    dxn = dz * gain_ref[...]
    dx = inv * (dxn - xn * jnp.mean(dxn * xn, axis=-1, keepdims=True))
    dres = (go_ref[0].astype(F32) + dx).astype(BF)
    dres_ref[0] = dres
    keys = kv_ref[:, 0, :, :hd].reshape(seq, hd)
    vals = kv_ref[:, 0, :, hd:].reshape(seq, hd)
    kt_ref[...] = keys.astype(F32).T.astype(BF)
    for h in range(heads):
        do_ref[h * sl : (h + 1) * sl, :] = dot_nt(dres, wo_ref[h * hd : (h + 1) * hd, :]).astype(BF)
        qs_ref[h * sl : (h + 1) * sl, :] = q_ref[0, :, h * hd : (h + 1) * hd]
    scale = hd**-0.5
    cos_t, sin_t = cos_ref[...], sin_ref[...]

    def dprobs(h):
        return dot_nt(vals, do_ref[h * sl : (h + 1) * sl, :])

    dp_ref[0] = dprobs(0)
    for h in range(heads):
        if h + 1 < heads:
            dp_ref[(h + 1) % 2] = dprobs(h + 1)
        p = pt_ref[0, :, h * sl : (h + 1) * sl].astype(F32)
        t = p * dp_ref[h % 2]
        ds = ((t - p * jnp.sum(t, axis=0, keepdims=True)) * scale).astype(BF)
        ds_ref[:, h * sl : (h + 1) * sl] = ds
        dq = dot_nn(kt_ref[...], ds).T
        first, second = rope_bwd(dq[:, : hd // 2], dq[:, hd // 2 :], cos_t, sin_t)
        dq_ref[0, :, h * hd : h * hd + hd // 2] = first.astype(BF)
        dq_ref[0, :, h * hd + hd // 2 : (h + 1) * hd] = second.astype(BF)
    shape = (kv_ref.shape[0], kv_ref.shape[2], hd)
    dkv_ref[:, 0, :, :hd] = dot_nn(ds_ref[...], qs_ref[...]).astype(BF).reshape(shape)
    dkv_ref[:, 0, :, hd:] = dot_nn(pt_ref[0], do_ref[...]).astype(BF).reshape(shape)


def last_kernel(me_ref, dkv_ref, dq_ref, u_ref, h_ref, dres_ref, gain_ref, wq_ref, wk_ref, wv_ref, cos_ref, sin_ref, gm_ref, token0_ref, token1_ref,
                gh_ref, gkv_ref, acc_ref):
    b = pl.program_id(0)
    tp_n, dim, cols = wq_ref.shape
    hd = wk_ref.shape[1]
    raw = dkv_ref[0]
    dk = raw[:, :hd].astype(F32)
    first, second = rope_bwd(dk[:, : hd // 2], dk[:, hd // 2 :], cos_ref[...], sin_ref[...])
    dk = jnp.concatenate([first, second], axis=1).astype(BF)
    dv = raw[:, hd:]
    dn = dot_nt(dk, wk_ref[...]) + dot_nt(dv, wv_ref[...])
    for s in range(tp_n):
        dn = dn + dot_nt(dq_ref[0, :, s * cols : (s + 1) * cols], wq_ref[s])
    x = h_ref[0].astype(F32)
    inv = lax.rsqrt(jnp.mean(x * x, axis=-1, keepdims=True) + EPS)
    xn = x * inv
    part = jnp.sum(dn * xn, axis=0, keepdims=True)
    dxn = dn * gain_ref[...]
    dx = inv * (dxn - xn * jnp.mean(dxn * xn, axis=-1, keepdims=True))
    gh_ref[0] = (dres_ref[0].astype(F32) + dx).astype(BF)
    gk = dot_tn(u_ref[0], jnp.concatenate([dk, dv], axis=1))

    @pl.when(b == 0)
    def _():
        acc_ref[...] = part
        gkv_ref[:dim, :] = gk

    @pl.when(b > 0)
    def _():
        acc_ref[...] += part
        gkv_ref[:dim, :] += gk

    @pl.when(b == pl.num_programs(0) - 1)
    def _():
        width = 2 * hd
        per = dim // width
        for i in range(per):
            gkv_ref[dim + i : dim + i + 1, :] = gm_ref[:, i * width : (i + 1) * width]
            gkv_ref[dim + per + i : dim + per + i + 1, :] = acc_ref[:, i * width : (i + 1) * width]


def wgrad_kernel(x_ref, y_ref, o_ref):
    o_ref[0] = dot_tn(x_ref[...], y_ref[...])


def tie_kernel(x_ref, *rest):
    del x_ref, rest


def tie(x, *tokens):
    return pl.pallas_call(
        tie_kernel,
        name="tie",
        in_specs=[ANY] * (1 + len(tokens)),
        out_specs=ANY,
        out_shape=jax.ShapeDtypeStruct(x.shape, x.dtype),
        input_output_aliases={0: 0},
    )(x, *tokens)


def solution(mesh):
    act_spec = P("dp", "tp", None)
    in_specs = (act_spec, act_spec, P("dp"), P("dp"), P(None), P(None, "tp"), P(None, None), P(None, None), P("tp", None), P(None), P(None, "tp"), P(None, "tp"), P("tp", None))
    out_specs = (act_spec, act_spec, P("dp"), P("dp", "tp"), P("dp", None), P("dp", None), P(("dp", "tp"), None), P("dp"), P("dp", "tp"), P("dp", "tp"), P(("dp", "tp"), None))
    core_flip = [(0, 1), (1, 0), (2, 3), (3, 2)]
    chip_flip = [(0, 2), (2, 0), (1, 3), (3, 1)]

    def to_core(x):
        return lax.ppermute(x, "tp", core_flip)

    def to_chip(x):
        return lax.ppermute(x, "tp", chip_flip)

    def local_layer(hidden, grad_out, prefix_len, valid_len, attn_norm, w_query, w_key, w_value, w_out, mlp_norm, w_gate, w_up, w_down):
        batch, sl, dim = hidden.shape
        half = batch // 2
        rows = half * sl
        hd = w_key.shape[1]
        cols = w_query.shape[1]
        tp_n = mesh.shape["tp"]
        seq = sl * tp_n
        qd = cols * tp_n
        heads = qd // hd
        ffn = w_gate.shape[1]
        own = batch * sl
        me = lax.axis_index("tp").astype(jnp.int32).reshape(1)

        inv_freq = np.exp(np.arange(hd // 2, dtype=np.float32) * np.float32(2.0 / hd) * np.float32(-math.log(10000.0)))
        angles = np.arange(seq, dtype=np.float32)[:, None] * inv_freq[None, :]
        cos_t, sin_t = jnp.asarray(np.cos(angles)), jnp.asarray(np.sin(angles))
        gain1 = (1.0 + attn_norm.astype(F32)).reshape(1, dim)
        gain2 = (1.0 + mlp_norm.astype(F32)).reshape(1, dim)

        def sds(shape, dtype=BF):
            return jax.ShapeDtypeStruct(shape, dtype)

        def block(shape, at, single=False):
            return pl.BlockSpec(shape, at, pipeline_mode=pl.Buffered(1) if single else None)

        tok_spec = block((1, sl, dim), lambda b, *_: (b, 0, 0))
        q_spec = block((1, sl, qd), lambda b, *_: (b, 0, 0))
        kv_spec = block((1, sl, 2 * hd), lambda b, *_: (b, 0, 0))
        kv4_spec = block((tp_n, 1, sl, 2 * hd), lambda b, *_: (0, b, 0, 0))
        pt_spec = block((1, seq, heads * sl), lambda b, *_: (b, 0, 0))
        rope_spec = block((sl, hd // 2), lambda b, m, *_: (m[0], 0), True)
        gain_spec = const_spec((1, dim))
        dma = lambda n: pltpu.SemaphoreType.DMA((n,))

        wq4 = lax.all_gather(w_query, "tp", axis=0)
        g_mate = to_core(grad_out)
        u, kv = run(
            pre_kernel, (batch,),
            [tok_spec, gain_spec, const_spec((dim, hd)), const_spec((dim, hd)), rope_spec, rope_spec],
            [tok_spec, kv_spec], [sds((batch, sl, dim)), sds((batch, sl, 2 * hd))],
            (me, hidden, gain1, w_key, w_value, cos_t, sin_t), prefetch=1,
            flops=4 * own * dim * hd, nbytes=6 * own * dim)
        kv4 = lax.all_gather(kv, "tp", axis=0)
        wo_all = lax.all_gather(w_out, "tp", axis=0, tiled=True)

        bn = 512
        whole_spec = block((batch, sl, dim), lambda n, *_: (0, 0, 0), True)
        half_spec = block((half, sl, dim), lambda n, *_: (0, 0, 0), True)
        cat_shape = (2, 2, half, sl, dim)
        da_near, gcat0, gcat1, go0, go1 = run(
            dact_near_kernel, (ffn // bn,),
            [whole_spec, whole_spec, block((bn, dim), lambda n, *_: (n, 0)), ANY],
            [block((2, 2, rows, bn), lambda n, *_: (0, 0, 0, n))] + [ANY] * 4,
            [sds((2, 2, rows, ffn))] + [sds(cat_shape)] * 2 + [sds((half, sl, dim))] * 2,
            (me, grad_out, g_mate, w_down, kv), prefetch=1, scratch=[dma(6)],
            flops=8 * rows * dim * ffn, nbytes=2 * ffn * dim + 8 * rows * ffn)

        q, pt, mixed = run(
            attn_fwd_kernel, (batch,),
            [tok_spec, const_spec((tp_n, dim, cols)), kv4_spec, rope_spec, rope_spec, ANY],
            [q_spec, pt_spec, q_spec],
            [sds((batch, sl, qd)), sds((batch, seq, heads * sl)), sds((batch, sl, qd))],
            (me, prefix_len, valid_len, u, wq4, kv4, cos_t, sin_t, da_near), prefetch=3,
            scratch=[pltpu.VMEM((hd, seq), BF), pltpu.VMEM((2, seq, sl), F32)],
            flops=2 * own * dim * qd + 4 * own * seq * qd, nbytes=2 * own * heads * seq)

        g_far = [to_chip(tie(go0, mixed))]

        def out_proj(c, prev):
            at = lambda b: (b + c * half, 0, 0)
            extra = [prev] if c else []
            return run(
                out_kernel, (half,),
                [block((1, sl, qd), at), const_spec((qd, dim)), block((1, sl, dim), at), gain_spec] + [ANY] * len(extra),
                [block((1, sl, dim), at), block((1, sl, dim), lambda b: (b, 0, 0))],
                [sds((batch, sl, dim)), sds((half, sl, dim))],
                (mixed, wo_all, hidden, gain2, *extra), aliases={4: 0} if c else None,
                flops=own * dim * qd, nbytes=4 * own * dim)

        resid, z0 = out_proj(0, None)
        resid, z1 = out_proj(1, resid)
        zs = [z0, z1]
        z_mate = [to_core(z) for z in zs]
        z_far = [to_chip(z0)]
        z_far.append(to_chip(z1))
        g_far.append(to_chip(tie(go1, z1)))

        o_shape = (2, 2, rows, ffn)

        def mlp(other, c, za, zb, da, prev, token):
            extra = list(prev) if prev is not None else []
            o_spec = block((1, 2, rows, bn), lambda n, m: (abs(other - m[0] // 2), 0, 0, n))
            w_spec = block((dim, bn), lambda n, *_: (0, n))
            return run(
                functools.partial(mlp_kernel, other), (ffn // bn,),
                [half_spec, half_spec, block((1, 2, rows, bn), lambda n, *_: (c, 0, 0, n)), w_spec, w_spec] + [ANY] * (len(extra) + 1),
                [o_spec] * 3 + [ANY], [sds(o_shape)] * 3 + [sds(cat_shape)],
                (me, za, zb, da, w_gate, w_up, *extra, token),
                prefetch=1, scratch=[dma(2)], aliases={6 + i: i for i in range(4)} if extra else None,
                flops=8 * rows * dim * ffn, nbytes=4 * ffn * dim + 16 * rows * ffn)

        near0 = mlp(0, 0, zs[0], z_mate[0], da_near, None, z1)
        near1 = mlp(0, 1, zs[1], z_mate[1], da_near, None, near0[0])

        ga = tie(g_far[0], near0[0])
        gb = to_core(ga)
        da_far, gcat0 = run(
            dact_far_kernel, (ffn // bn,),
            [half_spec, half_spec, block((bn, dim), lambda n, *_: (n, 0)), ANY, ANY],
            [block((1, 2, rows, bn), lambda n, *_: (0, 0, 0, n)), ANY],
            [sds((1, 2, rows, ffn)), sds(cat_shape)],
            (me, ga, gb, w_down, gcat0, near1[0]), prefetch=1, scratch=[dma(2)], aliases={4: 1},
            flops=4 * rows * dim * ffn, nbytes=2 * ffn * dim + 4 * rows * ffn)
        za = tie(z_far[0], near1[0])
        zb = to_core(za)
        full0 = mlp(1, 0, za, zb, da_far, near0, da_far)

        def gated_grad(full):
            flat = (4 * rows, ffn)
            return (dot_nt(full[1].reshape(flat), w_gate) + dot_nt(full[2].reshape(flat), w_up)).astype(BF)

        def mlp_out(full):
            return dot_nn(full[0].reshape(4 * rows, ffn), w_down).astype(BF)

        def scatter(x):
            return lax.psum_scatter(x.reshape(tp_n, rows, dim), "tp", scatter_dimension=0).reshape(half, sl, dim)

        dz_part0 = gated_grad(full0)
        dz0 = scatter(dz_part0)
        mlp_part0 = mlp_out(full0)
        part0 = scatter(mlp_part0)

        ga, za = tie(g_far[1], full0[0]), tie(z_far[1], full0[0])
        gb, zb = to_core(ga), to_core(za)
        bf = 512
        o_spec = block((1, 2, rows, bf), lambda n, m: (1 - m[0] // 2, 0, 0, n))
        w_spec = block((dim, bf), lambda n, *_: (0, n))
        full1 = run(
            functools.partial(mlp_fused_kernel, 1), (ffn // bf,),
            [half_spec] * 4 + [w_spec, w_spec, block((bf, dim), lambda n, *_: (n, 0))] + [ANY] * 7,
            [o_spec] * 3 + [ANY] * 2, [sds(o_shape)] * 3 + [sds(cat_shape)] * 2,
            (me, za, zb, ga, gb, w_gate, w_up, w_down, *near1, gcat1, dz_part0, mlp_part0),
            prefetch=1, scratch=[dma(4)], aliases={8 + i: i for i in range(5)},
            flops=12 * rows * dim * ffn, nbytes=6 * ffn * dim + 12 * rows * ffn)
        gcat1 = full1[4]
        dz_part1 = gated_grad(full1)
        dz1 = scatter(dz_part1)
        mlp_part1 = mlp_out(full1)
        part1 = scatter(mlp_part1)
        hidden_out = (resid.astype(F32) + jnp.concatenate([part0, part1]).astype(F32)).astype(BF)

        def grad_half(a, b):
            return dot_tn(a.reshape(4 * rows, -1), b.reshape(4 * rows, -1))

        g_down_half = grad_half(full0[0], gcat0)

        d_resid, d_q, dkv_part, gn2 = run(
            attn_bwd_kernel, (batch,),
            [block((1, sl, dim), lambda b, *_: (jnp.minimum(b, half - 1), 0, 0)), block((1, sl, dim), lambda b, *_: (jnp.maximum(b - half, 0), 0, 0)),
             tok_spec, tok_spec, gain_spec, const_spec((qd, dim)), kv4_spec, q_spec, pt_spec, rope_spec, rope_spec, ANY, ANY, ANY],
            [tok_spec, q_spec, kv4_spec, block((1, dim), lambda b, *_: (0, 0))],
            [sds((batch, sl, dim)), sds((batch, sl, qd)), sds((tp_n, batch, sl, 2 * hd)), sds((1, dim), F32)],
            (me, dz0, dz1, resid, grad_out, gain2, wo_all, kv4, q, pt, cos_t, sin_t, mlp_part1, g_down_half, part0), prefetch=1,
            scratch=[pltpu.VMEM((hd, seq), BF), pltpu.VMEM((heads * sl, hd), BF), pltpu.VMEM((heads * sl, hd), BF), pltpu.VMEM((seq, heads * sl), BF), pltpu.VMEM((2, seq, sl), F32)],
            flops=2 * own * dim * qd + 8 * own * seq * qd, nbytes=2 * own * heads * seq)
        dkv = lax.psum_scatter(tie(dkv_part, part1), "tp", scatter_dimension=0)

        g_out = dot_tn(mixed.reshape(own, qd), d_resid.reshape(own, dim))
        g_out_sum = lax.psum_scatter(g_out, "tp", scatter_dimension=0, tiled=True)
        bm = dim // 2
        g_query = run(
            wgrad_kernel, (dim // bm, tp_n),
            [block((own, bm), lambda i, j: (0, i)), block((own, cols), lambda i, j: (0, j))],
            block((1, bm, cols), lambda i, j: (j, i, 0)), sds((tp_n, dim, cols), F32),
            (u.reshape(own, dim), d_q.reshape(own, qd)), flops=2 * own * dim * qd, nbytes=4 * dim * qd)
        g_query_sum = lax.psum_scatter(g_query, "tp", scatter_dimension=0)

        extra = dim // hd
        grad_hidden, gkv = run(
            last_kernel, (batch,),
            [kv_spec, q_spec, tok_spec, tok_spec, tok_spec, gain_spec,
             const_spec((tp_n, dim, cols)), const_spec((dim, hd)), const_spec((dim, hd)), rope_spec, rope_spec, const_spec((1, dim)), ANY, ANY],
            [tok_spec, block((dim + extra, 2 * hd), lambda b, *_: (0, 0))],
            [sds((batch, sl, dim)), sds((dim + extra, 2 * hd), F32)],
            (me, dkv, d_q, u, hidden, d_resid, gain1, wq4, w_key, w_value, cos_t, sin_t, gn2, g_out, g_query), prefetch=1,
            scratch=[pltpu.VMEM((1, dim), F32)],
            flops=2 * own * dim * (qd + 4 * hd), nbytes=8 * own * dim)
        gkv = lax.psum(gkv, "tp")
        g_key, g_value = gkv[:dim, :hd], gkv[:dim, hd:]
        g_mlp_norm = gkv[dim : dim + extra // 2].reshape(dim)
        g_attn_norm = gkv[dim + extra // 2 :].reshape(dim)

        g_down = g_down_half + grad_half(full1[0], gcat1)
        g_gate = grad_half(full0[3], full0[1]) + grad_half(full1[3], full1[1])
        g_up = grad_half(full0[3], full0[2]) + grad_half(full1[3], full1[2])
        return (hidden_out, grad_hidden, g_attn_norm, g_query_sum, g_key, g_value, g_out_sum, g_mlp_norm, g_gate, g_up, g_down)

    return jax.shard_map(local_layer, mesh=mesh, in_specs=in_specs, out_specs=out_specs, check_vma=False)
```

profile of v0, /device:TPU:0, one launch (start us, length us, event | category | flops | bytes accessed | tf_op | source)
XLA Modules:
  0.0 1736.2 jit_solution(17742322104336873085)
XLA Ops:
  7.2 1.3 convert_add_fusion.1
  8.5 9.3 shard_map.230
  17.9 0.7 all-gather.8.cloned.1.call-update
  18.6 0.9 collective-permute-start
  19.6 0.6 convert_add_fusion
  20.2 11.7 collective-permute-done.gb_ref
  31.9 61.2 %shard_map.231 = (bf16[2,2,768,4096]{3,2,1,0:T(8,128)(2,1)}, bf16[2,2,3,256,2048]{4,3,2,1,0:T(8,128)(2,1)}, bf16[2,2,3,256,2048]{4,3,2,1,0:T(8,128)(2,1)}, bf16[...) custom-call(s32[1]{0:T(128)} %bitcast.me_ref, bf16[6,256,2048]{2,1,0:T(8,128)(2,1)} %go_ref.1, ...), custom_call_target="tpu_custom_call" | custom-call | flops 51539607552 | bytes 41943040 | tf_op jit(solution)/shard_map/pallas_call | solution.py:39
  93.2 28.3 %all-gather.8.cloned.1.call-done = bf16[8192,512]{1,0:T(8,128)(2,1)} async-done(((bf16[2048,512]{1,0:T(8,128)(2,1)}), bf16[8192,512]{1,0:T(8,128)(2,1)}) %all-gather.8.cloned.1.call-update) | async-done | bytes 8388624 | tf_op jit(solution)/shard_map/all_gather | solution.py:379
  121.4 44.5 %shard_map.232 = (bf16[6,256,2048]{2,1,0:T(8,128)(2,1)}, bf16[6,1024,2048]{2,1,0:T(8,128)(2,1)}, bf16[6,256,2048]{2,1,0:T(8,128)(2,1)}) custom-call(s32[1]{0:T(128)} %bitcast.me_ref, s32[6]{0:T(128)} %pre_ref.1, s32[6]{0:T(128)} %val_ref.1, bf16[6,256,2048]{2,1,0:T(8,128)(2,1)} %get-tuple-element.50.u_ref, bf16[4,2048,512]{2,1,0:T(8,128)(2,1)} %bitcast.72, ...), custom_call_target="tpu_custom_call" | custom-call | flops 25769803776 | bytes 25165824 | tf_op jit(solution)/shard_map/pallas_call | solution.py:39
  165.9 12.6 all-gather.6.cloned.1.call-done.wo_ref
  178.5 13.3 shard_map.233
  192.3 1.7 collective-permute-start.5
  194.0 13.1 shard_map.234
  207.2 67.3 %shard_map.235 = (bf16[2,2,768,4096]{3,2,1,0:T(8,128)(2,1)}, bf16[2,2,768,4096]{3,2,1,0:T(8,128)(2,1)}, bf16[2,2,768,4096]{3,2,1,0:T(8,128)(2,1)}, bf16[2,2,3,256,2048]{4,3,2,1,0:T(8,128)(2,1)}) custom-call(s32[1]{0:T(128)} %bitcast.me_ref, bf16[3,256,2048]{2,1,0:T(8,128)(2,1)} %get-tuple-element.56.za_ref, ...), custom_call_target="tpu_custom_call" | custom-call | flops 51539607552 | bytes 83886080 | tf_op jit(solution)/shard_map/pallas_call | solution.py:39
  274.4 55.6 %collective-permute-done.5.x_ref = bf16[3,256,2048]{2,1,0:T(8,128)(2,1)} collective-permute-done((bf16[3,256,2048]{2,1,0:T(8,128)(2,1)}, bf16[3,256,2048]{2,1,0:T(8,128)(2,1)}, u32[]{:S(2)}, u32[]{:S(2)}) %collective-permute-start.5) | collective-permute-done | bytes 3145760 | tf_op jit(solution)/shard_map/ppermute | solution.py:342
  330.0 67.5 %shard_map.236 = (bf16[2,2,768,4096]{3,2,1,0:T(8,128)(2,1)}, bf16[2,2,768,4096]{3,2,1,0:T(8,128)(2,1)}, bf16[2,2,768,4096]{3,2,1,0:T(8,128)(2,1)}, bf16[2,2,3,256,2048]{4,3,2,1,0:T(8,128)(2,1)}) custom-call(s32[1]{0:T(128)} %bitcast.me_ref, bf16[3,256,2048]{2,1,0:T(8,128)(2,1)} %get-tuple-element.57.rest_0_.za_ref, ...), custom_call_target="tpu_custom_call" | custom-call | flops 51539607552 | bytes 83886080 | tf_op jit(solution)/shard_map/pallas_call | solution.py:39
  397.5 1.7 copy-done.2
  399.7 32.4 %shard_map.237 = (bf16[1,2,768,4096]{3,2,1,0:T(8,128)(2,1)}, bf16[2,2,3,256,2048]{4,3,2,1,0:T(8,128)(2,1)}) custom-call(s32[1]{0:T(128)} %bitcast.me_ref, bf16[3,256,2048]{2,1,0:T(8,128)(2,1)} %tie.9.ga_ref, bf16[3,256,2048]{2,1,0:T(8,128)(2,1)} %collective-permute-done.6.gb_ref, bf16[4096,2048]{1,0:T(8,128)(2,1)} %wd_ref.5, ...), custom_call_target="tpu_custom_call", output_to_operand_aliasing={{1}: (4, {})} | custom-call | flops 25769803776 | bytes 29360128 | tf_op jit(solution)/shard_map/pallas_call | solution.py:39
  432.0 1.6 copy-done.5
  433.7 67.7 %shard_map.238 = (bf16[2,2,768,4096]{3,2,1,0:T(8,128)(2,1)}, bf16[2,2,768,4096]{3,2,1,0:T(8,128)(2,1)}, bf16[2,2,768,4096]{3,2,1,0:T(8,128)(2,1)}, bf16[2,2,3,256,2048]{4,3,2,1,0:T(8,128)(2,1)}) custom-call(s32[1]{0:T(128)} %bitcast.me_ref, ...), custom_call_target="tpu_custom_call", output_to_operand_aliasing={{0}: (6, {}), {1}: (7, {}), {2}: (8, {}), {3}: (9, {})} | custom-call | flops 51539607552 | bytes 83886080 | tf_op jit(solution)/shard_map/pallas_call | solution.py:39
  501.3 60.9 %fusion.1 = f32[3072,2048]{1,0:T(8,128)} fusion(bf16[3072,4096]{1,0:T(8,128)(2,1)} %bitcast.97, bf16[2048,4096]{1,0:T(8,128)(2,1)} %wu_ref.7), kind=kOutput, calls=%fused_computation.14 | convolution fusion | flops 51539607552 | bytes 67108864 | tf_op jit(solution)/shard_map/dot_general | solution.py:25
  562.3 61.1 %add_convert_fusion.1.rest_5_ = bf16[3072,2048]{1,0:T(8,128)(2,1)} fusion(f32[3072,2048]{1,0:T(8,128)} %fusion.1, bf16[3072,4096]{1,0:T(8,128)(2,1)} %bitcast.95, bf16[2048,4096]{1,0:T(8,128)(2,1)} %wg_ref.7), kind=kOutput, calls=%fused_computation.1 | convolution fusion | flops 51552190464 | bytes 79691776 | tf_op jit(solution)/shard_map/dot_general | solution.py:25
  623.8 1.5 copy-done.1
  625.6 115.2 %collective-permute-done.9.x_ref = bf16[3,256,2048]{2,1,0:T(8,128)(2,1)} collective-permute-done((bf16[3,256,2048]{2,1,0:T(8,128)(2,1)}, bf16[3,256,2048]{2,1,0:T(8,128)(2,1)}, u32[]{:S(2)}, u32[]{:S(2)}) %collective-permute-start.9) | collective-permute-done | bytes 3145760 | tf_op jit(solution)/shard_map/ppermute | solution.py:342
  740.8 87.9 %collective-permute-done.7.x_ref = bf16[3,256,2048]{2,1,0:T(8,128)(2,1)} collective-permute-done((bf16[3,256,2048]{2,1,0:T(8,128)(2,1)S(1)}, bf16[3,256,2048]{2,1,0:T(8,128)(2,1)}, u32[]{:S(2)}, u32[]{:S(2)}) %collective-permute-start.7) | collective-permute-done | bytes 3145760 | tf_op jit(solution)/shard_map/ppermute | solution.py:342
  828.6 60.1 %convolution_convert_fusion.1.rest_6_ = bf16[3072,2048]{1,0:T(8,128)(2,1)} fusion(bf16[3072,4096]{1,0:T(8,128)(2,1)} %bitcast.62, bf16[4096,2048]{1,0:T(8,128)(2,1)} %wd_ref.5), kind=kOutput, calls=%fused_computation.7 | convolution fusion | flops 51545899008 | bytes 54525952 | tf_op jit(solution)/shard_map/dot_general | solution.py:21
  888.8 1.7 copy-done.4
  890.5 101.2 %shard_map.239 = (bf16[2,2,768,4096]{3,2,1,0:T(8,128)(2,1)}, bf16[2,2,768,4096]{3,2,1,0:T(8,128)(2,1)}, bf16[2,2,768,4096]{3,2,1,0:T(8,128)(2,1)}, bf16[2,2,3,25...) custom-call(s32[1]{0:T(128)} %bitcast.me_ref, ...), custom_call_target="tpu_custom_call", output_to_operand_aliasing={{0}: (8, {}), {1}: (9, {}), {2}: (10, {}), {3}: (11, {}), {... | custom-call | flops 77309411328 | bytes 88080384 | tf_op jit(solution)/shard_map/pallas_call | solution.py:39
  991.7 60.9 %fusion.2 = f32[3072,2048]{1,0:T(8,128)} fusion(bf16[3072,4096]{1,0:T(8,128)(2,1)} %bitcast.93, bf16[2048,4096]{1,0:T(8,128)(2,1)} %wu_ref.7), kind=kOutput, calls=%fused_computation.15 | convolution fusion | flops 51539607552 | bytes 67108864 | tf_op jit(solution)/shard_map/dot_general | solution.py:25
  1052.6 61.1 %add_convert_fusion = bf16[3072,2048]{1,0:T(8,128)(2,1)} fusion(f32[3072,2048]{1,0:T(8,128)} %fusion.2, bf16[3072,4096]{1,0:T(8,128)(2,1)} %bitcast.91, bf16[2048,4096]{1,0:T(8,128)(2,1)} %wg_ref.7), kind=kOutput, calls=%fused_computation | convolution fusion | flops 51552190464 | bytes 79691776 | tf_op jit(solution)/shard_map/dot_general | solution.py:25
  1113.7 61.8 %convolution_convert_fusion.token0_ref = bf16[3072,2048]{1,0:T(8,128)(2,1)} fusion(bf16[3072,4096]{1,0:T(8,128)(2,1)} %bitcast.64, bf16[4096,2048]{1,0:T(8,128)(2,1)} %wd_ref.5), kind=kOutput, calls=%fused_computation.6 | convolution fusion | flops 51545899008 | bytes 54525952 | tf_op jit(solution)/shard_map/dot_general | solution.py:21
  1175.6 63.7 %fusion.3.token1_ref = f32[4096,2048]{1,0:T(8,128)} fusion(bf16[3072,4096]{1,0:T(8,128)(2,1)} %bitcast.63, bf16[3072,2048]{1,0:T(8,128)(2,1)} %bitcast.102), kind=kOutput, calls=%fused_computation.16 | convolution fusion | flops 51539607552 | bytes 71303168 | tf_op jit(solution)/shard_map/dot_general | solution.py:29
  1239.4 64.6 %shard_map.240 = (bf16[6,256,2048]{2,1,0:T(8,128)(2,1)}, bf16[6,256,2048]{2,1,0:T(8,128)(2,1)}, bf16[4,6,256,512]{3,2,1,0:T(8,128)(2,1)}, f32[1,2048]{1,0:T(1,128)}) custom-call(s32[1]{0:T(128)} %bitcast.me_ref, bf16[3,256,2048]{2,1,0:T(8,128)(2,1)} %bitcast.89, bf16[3,256,2048]{2,1,0:T(8,128)(2,1)} %bitcast.90, ...), custom_call_target="tpu_custom_call" | custom-call | flops 38654705664 | bytes 25165824 | tf_op jit(solution)/shard_map/pallas_call | solution.py:39
  1304.0 0.8 reduce-scatter.24.cloned.1.call-done
  1304.9 22.4 %shard_map.241.token1_ref = f32[4,2048,512]{2,1,0:T(8,128)} custom-call(bf16[1536,2048]{1,0:T(8,128)(2,1)} %bitcast.74, bf16[1536,2048]{1,0:T(8,128)(2,1)} %bitcast.75), custom_call_target="tpu_custom_call" | custom-call | flops 12884901888 | bytes 16777216 | tf_op jit(solution)/shard_map/pallas_call | solution.py:39
  1327.3 20.6 %convolution_bitcast_fusion.token0_ref = f32[2048,2048]{1,0:T(8,128)} fusion(bf16[6,256,2048]{2,1,0:T(8,128)(2,1)} %get-tuple-element.53.mix_ref.rest_0_, bf16[6,256,2048]{2,1,0:T(8,128)(2,1)} %get-tuple-element.82.dres_ref), kind=kOutput, calls=%fused_computation.8 | convolution fusion | flops 12884901888 | bytes 29360128 | tf_op jit(solution)/shard_map/dot_general | solution.py:29
  1348.0 12.7 reduce-scatter.30.cloned.1.call-done
  1360.7 33.8 %shard_map.242 = (bf16[6,256,2048]{2,1,0:T(8,128)(2,1)}, f32[2056,512]{1,0:T(8,128)}) custom-call(s32[1]{0:T(128)} %bitcast.me_ref, bf16[6,256,512]{2,1,0:T(8,128)(2,1)} %bitcast.78, bf16[6,256,2048]{2,1,0:T(8,128)(2,1)} %get-tuple-element.81.dq_ref, bf16[6,256,2048]{2,1,0:T(8,128)(2,1)} %get-tuple-element.50.u_ref, bf16[6,256,2048]{2,1,0:T(8,128)(2,1)} %h_ref.7, ...), custom_call_target="tpu_custom_call" | custom-call | flops 19327352832 | bytes 25165824 | tf_op jit(solution)/shard_map/pallas_call | solution.py:39
  1395.1 64.3 %fusion.5 = f32[2048,4096]{1,0:T(8,128)} fusion(bf16[3072,2048]{1,0:T(8,128)(2,1)} %bitcast.100, bf16[3072,4096]{1,0:T(8,128)(2,1)} %bitcast.94), kind=kOutput, calls=%fused_computation.18 | convolution fusion | flops 51539607552 | bytes 71303168 | tf_op jit(solution)/shard_map/dot_general | solution.py:29
  1459.4 63.6 %fusion.4 = f32[2048,4096]{1,0:T(8,128)} fusion(bf16[3072,2048]{1,0:T(8,128)(2,1)} %bitcast.101, bf16[3072,4096]{1,0:T(8,128)(2,1)} %bitcast.92), kind=kOutput, calls=%fused_computation.17 | convolution fusion | flops 51539607552 | bytes 71303168 | tf_op jit(solution)/shard_map/dot_general | solution.py:29
  1523.0 63.2 %convolution_add_fusion.1 = f32[2048,4096]{1,0:T(8,128)} fusion(f32[2048,4096]{1,0:T(8,128)} %fusion.5, bf16[3072,2048]{1,0:T(8,128)(2,1)} %bitcast.103, bf16[3072,4096]{1,0:T(8,128)(2,1)} %bitcast.98), kind=kOutput, calls=%fused_computation.3 | convolution fusion | flops 51547996160 | bytes 104857600 | tf_op jit(solution)/shard_map/dot_general | solution.py:29
  1586.2 63.0 %convolution_add_fusion.2 = f32[2048,4096]{1,0:T(8,128)} fusion(f32[2048,4096]{1,0:T(8,128)} %fusion.4, bf16[3072,2048]{1,0:T(8,128)(2,1)} %bitcast.104, bf16[3072,4096]{1,0:T(8,128)(2,1)} %bitcast.96), kind=kOutput, calls=%fused_computation.4 | convolution fusion | flops 51547996160 | bytes 104857600 | tf_op jit(solution)/shard_map/dot_general | solution.py:29
  1649.3 63.6 %convolution_add_fusion = f32[4096,2048]{1,0:T(8,128)} fusion(f32[4096,2048]{1,0:T(8,128)} %fusion.3.token1_ref, bf16[3072,4096]{1,0:T(8,128)(2,1)} %bitcast.65, bf16[3072,2048]{1,0:T(8,128)(2,1)} %bitcast.99), kind=kOutput, calls=%fused_computation.2 | convolution fusion | flops 51547996160 | bytes 104857600 | tf_op jit(solution)/shard_map/dot_general | solution.py:29
  1712.9 9.8 add_convert_fusion.2
  1722.7 0.8 slice_bitcast_fusion
  1723.5 0.6 copy.47
  1724.1 0.6 copy.48
  1724.7 4.5 fusion
  (59 shorter events, 3.0 us)
Async XLA Ops:
  7.2 12.4 copy-start.3
  7.2 86.0 %all-gather.10.cloned.1.call-start = ((), (), s32[]{:S(2)}) async-start(), calls=%async_computation.11 | async-start | bytes 7864320 | tf_op jit(solution)/shard_map/all_gather | solution.py:387
  17.8 103.6 %all-gather.8.cloned.1.call-start = ((), (), s32[]{:S(2)}) async-start(), calls=%async_computation.10 | async-start | bytes 10485760 | tf_op jit(solution)/shard_map/all_gather | solution.py:379
  18.6 159.9 %all-gather.6.cloned.1.call-start = ((), (), s32[]{:S(2)}) async-start(), calls=%async_computation.7 | async-start | bytes 10485760 | tf_op jit(solution)/shard_map/all_gather | solution.py:388
  18.6 13.2 collective-permute-start
  19.5 1219.8 %reduce-scatter.26.cloned.1.call-start = ((), (), s32[]{:S(2)}) async-start(), calls=%async_computation.14 | async-start | bytes 15728640
  191.7 15.4 collective-permute-start.3
  192.0 205.5 %collective-permute-start.1 = (bf16[3,256,2048]{2,1,0:T(8,128)(2,1)}, bf16[3,256,2048]{2,1,0:T(8,128)(2,1)S(1)}, u32[]{:S(2)}, u32[]{:S(2)}) collective-permute-start(bf16[3,256,2048]{2,1,0:T(8,128)(2,1)} %get-tuple-element.56.za_ref), channel_id=1, source_target_pairs={{0,2},{2,0},{1,3},{3,1},{4,6},{6,4},{5,7},{7,5}} | collective-permute-start | bytes 9437192 | tf_op jit(solution)/shard_map/ppermute | solution.py:342
  192.3 137.7 %collective-permute-start.5 = (bf16[3,256,2048]{2,1,0:T(8,128)(2,1)}, bf16[3,256,2048]{2,1,0:T(8,128)(2,1)}, u32[]{:S(2)}, u32[]{:S(2)}) collective-permute-start(bf16[3,256,2048]{2,1,0:T(8,128)(2,1)} %tie.8), channel_id=1, source_target_pairs={{0,2},{2,0},{1,3},{3,1},{4,6},{6,4},{5,7},{7,5}} | collective-permute-start | bytes 9437192 | tf_op jit(solution)/shard_map/ppermute | solution.py:342
  207.2 122.8 %collective-permute-start.2 = (bf16[3,256,2048]{2,1,0:T(8,128)(2,1)}, bf16[3,256,2048]{2,1,0:T(8,128)(2,1)}, u32[]{:S(2)}, u32[]{:S(2)}) collective-permute-start(bf16[3,256,2048]{2,1,0:T(8,128)(2,1)} %get-tuple-element.57.rest_0_.za_ref), channel_id=1, source_target_pairs={{0,1},{1,0},{2,3},{3,2},{4,5},{5,4},{6,7},{7,6}} | collective-permute-start | bytes 9437192 | tf_op jit(solution)/shard_map/ppermute | solution.py:339
  330.0 69.7 %collective-permute-start.6 = (bf16[3,256,2048]{2,1,0:T(8,128)(2,1)}, bf16[3,256,2048]{2,1,0:T(8,128)(2,1)}, u32[]{:S(2)}, u32[]{:S(2)}) collective-permute-start(bf16[3,256,2048]{2,1,0:T(8,128)(2,1)} %tie.9.ga_ref), channel_id=1, source_target_pairs={{0,1},{1,0},{2,3},{3,2},{4,5},{5,4},{6,7},{7,6}} | collective-permute-start | bytes 9437192 | tf_op jit(solution)/shard_map/ppermute | solution.py:339
  397.5 1.7 copy-start.2
  399.2 32.9 %collective-permute-start.4 = (bf16[3,256,2048]{2,1,0:T(8,128)(2,1)}, bf16[3,256,2048]{2,1,0:T(8,128)(2,1)S(1)}, u32[]{:S(2)}, u32[]{:S(2)}) collective-permute-start(bf16[3,256,2048]{2,1,0:T(8,128)(2,1)} %tie.7.za_ref), channel_id=1, source_target_pairs={{0,1},{1,0},{2,3},{3,2},{4,5},{5,4},{6,7},{7,6}} | collective-permute-start | bytes 9437192 | tf_op jit(solution)/shard_map/ppermute | solution.py:339
  432.0 1.6 copy-start.5
  623.3 1.9 copy-start.1
  623.4 616.0 %reduce-scatter.22.cloned.1.call-start = ((), (), s32[]{:S(2)}) async-start(), calls=%async_computation.12 | async-start | bytes 15728640
  623.4 117.3 %collective-permute-start.9 = (bf16[3,256,2048]{2,1,0:T(8,128)(2,1)}, bf16[3,256,2048]{2,1,0:T(8,128)(2,1)}, u32[]{:S(2)}, u32[]{:S(2)}) collective-permute-start(bf16[3,256,2048]{2,1,0:T(8,128)(2,1)} %tie.11), channel_id=1, source_target_pairs={{0,2},{2,0},{1,3},{3,1},{4,6},{6,4},{5,7},{7,5}} | collective-permute-start | bytes 9437192 | tf_op jit(solution)/shard_map/ppermute | solution.py:342
  625.2 203.4 %collective-permute-start.7 = (bf16[3,256,2048]{2,1,0:T(8,128)(2,1)S(1)}, bf16[3,256,2048]{2,1,0:T(8,128)(2,1)}, u32[]{:S(2)}, u32[]{:S(2)}) collective-permute-start(bf16[3,256,2048]{2,1,0:T(8,128)(2,1)S(1)} %copy-done.1), channel_id=1, source_target_pairs={{0,2},{2,0},{1,3},{3,1},{4,6},{6,4},{5,7},{7,5}} | collective-permute-start | bytes 9437192 | tf_op jit(solution)/shard_map/ppermute | solution.py:342
  740.7 148.0 %collective-permute-start.10 = (bf16[3,256,2048]{2,1,0:T(8,128)(2,1)}, bf16[3,256,2048]{2,1,0:T(8,128)(2,1)}, u32[]{:S(2)}, u32[]{:S(2)}) collective-permute-start(bf16[3,256,2048]{2,1,0:T(8,128)(2,1)} %tie.12.ga_ref), channel_id=1, source_target_pairs={{0,1},{1,0},{2,3},{3,2},{4,5},{5,4},{6,7},{7,6}} | collective-permute-start | bytes 9437192 | tf_op jit(solution)/shard_map/ppermute | solution.py:339
  828.6 60.2 %collective-permute-start.8 = (bf16[3,256,2048]{2,1,0:T(8,128)(2,1)}, bf16[3,256,2048]{2,1,0:T(8,128)(2,1)S(1)}, u32[]{:S(2)}, u32[]{:S(2)}) collective-permute-start(bf16[3,256,2048]{2,1,0:T(8,128)(2,1)} %tie.10.za_ref), channel_id=1, source_target_pairs={{0,1},{1,0},{2,3},{3,2},{4,5},{5,4},{6,7},{7,6}} | collective-permute-start | bytes 9437192 | tf_op jit(solution)/shard_map/ppermute | solution.py:339
  888.7 350.7 %reduce-scatter.28.cloned.1.call-start = ((), (), s32[]{:S(2)}) async-start(), calls=%async_computation.15 | async-start | bytes 15728640
  888.8 1.7 copy-start.4
  1113.7 191.1 %reduce-scatter.24.cloned.1.call-start = ((), (), s32[]{:S(2)}) async-start(), calls=%async_computation.13 | async-start | bytes 15728640
  1175.6 185.1 %reduce-scatter.30.cloned.1.call-start = ((), (), s32[]{:S(2)}) async-start(), calls=%async_computation.16 | async-start | bytes 7864320
  1304.9 417.8 %all-reduce.8.cloned.1.call-start = ((), (), s32[]{:S(2)}) async-start(), calls=%async_computation.8 | async-start | bytes 8421376 | tf_op jit(solution)/shard_map/psum | solution.py:532
  1394.5 334.7 %reduce-scatter.32.cloned.1.call-start = ((), (), s32[]{:S(2)}) async-start(), calls=%async_computation.17 | async-start | bytes 20971520
  1395.1 334.1 %reduce-scatter.20.cloned.1.call-start = ((), (), s32[]{:S(2)}) async-start(), calls=%async_computation.9 | async-start | bytes 20971520 | tf_op jit(solution)/shard_map/reduce_scatter | solution.py:513
  1649.3 63.6 %copy-start = (bf16[1,768,2048]{2,1,0:T(8,128)(2,1)S(1)}, bf16[1,768,2048]{2,1,0:T(8,128)(2,1)}, u32[]{:S(2)}) copy-start(bf16[1,768,2048]{2,1,0:T(8,128)(2,1)} %reduce-scatter.24.cloned.1.call-done) | copy-start | bytes 9437188
Sparse Core Ops, SparseCore 0:
  18.0 46.3 all-gather.9
  65.9 55.4 all-gather.7
  122.9 55.4 all-gather.5
  623.5 161.7 reduce-scatter.25
  888.8 94.2 reduce-scatter.21
  1113.8 94.3 reduce-scatter.27
  1210.7 94.0 reduce-scatter.23
  1307.3 53.2 reduce-scatter.29
  1394.6 80.3 all-reduce.7
  1477.9 119.5 reduce-scatter.31
  1600.6 119.4 reduce-scatter.19
where the time goes:
time: 1750 us; the launch traced here: 1740 us
  matrix products  768 us (44%)
  Pallas kernels  598 us (34%)
  waiting for transfers between devices  326 us (19%)
    pallas_call x13, Pallas kernels, run(): pl.pallas_call(kernel, grid_spec=spec, out_shape=out_shape, input_output_...  598 us
    dot_general x7, matrix products, dot_tn(): lax.dot_general(a, b, (((0,), (0,)), ((), ())), preferred_element_type=F32)  402 us
    ppermute x4, waiting for transfers between devices, to_chip(): return lax.ppermute(x, 'tp', chip_flip)  259 us
    dot_general x4, matrix products, dot_nt(): lax.dot_general(a, b, (((1,), (1,)), ((), ())), preferred_element_type=F32)  244 us
    dot_general x2, matrix products, dot_nn(): lax.dot_general(a, b, (((1,), (0,)), ((), ())), preferred_element_type=F32)  122 us
  transfers between devices with their start and end apart: 22, of which 8 were waited for; matrix products, arithmetic and copies ran while one was open for 38% of the time, Pallas kernels for 27%

commit v1 on v0

--- a/solution.py
+++ b/solution.py
@@ -68,32 +68,36 @@
     kv_ref[0, :, hd:] = dot_nn(u, wv_ref[...]).astype(BF)
 
 
-def attn_fwd_kernel(me_ref, pre_ref, val_ref, u_ref, wq_ref, kv_ref, cos_ref, sin_ref, token_ref, q_ref, pt_ref, mix_ref, vt_ref, s_ref):
+def attn_fwd_kernel(me_ref, pre_ref, val_ref, u_ref, w0_ref, w1_ref, w2_ref, w3_ref, k0_ref, k1_ref, k2_ref, k3_ref, cos_ref, sin_ref, token_ref,
+                    q_ref, pt_ref, mix_ref, keys_ref, vt_ref, s_ref):
     b = pl.program_id(0)
-    tp_n, _, cols = wq_ref.shape
-    hd = kv_ref.shape[-1] // 2
-    seq = kv_ref.shape[0] * kv_ref.shape[2]
+    cols = w0_ref.shape[1]
+    _, hd = keys_ref.shape
     sl = u_ref.shape[1]
-    heads = tp_n * cols // hd
+    heads = q_ref.shape[2] // hd
     u = u_ref[0]
+    me = me_ref[0]
     cos_t, sin_t = cos_ref[...], sin_ref[...]
-    keys = kv_ref[:, 0, :, :hd].reshape(seq, hd)
-    vt_ref[...] = kv_ref[:, 0, :, hd:].reshape(seq, hd).astype(F32).T.astype(BF)
-    for s in range(tp_n):
-        qs = dot_nn(u, wq_ref[s])
+    place = []
+    for r, kv_ref in enumerate((k0_ref, k1_ref, k2_ref, k3_ref)):
+        keys_ref[r * sl : (r + 1) * sl, :] = kv_ref[0, :, :hd]
+        vt_ref[:, r * sl : (r + 1) * sl] = kv_ref[0, :, hd:].astype(F32).T.astype(BF)
+        place.append(lax.broadcasted_iota(jnp.int32, (sl, sl), 0) + (me ^ r) * sl)
+    for r, w_ref in enumerate((w0_ref, w1_ref, w2_ref, w3_ref)):
+        qs = dot_nn(u, w_ref[...])
         for j in range(cols // hd):
-            base = (s * (cols // hd) + j) * hd
+            base = r * cols + j * hd
             first, second = rope_fwd(qs[:, j * hd : (j + 1) * hd], cos_t, sin_t)
             q_ref[0, :, base : base + hd // 2] = first.astype(BF)
             q_ref[0, :, base + hd // 2 : base + hd] = second.astype(BF)
     prefix, valid = pre_ref[b], val_ref[b]
-    q_end = lax.broadcasted_iota(jnp.int32, (1, sl), 1) + (me_ref[0] * sl + 1)
+    q_end = lax.broadcasted_iota(jnp.int32, (1, sl), 1) + (me * sl + 1)
     limit = jnp.minimum(valid, jnp.maximum(prefix, q_end))
-    visible = lax.broadcasted_iota(jnp.int32, (seq, sl), 0) < limit
+    visible = jnp.concatenate(place, axis=0) < limit
     scale = (hd**-0.5) * math.log2(math.e)
 
     def scores(h):
-        return dot_nt(keys, q_ref[0, :, h * hd : (h + 1) * hd])
+        return dot_nt(keys_ref[...], q_ref[0, :, h * hd : (h + 1) * hd])
 
     s_ref[0] = scores(0)
     for h in range(heads):
@@ -107,8 +111,23 @@
         mix_ref[0, :, h * hd : (h + 1) * hd] = dot_nn(vt_ref[...], p).T.astype(BF)
 
 
-def out_kernel(mix_ref, wo_ref, h_ref, gain_ref, *rest):
-    resid_ref, z_ref = rest[-2:]
+def fetch_at_first(refs, dst, axis, sems):
+    @pl.when(pl.program_id(0) == 0)
+    def _():
+        at, copies = 0, []
+        for i, ref in enumerate(refs):
+            n = ref.shape[axis]
+            copies.append(pltpu.make_async_copy(ref, dst.at[pl.ds(at, n), :] if axis == 0 else dst.at[:, pl.ds(at, n)], sems.at[i]))
+            at += n
+        for c in copies:
+            c.start()
+        for c in copies:
+            c.wait()
+
+
+def out_kernel(mix_ref, w0_ref, w1_ref, w2_ref, w3_ref, h_ref, gain_ref, *rest):
+    resid_ref, z_ref, wo_ref, sems = rest[-4:]
+    fetch_at_first((w0_ref, w1_ref, w2_ref, w3_ref), wo_ref, 0, sems)
     x = (h_ref[0].astype(F32) + dot_nn(mix_ref[0], wo_ref[...])).astype(BF)
     resid_ref[0] = x
     x = x.astype(F32)
@@ -134,33 +153,35 @@
             c.wait()
 
 
-def dact_near_kernel(me_ref, ga_ref, gb_ref, wd_ref, *rest):
-    da_ref, cat0_ref, cat1_ref, own0_ref, own1_ref, sems = rest[-6:]
-    half = ga_ref.shape[0] // 2
-    rows, dim = half * ga_ref.shape[1], ga_ref.shape[2]
-    chip, core = me_ref[0] // 2, me_ref[0] % 2
+def dact_near_kernel(rel, me_ref, g_ref, wd_ref, *rest):
+    outs, sems = rest[-4 if rel else -6 : -1], rest[-1]
+    da_ref, cats, owns = outs[0], outs[1:3], outs[3:]
+    half = g_ref.shape[0] // 2
+    rows, dim = half * g_ref.shape[1], g_ref.shape[2]
+    chip = me_ref[0] // 2
+    core = abs(rel - me_ref[0] % 2)
     src, dst = [], []
-    for c, (cat, own) in enumerate(((cat0_ref, own0_ref), (cat1_ref, own1_ref))):
-        mine = ga_ref.at[pl.ds(c * half, half)]
-        src += [mine, gb_ref.at[pl.ds(c * half, half)], mine]
-        dst += [cat.at[chip, core], cat.at[chip, 1 - core], own]
+    for c in range(2):
+        piece = g_ref.at[pl.ds(c * half, half)]
+        src.append(piece)
+        dst.append(cats[c].at[chip, core])
+        if owns:
+            src.append(piece)
+            dst.append(owns[c])
     copies = place_copies(src, dst, sems)
     start_at_first(copies)
-    for c in range(2):
-        for rel, ref in enumerate((ga_ref, gb_ref)):
-            g = ref[c * half : (c + 1) * half].reshape(rows, dim)
-            da_ref[c, rel] = dot_nt(g, wd_ref[...]).astype(BF)
+    da_ref[...] = dot_nt(g_ref[...].reshape(2 * rows, dim), wd_ref[...]).astype(BF).reshape(da_ref.shape)
     wait_at_last(copies)
 
 
 def dact_far_kernel(me_ref, ga_ref, gb_ref, wd_ref, *rest):
-    da_ref, cat_ref, sems = rest[-3:]
+    da_ref, db_ref, cat_ref, sems = rest[-4:]
     rows, dim = ga_ref.shape[0] * ga_ref.shape[1], ga_ref.shape[2]
     chip, core = 1 - me_ref[0] // 2, me_ref[0] % 2
     copies = place_copies([ga_ref, gb_ref], [cat_ref.at[chip, core], cat_ref.at[chip, 1 - core]], sems)
     start_at_first(copies)
-    for rel, ref in enumerate((ga_ref, gb_ref)):
-        da_ref[0, rel] = dot_nt(ref[...].reshape(rows, dim), wd_ref[...]).astype(BF)
+    for ref, o_ref in ((ga_ref, da_ref), (gb_ref, db_ref)):
+        o_ref[0] = dot_nt(ref[...].reshape(rows, dim), wd_ref[...]).astype(BF)
     wait_at_last(copies)
 
 
@@ -174,7 +195,7 @@
     return (gelu * up).astype(BF), (da * up * slope).astype(BF), (da * gelu).astype(BF)
 
 
-def mlp_kernel(other, me_ref, za_ref, zb_ref, da_ref, wg_ref, wu_ref, *rest):
+def mlp_kernel(other, me_ref, za_ref, zb_ref, da_ref, db_ref, wg_ref, wu_ref, *rest):
     act_ref, dg_ref, du_ref, cat_ref, sems = rest[-5:]
     rows, dim = za_ref.shape[0] * za_ref.shape[1], za_ref.shape[2]
     core = me_ref[0] % 2
@@ -182,12 +203,12 @@
     copies = place_copies([za_ref, zb_ref], [cat_ref.at[chip, core], cat_ref.at[chip, 1 - core]], sems)
     start_at_first(copies)
     step = rows // 2
-    for rel, ref in enumerate((za_ref, zb_ref)):
+    for rel, (ref, d_ref) in enumerate(((za_ref, da_ref), (zb_ref, db_ref))):
         place = core if rel == 0 else 1 - core
         z = ref[...].reshape(rows, dim)
         for r in range(0, rows, step):
             zr = z[r : r + step]
-            out = gated(dot_nn(zr, wg_ref[...]), dot_nn(zr, wu_ref[...]), da_ref[0, rel, r : r + step, :].astype(F32))
+            out = gated(dot_nn(zr, wg_ref[...]), dot_nn(zr, wu_ref[...]), d_ref[0, r : r + step, :].astype(F32))
             for o_ref, o in zip((act_ref, dg_ref, du_ref), out):
                 o_ref[0, place, r : r + step, :] = o
     wait_at_last(copies)
@@ -213,14 +234,15 @@
     wait_at_last(copies)
 
 
-def attn_bwd_kernel(me_ref, dz0_ref, dz1_ref, res_ref, go_ref, gain_ref, wo_ref, kv_ref, q_ref, pt_ref, cos_ref, sin_ref, token0_ref, token1_ref, token2_ref,
-                    dres_ref, dq_ref, dkv_ref, gn_ref, kt_ref, do_ref, qs_ref, ds_ref, dp_ref):
+def attn_bwd_kernel(me_ref, dz0_ref, dz1_ref, res_ref, go_ref, gain_ref, w0_ref, w1_ref, w2_ref, w3_ref, k0_ref, k1_ref, k2_ref, k3_ref,
+                    q_ref, pt_ref, cos_ref, sin_ref, token0_ref, token1_ref, token2_ref,
+                    dres_ref, dq_ref, dkv_ref, gn_ref, kt_ref, v_ref, do_ref, qs_ref, ds_ref, dp_ref):
     b = pl.program_id(0)
     half = pl.num_programs(0) // 2
-    hd = kv_ref.shape[-1] // 2
-    seq = kv_ref.shape[0] * kv_ref.shape[2]
+    seq, hd = v_ref.shape
     sl = q_ref.shape[1]
     heads = q_ref.shape[2] // hd
+    me = me_ref[0]
     x = res_ref[0].astype(F32)
     dz = jnp.where(b < half, dz0_ref[0], dz1_ref[0]).astype(F32)
     inv = lax.rsqrt(jnp.mean(x * x, axis=-1, keepdims=True) + EPS)
@@ -239,17 +261,21 @@
     dx = inv * (dxn - xn * jnp.mean(dxn * xn, axis=-1, keepdims=True))
     dres = (go_ref[0].astype(F32) + dx).astype(BF)
     dres_ref[0] = dres
-    keys = kv_ref[:, 0, :, :hd].reshape(seq, hd)
-    vals = kv_ref[:, 0, :, hd:].reshape(seq, hd)
-    kt_ref[...] = keys.astype(F32).T.astype(BF)
-    for h in range(heads):
-        do_ref[h * sl : (h + 1) * sl, :] = dot_nt(dres, wo_ref[h * hd : (h + 1) * hd, :]).astype(BF)
-        qs_ref[h * sl : (h + 1) * sl, :] = q_ref[0, :, h * hd : (h + 1) * hd]
+    for r, kv_ref in enumerate((k0_ref, k1_ref, k2_ref, k3_ref)):
+        kt_ref[:, r * sl : (r + 1) * sl] = kv_ref[0, :, :hd].astype(F32).T.astype(BF)
+        v_ref[r * sl : (r + 1) * sl, :] = kv_ref[0, :, hd:]
+    for r, w_ref in enumerate((w0_ref, w1_ref, w2_ref, w3_ref)):
+        dm = dot_nt(dres, w_ref[...]).astype(BF)
+        per = w_ref.shape[0] // hd
+        for j in range(per):
+            h = r * per + j
+            do_ref[h * sl : (h + 1) * sl, :] = dm[:, j * hd : (j + 1) * hd]
+            qs_ref[h * sl : (h + 1) * sl, :] = q_ref[0, :, h * hd : (h + 1) * hd]
     scale = hd**-0.5
     cos_t, sin_t = cos_ref[...], sin_ref[...]
 
     def dprobs(h):
-        return dot_nt(vals, do_ref[h * sl : (h + 1) * sl, :])
+        return dot_nt(v_ref[...], do_ref[h * sl : (h + 1) * sl, :])
 
     dp_ref[0] = dprobs(0)
     for h in range(heads):
@@ -263,24 +289,28 @@
         first, second = rope_bwd(dq[:, : hd // 2], dq[:, hd // 2 :], cos_t, sin_t)
         dq_ref[0, :, h * hd : h * hd + hd // 2] = first.astype(BF)
         dq_ref[0, :, h * hd + hd // 2 : (h + 1) * hd] = second.astype(BF)
-    shape = (kv_ref.shape[0], kv_ref.shape[2], hd)
-    dkv_ref[:, 0, :, :hd] = dot_nn(ds_ref[...], qs_ref[...]).astype(BF).reshape(shape)
-    dkv_ref[:, 0, :, hd:] = dot_nn(pt_ref[0], do_ref[...]).astype(BF).reshape(shape)
-
-
-def last_kernel(me_ref, dkv_ref, dq_ref, u_ref, h_ref, dres_ref, gain_ref, wq_ref, wk_ref, wv_ref, cos_ref, sin_ref, gm_ref, token0_ref, token1_ref,
-                gh_ref, gkv_ref, acc_ref):
+    dk = dot_nn(ds_ref[...], qs_ref[...]).astype(BF)
+    dv = dot_nn(pt_ref[0], do_ref[...]).astype(BF)
+    for r in range(seq // sl):
+        dkv_ref[me ^ r, 0, :, :hd] = dk[r * sl : (r + 1) * sl]
+        dkv_ref[me ^ r, 0, :, hd:] = dv[r * sl : (r + 1) * sl]
+
+
+def last_kernel(me_ref, dkv_ref, dq_ref, u_ref, h_ref, dres_ref, gain_ref, w0_ref, w1_ref, w2_ref, w3_ref, wk_ref, wv_ref, cos_ref, sin_ref, gm_ref,
+                token0_ref, token1_ref, gh_ref, gkv_ref, acc_ref, w_ref, d_ref, sems):
     b = pl.program_id(0)
-    tp_n, dim, cols = wq_ref.shape
-    hd = wk_ref.shape[1]
+    dim, hd = wk_ref.shape
+    qd = dq_ref.shape[2]
+    fetch_at_first((w0_ref, w1_ref, w2_ref, w3_ref, wk_ref, wv_ref), w_ref, 1, sems)
     raw = dkv_ref[0]
     dk = raw[:, :hd].astype(F32)
     first, second = rope_bwd(dk[:, : hd // 2], dk[:, hd // 2 :], cos_ref[...], sin_ref[...])
-    dk = jnp.concatenate([first, second], axis=1).astype(BF)
-    dv = raw[:, hd:]
-    dn = dot_nt(dk, wk_ref[...]) + dot_nt(dv, wv_ref[...])
-    for s in range(tp_n):
-        dn = dn + dot_nt(dq_ref[0, :, s * cols : (s + 1) * cols], wq_ref[s])
+    d_ref[:, :qd] = dq_ref[0]
+    d_ref[:, qd : qd + hd // 2] = first.astype(BF)
+    d_ref[:, qd + hd // 2 : qd + hd] = second.astype(BF)
+    d_ref[:, qd + hd :] = raw[:, hd:]
+    dn = dot_nt(d_ref[...], w_ref[...])
+    gk = dot_tn(u_ref[0], d_ref[:, qd:])
     x = h_ref[0].astype(F32)
     inv = lax.rsqrt(jnp.mean(x * x, axis=-1, keepdims=True) + EPS)
     xn = x * inv
@@ -288,7 +318,6 @@
     dxn = dn * gain_ref[...]
     dx = inv * (dxn - xn * jnp.mean(dxn * xn, axis=-1, keepdims=True))
     gh_ref[0] = (dres_ref[0].astype(F32) + dx).astype(BF)
-    gk = dot_tn(u_ref[0], jnp.concatenate([dk, dv], axis=1))
 
     @pl.when(b == 0)
     def _():
@@ -309,8 +338,15 @@
             gkv_ref[dim + per + i : dim + per + i + 1, :] = acc_ref[:, i * width : (i + 1) * width]
 
 
-def wgrad_kernel(x_ref, y_ref, o_ref):
-    o_ref[0] = dot_tn(x_ref[...], y_ref[...])
+def block_grad_kernel(n_add, x_ref, y_ref, *rest):
+    out = dot_tn(x_ref[...], y_ref[...])
+    for ref in rest[:n_add]:
+        out = out + ref[...].reshape(out.shape)
+    rest[-1][...] = out.reshape(rest[-1].shape)
+
+
+def wgrad_kernel(x0_ref, x1_ref, y0_ref, y1_ref, *rest):
+    rest[-1][...] = dot_tn(x0_ref[...], y0_ref[...]) + dot_tn(x1_ref[...], y1_ref[...])
 
 
 def tie_kernel(x_ref, *rest):
@@ -376,7 +412,8 @@
         gain_spec = const_spec((1, dim))
         dma = lambda n: pltpu.SemaphoreType.DMA((n,))
 
-        wq4 = lax.all_gather(w_query, "tp", axis=0)
+        wq_far = to_chip(w_query)
+        wq_mate = to_core(w_query)
         g_mate = to_core(grad_out)
         u, kv = run(
             pre_kernel, (batch,),
@@ -384,29 +421,48 @@
             [tok_spec, kv_spec], [sds((batch, sl, dim)), sds((batch, sl, 2 * hd))],
             (me, hidden, gain1, w_key, w_value, cos_t, sin_t), prefetch=1,
             flops=4 * own * dim * hd, nbytes=6 * own * dim)
-        kv4 = lax.all_gather(kv, "tp", axis=0)
-        wo_all = lax.all_gather(w_out, "tp", axis=0, tiled=True)
+        kv_far = to_chip(kv)
+        kv_mate = to_core(kv)
+        wo_far = to_chip(w_out)
+        wo_mate = to_core(w_out)
 
         bn = 512
         whole_spec = block((batch, sl, dim), lambda n, *_: (0, 0, 0), True)
         half_spec = block((half, sl, dim), lambda n, *_: (0, 0, 0), True)
         cat_shape = (2, 2, half, sl, dim)
-        da_near, gcat0, gcat1, go0, go1 = run(
-            dact_near_kernel, (ffn // bn,),
-            [whole_spec, whole_spec, block((bn, dim), lambda n, *_: (n, 0)), ANY],
-            [block((2, 2, rows, bn), lambda n, *_: (0, 0, 0, n))] + [ANY] * 4,
-            [sds((2, 2, rows, ffn))] + [sds(cat_shape)] * 2 + [sds((half, sl, dim))] * 2,
-            (me, grad_out, g_mate, w_down, kv), prefetch=1, scratch=[dma(6)],
-            flops=8 * rows * dim * ffn, nbytes=2 * ffn * dim + 8 * rows * ffn)
+        da_shape = (2, rows, ffn)
+
+        def dact_near(rel, g, token, cats):
+            return run(
+                functools.partial(dact_near_kernel, rel), (ffn // bn,),
+                [whole_spec, block((bn, dim), lambda n, *_: (n, 0))] + [ANY] * (1 + len(cats)),
+                [block((2, rows, bn), lambda n, *_: (0, 0, n))] + [ANY] * (2 if rel else 4),
+                [sds(da_shape)] + [sds(cat_shape)] * 2 + ([] if rel else [sds((half, sl, dim))] * 2),
+                (me, g, w_down, token, *cats), prefetch=1, scratch=[dma(2 if rel else 4)], aliases={4: 1, 5: 2} if rel else None,
+                flops=4 * rows * dim * ffn, nbytes=2 * ffn * dim + 4 * rows * ffn)
+
+        da_own, gcat0, gcat1, go0, go1 = dact_near(0, grad_out, kv, ())
+        wq_far = tie(wq_far, da_own)
+        wq_far_mate = to_core(wq_far)
+        da_mate, gcat0, gcat1 = dact_near(1, g_mate, da_own, (gcat0, gcat1))
+        kv_far = tie(kv_far, da_mate)
+        kv_far_mate = to_core(kv_far)
+        wqs = (w_query, wq_mate, wq_far, wq_far_mate)
+        kvs = (kv, kv_mate, kv_far, kv_far_mate)
+        wq_specs = [const_spec((dim, cols))] * 4
+        wo_specs = [const_spec((cols, dim))] * 4
 
         q, pt, mixed = run(
             attn_fwd_kernel, (batch,),
-            [tok_spec, const_spec((tp_n, dim, cols)), kv4_spec, rope_spec, rope_spec, ANY],
+            [tok_spec] + wq_specs + [kv_spec] * 4 + [rope_spec, rope_spec, ANY],
             [q_spec, pt_spec, q_spec],
             [sds((batch, sl, qd)), sds((batch, seq, heads * sl)), sds((batch, sl, qd))],
-            (me, prefix_len, valid_len, u, wq4, kv4, cos_t, sin_t, da_near), prefetch=3,
-            scratch=[pltpu.VMEM((hd, seq), BF), pltpu.VMEM((2, seq, sl), F32)],
+            (me, prefix_len, valid_len, u, *wqs, *kvs, cos_t, sin_t, da_mate), prefetch=3,
+            scratch=[pltpu.VMEM((seq, hd), BF), pltpu.VMEM((hd, seq), BF), pltpu.VMEM((2, seq, sl), F32)],
             flops=2 * own * dim * qd + 4 * own * seq * qd, nbytes=2 * own * heads * seq)
+        wo_far = tie(wo_far, mixed)
+        wo_far_mate = to_core(wo_far)
+        wos = (w_out, wo_mate, wo_far, wo_far_mate)
 
         g_far = [to_chip(tie(go0, mixed))]
 
@@ -415,10 +471,11 @@
             extra = [prev] if c else []
             return run(
                 out_kernel, (half,),
-                [block((1, sl, qd), at), const_spec((qd, dim)), block((1, sl, dim), at), gain_spec] + [ANY] * len(extra),
+                [block((1, sl, qd), at)] + [ANY] * 4 + [block((1, sl, dim), at), gain_spec] + [ANY] * len(extra),
                 [block((1, sl, dim), at), block((1, sl, dim), lambda b: (b, 0, 0))],
                 [sds((batch, sl, dim)), sds((half, sl, dim))],
-                (mixed, wo_all, hidden, gain2, *extra), aliases={4: 0} if c else None,
+                (mixed, *wos, hidden, gain2, *extra), aliases={7: 0} if c else None,
+                scratch=[pltpu.VMEM((qd, dim), BF), dma(4)],
                 flops=own * dim * qd, nbytes=4 * own * dim)
 
         resid, z0 = out_proj(0, None)
@@ -431,33 +488,34 @@
 
         o_shape = (2, 2, rows, ffn)
 
-        def mlp(other, c, za, zb, da, prev, token):
+        def mlp(other, c, za, zb, da, db, prev, token):
             extra = list(prev) if prev is not None else []
             o_spec = block((1, 2, rows, bn), lambda n, m: (abs(other - m[0] // 2), 0, 0, n))
             w_spec = block((dim, bn), lambda n, *_: (0, n))
+            d_spec = block((1, rows, bn), lambda n, *_: (c, 0, n))
             return run(
                 functools.partial(mlp_kernel, other), (ffn // bn,),
-                [half_spec, half_spec, block((1, 2, rows, bn), lambda n, *_: (c, 0, 0, n)), w_spec, w_spec] + [ANY] * (len(extra) + 1),
+                [half_spec, half_spec, d_spec, d_spec, w_spec, w_spec] + [ANY] * (len(extra) + 1),
                 [o_spec] * 3 + [ANY], [sds(o_shape)] * 3 + [sds(cat_shape)],
-                (me, za, zb, da, w_gate, w_up, *extra, token),
-                prefetch=1, scratch=[dma(2)], aliases={6 + i: i for i in range(4)} if extra else None,
+                (me, za, zb, da, db, w_gate, w_up, *extra, token),
+                prefetch=1, scratch=[dma(2)], aliases={7 + i: i for i in range(4)} if extra else None,
                 flops=8 * rows * dim * ffn, nbytes=4 * ffn * dim + 16 * rows * ffn)
 
-        near0 = mlp(0, 0, zs[0], z_mate[0], da_near, None, z1)
-        near1 = mlp(0, 1, zs[1], z_mate[1], da_near, None, near0[0])
+        near0 = mlp(0, 0, zs[0], z_mate[0], da_own, da_mate, None, z1)
+        near1 = mlp(0, 1, zs[1], z_mate[1], da_own, da_mate, None, near0[0])
 
         ga = tie(g_far[0], near0[0])
         gb = to_core(ga)
-        da_far, gcat0 = run(
+        da_far, db_far, gcat0 = run(
             dact_far_kernel, (ffn // bn,),
             [half_spec, half_spec, block((bn, dim), lambda n, *_: (n, 0)), ANY, ANY],
-            [block((1, 2, rows, bn), lambda n, *_: (0, 0, 0, n)), ANY],
-            [sds((1, 2, rows, ffn)), sds(cat_shape)],
-            (me, ga, gb, w_down, gcat0, near1[0]), prefetch=1, scratch=[dma(2)], aliases={4: 1},
+            [block((1, rows, bn), lambda n, *_: (0, 0, n))] * 2 + [ANY],
+            [sds((1, rows, ffn))] * 2 + [sds(cat_shape)],
+            (me, ga, gb, w_down, gcat0, near1[0]), prefetch=1, scratch=[dma(2)], aliases={4: 2},
             flops=4 * rows * dim * ffn, nbytes=2 * ffn * dim + 4 * rows * ffn)
         za = tie(z_far[0], near1[0])
         zb = to_core(za)
-        full0 = mlp(1, 0, za, zb, da_far, near0, da_far)
+        full0 = mlp(1, 0, za, zb, da_far, db_far, near0, da_far)
 
         def gated_grad(full):
             flat = (4 * rows, ffn)
@@ -493,50 +551,70 @@
         part1 = scatter(mlp_part1)
         hidden_out = (resid.astype(F32) + jnp.concatenate([part0, part1]).astype(F32)).astype(BF)
 
-        def grad_half(a, b):
-            return dot_tn(a.reshape(4 * rows, -1), b.reshape(4 * rows, -1))
-
-        g_down_half = grad_half(full0[0], gcat0)
+        def weight_grad(x, y, token):
+            x0, x1 = (a.reshape(4 * rows, -1) for a in x)
+            y0, y1 = (a.reshape(4 * rows, -1) for a in y)
+            m, n = x0.shape[1], y0.shape[1]
+            bm, by = 1024, 512
+            x_spec = block((4 * rows, bm), lambda i, j: (0, i))
+            y_spec = block((4 * rows, by), lambda i, j: (0, j))
+            return run(
+                wgrad_kernel, (m // bm, n // by), [x_spec, x_spec, y_spec, y_spec, ANY], block((bm, by), lambda i, j: (i, j)),
+                sds((m, n), F32), (x0, x1, y0, y1, token), flops=16 * rows * m * n, nbytes=4 * m * n)
+
+        g_down = weight_grad((full0[0], full1[0]), (gcat0, gcat1), mlp_part1)
 
         d_resid, d_q, dkv_part, gn2 = run(
             attn_bwd_kernel, (batch,),
             [block((1, sl, dim), lambda b, *_: (jnp.minimum(b, half - 1), 0, 0)), block((1, sl, dim), lambda b, *_: (jnp.maximum(b - half, 0), 0, 0)),
-             tok_spec, tok_spec, gain_spec, const_spec((qd, dim)), kv4_spec, q_spec, pt_spec, rope_spec, rope_spec, ANY, ANY, ANY],
+             tok_spec, tok_spec, gain_spec] + wo_specs + [kv_spec] * 4 + [q_spec, pt_spec, rope_spec, rope_spec, ANY, ANY, ANY],
             [tok_spec, q_spec, kv4_spec, block((1, dim), lambda b, *_: (0, 0))],
             [sds((batch, sl, dim)), sds((batch, sl, qd)), sds((tp_n, batch, sl, 2 * hd)), sds((1, dim), F32)],
-            (me, dz0, dz1, resid, grad_out, gain2, wo_all, kv4, q, pt, cos_t, sin_t, mlp_part1, g_down_half, part0), prefetch=1,
-            scratch=[pltpu.VMEM((hd, seq), BF), pltpu.VMEM((heads * sl, hd), BF), pltpu.VMEM((heads * sl, hd), BF), pltpu.VMEM((seq, heads * sl), BF), pltpu.VMEM((2, seq, sl), F32)],
+            (me, dz0, dz1, resid, grad_out, gain2, *wos, *kvs, q, pt, cos_t, sin_t, mlp_part1, g_down, part0), prefetch=1,
+            scratch=[pltpu.VMEM((hd, seq), BF), pltpu.VMEM((seq, hd), BF), pltpu.VMEM((heads * sl, hd), BF), pltpu.VMEM((heads * sl, hd), BF), pltpu.VMEM((seq, heads * sl), BF), pltpu.VMEM((2, seq, sl), F32)],
             flops=2 * own * dim * qd + 8 * own * seq * qd, nbytes=2 * own * heads * seq)
         dkv = lax.psum_scatter(tie(dkv_part, part1), "tp", scatter_dimension=0)
 
-        g_out = dot_tn(mixed.reshape(own, qd), d_resid.reshape(own, dim))
-        g_out_sum = lax.psum_scatter(g_out, "tp", scatter_dimension=0, tiled=True)
-        bm = dim // 2
-        g_query = run(
-            wgrad_kernel, (dim // bm, tp_n),
-            [block((own, bm), lambda i, j: (0, i)), block((own, cols), lambda i, j: (0, j))],
-            block((1, bm, cols), lambda i, j: (j, i, 0)), sds((tp_n, dim, cols), F32),
-            (u.reshape(own, dim), d_q.reshape(own, qd)), flops=2 * own * dim * qd, nbytes=4 * dim * qd)
-        g_query_sum = lax.psum_scatter(g_query, "tp", scatter_dimension=0)
+        mixed2, dres2, u2, dq2 = mixed.reshape(own, qd), d_resid.reshape(own, dim), u.reshape(own, dim), d_q.reshape(own, qd)
+
+        def block_grad(of_query, count, first, stride, adds, token):
+            pick = lambda j: (0, first + stride * j)
+            full, part = block((own, dim), lambda j: (0, 0), True), block((own, cols), pick)
+            o_dims = (dim, cols) if of_query else (cols, dim)
+            o_spec = block((1,) + o_dims, lambda j: (j, 0, 0))
+            return run(
+                functools.partial(block_grad_kernel, len(adds)), (count,),
+                ([full, part] if of_query else [part, full]) + [block((1,) + o_dims, lambda j, k=k: (k, 0, 0), True) for _, k in adds] + [ANY],
+                o_spec, sds((count,) + o_dims, F32), ((u2, dq2) if of_query else (mixed2, dres2)) + tuple(a for a, _ in adds) + (token,),
+                flops=2 * count * own * dim * cols, nbytes=4 * count * dim * cols)
+
+        to_mate = [block_grad(False, 2, 1, 2, (), d_resid)]
+        to_mate.append(block_grad(True, 2, 1, 2, (), to_mate[0]))
+        from_mate = [to_core(x) for x in to_mate]
+        far_sum = [block_grad(False, 1, 2, 1, ((from_mate[0], 1),), to_mate[1])]
+        far_sum.append(block_grad(True, 1, 2, 1, ((from_mate[1], 1),), far_sum[0]))
+        go_arrived = to_chip(far_sum[0])
+        gq_arrived = to_chip(far_sum[1])
 
         extra = dim // hd
         grad_hidden, gkv = run(
             last_kernel, (batch,),
             [kv_spec, q_spec, tok_spec, tok_spec, tok_spec, gain_spec,
-             const_spec((tp_n, dim, cols)), const_spec((dim, hd)), const_spec((dim, hd)), rope_spec, rope_spec, const_spec((1, dim)), ANY, ANY],
+             ] + [ANY] * 6 + [rope_spec, rope_spec, const_spec((1, dim)), ANY, ANY],
             [tok_spec, block((dim + extra, 2 * hd), lambda b, *_: (0, 0))],
             [sds((batch, sl, dim)), sds((dim + extra, 2 * hd), F32)],
-            (me, dkv, d_q, u, hidden, d_resid, gain1, wq4, w_key, w_value, cos_t, sin_t, gn2, g_out, g_query), prefetch=1,
-            scratch=[pltpu.VMEM((1, dim), F32)],
+            (me, dkv, d_q, u, hidden, d_resid, gain1, *wqs, w_key, w_value, cos_t, sin_t, gn2, *far_sum), prefetch=1,
+            scratch=[pltpu.VMEM((1, dim), F32), pltpu.VMEM((dim, qd + 2 * hd), BF), pltpu.VMEM((sl, qd + 2 * hd), BF), dma(6)],
             flops=2 * own * dim * (qd + 4 * hd), nbytes=8 * own * dim)
         gkv = lax.psum(gkv, "tp")
         g_key, g_value = gkv[:dim, :hd], gkv[:dim, hd:]
         g_mlp_norm = gkv[dim : dim + extra // 2].reshape(dim)
         g_attn_norm = gkv[dim + extra // 2 :].reshape(dim)
 
-        g_down = g_down_half + grad_half(full1[0], gcat1)
-        g_gate = grad_half(full0[3], full0[1]) + grad_half(full1[3], full1[1])
-        g_up = grad_half(full0[3], full0[2]) + grad_half(full1[3], full1[2])
+        g_gate = weight_grad((full0[3], full1[3]), (full0[1], full1[1]), grad_hidden)
+        g_up = weight_grad((full0[3], full1[3]), (full0[2], full1[2]), g_gate)
+        g_out_sum = block_grad(False, 1, 0, 1, ((from_mate[0], 0), (go_arrived, 0)), g_gate)[0]
+        g_query_sum = block_grad(True, 1, 0, 1, ((from_mate[1], 0), (gq_arrived, 0)), g_up)[0]
         return (hidden_out, grad_hidden, g_attn_norm, g_query_sum, g_key, g_value, g_out_sum, g_mlp_norm, g_gate, g_up, g_down)
 
     return jax.shard_map(local_layer, mesh=mesh, in_specs=in_specs, out_specs=out_specs, check_vma=False)

time: 1750 us -> 1480 us (0.85)
  Pallas kernels: 598 us -> 1000 us
  matrix products: 768 us -> 367 us
  waiting for transfers between devices: 326 us -> 45.4 us
    pallas_call x13 -> x22, Pallas kernels: 598 us -> 1000 us  [run(): pl.pallas_call(kernel, grid_spec=spec, out_shape=out_shape, input_output_...]
    dot_general x7 -> x0, matrix products: 402 us -> none  [dot_tn(): lax.dot_general(a, b, (((0,), (0,)), ((), ())), preferred_element_type=F32)]
    ppermute x4 -> x9, waiting for transfers between devices: 259 us -> 38.5 us  [to_chip(): return lax.ppermute(x, 'tp', chip_flip)]
    all_gather x3 -> x0, waiting for transfers between devices: 40.8 us -> none  [the longest x1 28.3 us: local_layer(): wq4 = lax.all_gather(w_query, 'tp', axis=0)]
  transfers between devices with their start and end apart: 22 -> 30, of which waited for: 8 -> 5; matrix products, arithmetic and copies ran while one was open for 38% -> 26% of each run, Pallas kernels for 27% -> 67%
where the time goes in v1:
time: 1480 us; the launch traced here: 1470 us
  Pallas kernels  1000 us (68%)
  matrix products  367 us (25%)
  waiting for transfers between devices  45.4 us (3%)
  local copies, waits for them, and re-layouts  15.2 us (1%)
  between operations  14.9 us (1%)
  starting transfers between devices  14.8 us (1%)
    pallas_call x22, Pallas kernels, run(): pl.pallas_call(kernel, grid_spec=spec, out_shape=out_shape, input_output_...  1000 us
    dot_general x4, matrix products, dot_nt(): lax.dot_general(a, b, (((1,), (1,)), ((), ())), preferred_element_type=F32)  246 us
    dot_general x2, matrix products, dot_nn(): lax.dot_general(a, b, (((1,), (0,)), ((), ())), preferred_element_type=F32)  121 us
    ppermute x9, waiting for transfers between devices, to_chip(): return lax.ppermute(x, 'tp', chip_flip)  38.5 us
  transfers between devices with their start and end apart: 30, of which 5 were waited for; matrix products, arithmetic and copies ran while one was open for 26% of the time, Pallas kernels for 67%

profile of v1, /device:TPU:0, one launch (start us, length us, event | category | flops | bytes accessed | tf_op | source)
XLA Modules:
  0.0 1471.0 jit_solution(8742024288282819906)
XLA Ops:
  7.2 0.9 collective-permute-start.5
  8.1 2.9 collective-permute-start.1
  11.1 1.3 convert_add_fusion.1
  12.4 9.3 shard_map.230
  21.7 33.6 %shard_map.231 = (bf16[2,768,4096]{2,1,0:T(8,128)(2,1)}, bf16[2,2,3,256,2048]{4,3,2,1,0:T(8,128)(2,1)}, bf16[2,2,3,256,2048]{4,3,2,1,0:T(8,128)(2,1)}, bf16[3,25...) custom-call(s32[1]{0:T(128)} %bitcast.me_ref, bf16[6,256,2048]{2,1,0:T(8,128)(2,1)} %go_ref.1, bf16[4096,2048]{1,0:T(8,128)(2,1)} %wd_ref.7, ...), custom_call_target="tpu_custom_call" | custom-call | flops 25769803776 | bytes 29360128 | tf_op jit(solution)/shard_map/pallas_call | solution.py:39
  55.3 2.4 collective-permute-done.1.x_ref
  57.8 1.3 copy-done.5
  59.1 32.5 %shard_map.232 = (bf16[2,768,4096]{2,1,0:T(8,128)(2,1)}, bf16[2,2,3,256,2048]{4,3,2,1,0:T(8,128)(2,1)}, bf16[2,2,3,256,2048]{4,3,2,1,0:T(8,128)(2,1)}) custom-call(s32[1]{0:T(128)} %bitcast.me_ref, bf16[6,256,2048]{2,1,0:T(8,128)(2,1)} %collective-permute-done.5.g_ref, bf16[4096,2048]{1,0:T(8,128)(2,1)} %wd_ref.7, ...), custom_call_target="tpu_custom_call", output_to_operand_aliasing={{1}: (4, {}), {2}: (5, {})} | custom-call | flops 25769803776 | bytes 29360128 | tf_op jit(solution)/shard_map/pallas_call | solution.py:39
  92.2 2.0 collective-permute-start.8
  94.2 1.2 collective-permute-done.6.k3_ref
  95.4 1.2 copy-done.7
  96.6 45.1 %shard_map.233 = (bf16[6,256,2048]{2,1,0:T(8,128)(2,1)}, bf16[6,1024,2048]{2,1,0:T(8,128)(2,1)}, bf16[6,256,2048]{2,1,0:T(8,128)(2,1)}) custom-call(s32[1]{0:T(128)} %bitcast.me_ref, s32[6]{0:T(128)} %pre_ref.1, s32[6]{0:T(128)} %val_ref.1, bf16[6,256,2048]{2,1,0:T(8,128)(2,1)} %get-tuple-element.54.u_ref, bf16[2048,512]{1,0:T(8,128)(2,1)} %w0_ref.9, ...), custom_call_target="tpu_custom_call" | custom-call | flops 25769803776 | bytes 25165824 | tf_op jit(solution)/shard_map/pallas_call | solution.py:39
  141.7 1.3 copy-done.1
  144.0 3.4 collective-permute-done.9.w3_ref
  147.4 1.3 copy-done.4
  148.7 14.3 shard_map.234
  163.4 2.0 collective-permute-start.14
  165.4 14.3 shard_map.235
  179.8 67.2 %shard_map.236 = (bf16[2,2,768,4096]{3,2,1,0:T(8,128)(2,1)}, bf16[2,2,768,4096]{3,2,1,0:T(8,128)(2,1)}, bf16[2,2,768,4096]{3,2,1,0:T(8,128)(2,1)}, bf16[2,2,3,256,2048]{4,3,2,1,0:T(8,128)(2,1)}) custom-call(s32[1]{0:T(128)} %bitcast.me_ref, bf16[3,256,2048]{2,1,0:T(8,128)(2,1)} %get-tuple-element.63.za_ref, ...), custom_call_target="tpu_custom_call" | custom-call | flops 51539607552 | bytes 83886080 | tf_op jit(solution)/shard_map/pallas_call | solution.py:39
  247.5 67.4 %shard_map.237 = (bf16[2,2,768,4096]{3,2,1,0:T(8,128)(2,1)}, bf16[2,2,768,4096]{3,2,1,0:T(8,128)(2,1)}, bf16[2,2,768,4096]{3,2,1,0:T(8,128)(2,1)}, bf16[2,2,3,256,2048]{4,3,2,1,0:T(8,128)(2,1)}) custom-call(s32[1]{0:T(128)} %bitcast.me_ref, bf16[3,256,2048]{2,1,0:T(8,128)(2,1)} %get-tuple-element.64.rest_0_.za_ref, ...), custom_call_target="tpu_custom_call" | custom-call | flops 51539607552 | bytes 83886080 | tf_op jit(solution)/shard_map/pallas_call | solution.py:39
  315.0 1.7 copy-done.3
  316.7 1.8 copy-done.2
  318.5 2.0 collective-permute-start.16
  320.6 32.5 %shard_map.238 = (bf16[1,768,4096]{2,1,0:T(8,128)(2,1)}, bf16[1,768,4096]{2,1,0:T(8,128)(2,1)}, bf16[2,2,3,256,2048]{4,3,2,1,0:T(8,128)(2,1)}) custom-call(s32[1]{0:T(128)} %bitcast.me_ref, bf16[3,256,2048]{2,1,0:T(8,128)(2,1)} %tie.15.ga_ref, bf16[3,256,2048]{2,1,0:T(8,128)(2,1)} %collective-permute-done.15.gb_ref, ...), custom_call_target="tpu_custom_call", output_to_operand_aliasing={{2}: (4, {})} | custom-call | flops 25769803776 | bytes 29360128 | tf_op jit(solution)/shard_map/pallas_call | solution.py:39
  353.1 67.2 %shard_map.239 = (bf16[2,2,768,4096]{3,2,1,0:T(8,128)(2,1)}, bf16[2,2,768,4096]{3,2,1,0:T(8,128)(2,1)}, bf16[2,2,768,4096]{3,2,1,0:T(8,128)(2,1)}, bf16[2,2,3,256,2048]{4,3,2,1,0:T(8,128)(2,1)}) custom-call(s32[1]{0:T(128)} %bitcast.me_ref, ...), custom_call_target="tpu_custom_call", output_to_operand_aliasing={{0}: (7, {}), {1}: (8, {}), {2}: (9, {}), {3}: (10, {})} | custom-call | flops 51539607552 | bytes 83886080 | tf_op jit(solution)/shard_map/pallas_call | solution.py:39
  420.3 36.0 %collective-permute-done.18.x_ref = bf16[3,256,2048]{2,1,0:T(8,128)(2,1)} collective-permute-done((bf16[3,256,2048]{2,1,0:T(8,128)(2,1)}, bf16[3,256,2048]{2,1,0:T(8,128)(2,1)}, u32[]{:S(2)}, u32[]{:S(2)}) %collective-permute-start.18) | collective-permute-done | bytes 3145760 | tf_op jit(solution)/shard_map/ppermute | solution.py:378
  456.4 60.3 %convolution_convert_fusion.1.rest_6_ = bf16[3072,2048]{1,0:T(8,128)(2,1)} fusion(bf16[3072,4096]{1,0:T(8,128)(2,1)} %bitcast.47, bf16[4096,2048]{1,0:T(8,128)(2,1)} %wd_ref.7), kind=kOutput, calls=%fused_computation.4 | convolution fusion | flops 51545899008 | bytes 54525952 | tf_op jit(solution)/shard_map/dot_general | solution.py:21
  516.8 62.2 %fusion.1 = f32[3072,2048]{1,0:T(8,128)} fusion(bf16[3072,4096]{1,0:T(8,128)(2,1)} %bitcast.89, bf16[2048,4096]{1,0:T(8,128)(2,1)} %wu_ref.7), kind=kOutput, calls=%fused_computation.10 | convolution fusion | flops 51539607552 | bytes 67108864 | tf_op jit(solution)/shard_map/dot_general | solution.py:25
  579.0 61.2 %add_convert_fusion.1.rest_5_ = bf16[3072,2048]{1,0:T(8,128)(2,1)} fusion(f32[3072,2048]{1,0:T(8,128)} %fusion.1, bf16[3072,4096]{1,0:T(8,128)(2,1)} %bitcast.87, bf16[2048,4096]{1,0:T(8,128)(2,1)} %wg_ref.7), kind=kOutput, calls=%fused_computation.1 | convolution fusion | flops 51552190464 | bytes 79691776 | tf_op jit(solution)/shard_map/dot_general | solution.py:25
  640.3 99.2 %shard_map.240 = (bf16[2,2,768,4096]{3,2,1,0:T(8,128)(2,1)}, bf16[2,2,768,4096]{3,2,1,0:T(8,128)(2,1)}, bf16[2,2,768,4096]{3,2,1,0:T(8,128)(2,1)}, bf16[2,2,3,25...) custom-call(s32[1]{0:T(128)} %bitcast.me_ref, ...), custom_call_target="tpu_custom_call", output_to_operand_aliasing={{0}: (8, {}), {1}: (9, {}), {2}: (10, {}), {3}: (11, {}), {... | custom-call | flops 77309411328 | bytes 88080384 | tf_op jit(solution)/shard_map/pallas_call | solution.py:39
  739.5 61.1 %fusion.2 = f32[3072,2048]{1,0:T(8,128)} fusion(bf16[3072,4096]{1,0:T(8,128)(2,1)} %bitcast.85, bf16[2048,4096]{1,0:T(8,128)(2,1)} %wu_ref.7), kind=kOutput, calls=%fused_computation.11 | convolution fusion | flops 51539607552 | bytes 67108864 | tf_op jit(solution)/shard_map/dot_general | solution.py:25
  800.6 61.1 %add_convert_fusion = bf16[3072,2048]{1,0:T(8,128)(2,1)} fusion(f32[3072,2048]{1,0:T(8,128)} %fusion.2, bf16[3072,4096]{1,0:T(8,128)(2,1)} %bitcast.83, bf16[2048,4096]{1,0:T(8,128)(2,1)} %wg_ref.7), kind=kOutput, calls=%fused_computation | convolution fusion | flops 51552190464 | bytes 79691776 | tf_op jit(solution)/shard_map/dot_general | solution.py:25
  861.7 61.1 %convolution_convert_fusion.rest_0_.token0_ref = bf16[3072,2048]{1,0:T(8,128)(2,1)} fusion(bf16[3072,4096]{1,0:T(8,128)(2,1)} %bitcast.61, bf16[4096,2048]{1,0:T(8,128)(2,1)} %wd_ref.7), kind=kOutput, calls=%fused_computation.3 | convolution fusion | flops 51545899008 | bytes 54525952 | tf_op jit(solution)/shard_map/dot_general | solution.py:21
  922.9 119.5 %shard_map.241.token1_ref = f32[4096,2048]{1,0:T(8,128)} custom-call(bf16[3072,4096]{1,0:T(8,128)(2,1)} %bitcast.48, bf16[3072,4096]{1,0:T(8,128)(2,1)} %bitcast.62, bf16[3072,2048]{1,0:T(8,128)(2,1)} %bitcast.95, bf16[3072,2048]{1,0:T(8,128)(2,1)} %bitcast.96, bf16[3072,2048]{1,0:T(8,128)(2,1)} %convolution_convert_fusion.rest_0_.token0_ref), custom_call_target="tpu_custom_call" | custom-call | flops 103079215104 | bytes 33554432 | tf_op jit(solution)/shard_map/pallas_call | solution.py:39
  1042.4 65.5 %shard_map.242 = (bf16[6,256,2048]{2,1,0:T(8,128)(2,1)}, bf16[6,256,2048]{2,1,0:T(8,128)(2,1)}, bf16[4,6,256,512]{3,2,1,0:T(8,128)(2,1)}, f32[1,2048]{1,0:T(1,128)}) custom-call(s32[1]{0:T(128)} %bitcast.me_ref, bf16[3,256,2048]{2,1,0:T(8,128)(2,1)} %bitcast.80, bf16[3,256,2048]{2,1,0:T(8,128)(2,1)} %bitcast.81, ...), custom_call_target="tpu_custom_call" | custom-call | flops 38654705664 | bytes 25165824 | tf_op jit(solution)/shard_map/pallas_call | solution.py:39
  1108.0 12.4 shard_map.243.rest_0_
  1120.4 12.6 shard_map.244.rest_1_
  1133.6 9.7 add_convert_fusion.2
  1143.3 10.1 shard_map.245.rest_1_.token0_ref
  1153.3 2.1 collective-permute-start.23
  1155.4 10.0 shard_map.246.token1_ref
  1165.4 2.2 reduce-scatter.24.cloned.1.call-done
  1167.6 34.8 %shard_map.247 = (bf16[6,256,2048]{2,1,0:T(8,128)(2,1)}, f32[2056,512]{1,0:T(8,128)}) custom-call(s32[1]{0:T(128)} %bitcast.me_ref, bf16[6,256,512]{2,1,0:T(8,128)(2,1)} %bitcast.82, bf16[6,256,2048]{2,1,0:T(8,128)(2,1)} %get-tuple-element.90.dq_ref, bf16[6,256,2048]{2,1,0:T(8,128)(2,1)} %get-tuple-element.54.u_ref, bf16[6,256,2048]{2,1,0:T(8,128)(2,1)} %h_ref.7, ...), custom_call_target="tpu_custom_call" | custom-call | flops 19327352832 | bytes 25165824 | tf_op jit(solution)/shard_map/pallas_call | solution.py:39
  1202.4 116.4 %shard_map.248.rest_0_.rest_2_ = f32[2048,4096]{1,0:T(8,128)} custom-call(bf16[3072,2048]{1,0:T(8,128)(2,1)} %bitcast.93, bf16[3072,2048]{1,0:T(8,128)(2,1)} %bitcast.91, bf16[3072,4096]{1,0:T(8,128)(2,1)} %bitcast.88, bf16[3072,4096]{1,0:T(8,128)(2,1)} %bitcast.84, bf16[6,256,2048]{2,1,0:T(8,128)(2,1)} %get-tuple-element.44.rest_0_), custom_call_target="tpu_custom_call" | custom-call | flops 103079215104 | bytes 33554432 | tf_op jit(solution)/shard_map/pallas_call | solution.py:39
  1318.8 115.9 %shard_map.249.rest_2_ = f32[2048,4096]{1,0:T(8,128)} custom-call(bf16[3072,2048]{1,0:T(8,128)(2,1)} %bitcast.94, bf16[3072,2048]{1,0:T(8,128)(2,1)} %bitcast.92, bf16[3072,4096]{1,0:T(8,128)(2,1)} %bitcast.90, bf16[3072,4096]{1,0:T(8,128)(2,1)} %bitcast.86, f32[2048,4096]{1,0:T(8,128)} %shard_map.248.rest_0_.rest_2_), custom_call_target="tpu_custom_call" | custom-call | flops 103079215104 | bytes 33554432 | tf_op jit(solution)/shard_map/pallas_call | solution.py:39
  1434.7 11.3 shard_map.251
  1446.0 11.2 shard_map.250
  1459.2 4.5 fusion
  (79 shorter events, 5.7 us)
Async XLA Ops:
  7.2 1035.2 %reduce-scatter.16.cloned.1.call-start = ((), (), s32[]{:S(2)}) async-start(), calls=%async_computation.6 | async-start | bytes 15728640
  7.2 51.9 %collective-permute-start.5 = (bf16[6,256,2048]{2,1,0:T(8,128)(2,1)}, bf16[6,256,2048]{2,1,0:T(8,128)(2,1)}, u32[]{:S(2)}, u32[]{:S(2)}) collective-permute-start(bf16[6,256,2048]{2,1,0:T(8,128)(2,1)} %go_ref.1), channel_id=1, source_target_pairs={{0,1},{1,0},{2,3},{3,2},{4,5},{5,4},{6,7},{7,6}} | collective-permute-start | bytes 18874376 | tf_op jit(solution)/shard_map/ppermute | solution.py:375
  8.1 86.2 %collective-permute-start = (bf16[2048,512]{1,0:T(8,128)(2,1)}, bf16[2048,512]{1,0:T(8,128)(2,1)}, u32[]{:S(2)}, u32[]{:S(2)}) collective-permute-start(bf16[2048,512]{1,0:T(8,128)(2,1)} %w0_ref.9), channel_id=1, source_target_pairs={{0,1},{1,0},{2,3},{3,2},{4,5},{5,4},{6,7},{7,6}} | collective-permute-start | bytes 6291464 | tf_op jit(solution)/shard_map/ppermute | solution.py:375
  8.1 49.6 %collective-permute-start.1 = (bf16[2048,512]{1,0:T(8,128)(2,1)}, bf16[2048,512]{1,0:T(8,128)(2,1)S(1)}, u32[]{:S(2)}, u32[]{:S(2)}) collective-permute-start(bf16[2048,512]{1,0:T(8,128)(2,1)} %w0_ref.9), channel_id=1, source_target_pairs={{0,2},{2,0},{1,3},{3,1},{4,6},{6,4},{5,7},{7,5}} | collective-permute-start | bytes 6291464 | tf_op jit(solution)/shard_map/ppermute | solution.py:378
  21.6 70.6 %collective-permute-start.3 = (bf16[6,256,512]{2,1,0:T(8,128)(2,1)}, bf16[6,256,512]{2,1,0:T(8,128)(2,1)}, u32[]{:S(2)}, u32[]{:S(2)}) collective-permute-start(bf16[6,256,512]{2,1,0:T(8,128)(2,1)} %get-tuple-element.55.rest_0_.k0_ref), channel_id=1, source_target_pairs={{0,1},{1,0},{2,3},{3,2},{4,5},{5,4},{6,7},{7,6}} | collective-permute-start | bytes 4718600 | tf_op jit(solution)/shard_map/ppermute | solution.py:375
  21.6 70.0 %collective-permute-start.4 = (bf16[6,256,512]{2,1,0:T(8,128)(2,1)}, bf16[6,256,512]{2,1,0:T(8,128)(2,1)}, u32[]{:S(2)}, u32[]{:S(2)}) collective-permute-start(bf16[6,256,512]{2,1,0:T(8,128)(2,1)} %get-tuple-element.55.rest_0_.k0_ref), channel_id=1, source_target_pairs={{0,2},{2,0},{1,3},{3,1},{4,6},{6,4},{5,7},{7,5}} | collective-permute-start | bytes 4718600 | tf_op jit(solution)/shard_map/ppermute | solution.py:378
  57.8 1.3 copy-start.5
  59.1 35.2 %collective-permute-start.2 = (bf16[2048,512]{1,0:T(8,128)(2,1)}, bf16[2048,512]{1,0:T(8,128)(2,1)}, u32[]{:S(2)}, u32[]{:S(2)}) collective-permute-start(bf16[2048,512]{1,0:T(8,128)(2,1)} %tie.10.w2_ref), channel_id=1, source_target_pairs={{0,1},{1,0},{2,3},{3,2},{4,5},{5,4},{6,7},{7,6}} | collective-permute-start | bytes 6291464 | tf_op jit(solution)/shard_map/ppermute | solution.py:375
  91.6 3.8 collective-permute-start.6
  92.2 51.8 %collective-permute-start.7 = (bf16[512,2048]{1,0:T(8,128)(2,1)}, bf16[512,2048]{1,0:T(8,128)(2,1)}, u32[]{:S(2)}, u32[]{:S(2)}) collective-permute-start(bf16[512,2048]{1,0:T(8,128)(2,1)} %w0_ref.8), channel_id=1, source_target_pairs={{0,1},{1,0},{2,3},{3,2},{4,5},{5,4},{6,7},{7,6}} | collective-permute-start | bytes 6291464 | tf_op jit(solution)/shard_map/ppermute | solution.py:375
  92.2 49.5 %collective-permute-start.8 = (bf16[512,2048]{1,0:T(8,128)(2,1)}, bf16[512,2048]{1,0:T(8,128)(2,1)S(1)}, u32[]{:S(2)}, u32[]{:S(2)}) collective-permute-start(bf16[512,2048]{1,0:T(8,128)(2,1)} %w0_ref.8), channel_id=1, source_target_pairs={{0,2},{2,0},{1,3},{3,1},{4,6},{6,4},{5,7},{7,5}} | collective-permute-start | bytes 6291464 | tf_op jit(solution)/shard_map/ppermute | solution.py:378
  95.4 1.2 copy-start.7
  96.6 46.8 %copy-start.6 = (bf16[2048]{0:T(1024)(128)(2,1)S(1)}, bf16[2048]{0:T(1024)(128)(2,1)}, u32[]{:S(2)}) copy-start(bf16[2048]{0:T(1024)(128)(2,1)} %param.24) | copy-start | bytes 12292
  141.7 1.3 copy-start.1
  143.0 4.4 collective-permute-start.9
  147.4 1.3 copy-start.4
  163.0 16.8 %collective-permute-start.12 = (bf16[3,256,2048]{2,1,0:T(8,128)(2,1)}, bf16[3,256,2048]{2,1,0:T(8,128)(2,1)}, u32[]{:S(2)}, u32[]{:S(2)}) collective-permute-start(bf16[3,256,2048]{2,1,0:T(8,128)(2,1)} %get-tuple-element.63.za_ref), channel_id=1, source_target_pairs={{0,1},{1,0},{2,3},{3,2},{4,5},{5,4},{6,7},{7,6}} | collective-permute-start | bytes 9437192 | tf_op jit(solution)/shard_map/ppermute | solution.py:375
  163.4 83.6 %collective-permute-start.14 = (bf16[3,256,2048]{2,1,0:T(8,128)(2,1)}, bf16[3,256,2048]{2,1,0:T(8,128)(2,1)}, u32[]{:S(2)}, u32[]{:S(2)}) collective-permute-start(bf16[3,256,2048]{2,1,0:T(8,128)(2,1)} %tie.14), channel_id=1, source_target_pairs={{0,2},{2,0},{1,3},{3,1},{4,6},{6,4},{5,7},{7,5}} | collective-permute-start | bytes 9437192 | tf_op jit(solution)/shard_map/ppermute | solution.py:378
  165.4 149.5 %collective-permute-start.10 = (bf16[3,256,2048]{2,1,0:T(8,128)(2,1)}, bf16[3,256,2048]{2,1,0:T(8,128)(2,1)S(1)}, u32[]{:S(2)}, u32[]{:S(2)}) collective-permute-start(bf16[3,256,2048]{2,1,0:T(8,128)(2,1)} %get-tuple-element.63.za_ref), channel_id=1, source_target_pairs={{0,2},{2,0},{1,3},{3,1},{4,6},{6,4},{5,7},{7,5}} | collective-permute-start | bytes 9437192 | tf_op jit(solution)/shard_map/ppermute | solution.py:378
  179.7 67.7 %collective-permute-start.11 = (bf16[3,256,2048]{2,1,0:T(8,128)(2,1)}, bf16[3,256,2048]{2,1,0:T(8,128)(2,1)}, u32[]{:S(2)}, u32[]{:S(2)}) collective-permute-start(bf16[3,256,2048]{2,1,0:T(8,128)(2,1)} %get-tuple-element.64.rest_0_.za_ref), channel_id=1, source_target_pairs={{0,1},{1,0},{2,3},{3,2},{4,5},{5,4},{6,7},{7,6}} | collective-permute-start | bytes 9437192 | tf_op jit(solution)/shard_map/ppermute | solution.py:375
  247.0 73.6 %collective-permute-start.15 = (bf16[3,256,2048]{2,1,0:T(8,128)(2,1)}, bf16[3,256,2048]{2,1,0:T(8,128)(2,1)}, u32[]{:S(2)}, u32[]{:S(2)}) collective-permute-start(bf16[3,256,2048]{2,1,0:T(8,128)(2,1)} %tie.15.ga_ref), channel_id=1, source_target_pairs={{0,1},{1,0},{2,3},{3,2},{4,5},{5,4},{6,7},{7,6}} | collective-permute-start | bytes 9437192 | tf_op jit(solution)/shard_map/ppermute | solution.py:375
  314.9 1.7 copy-start.3
  316.6 1.9 copy-start.2
  316.6 36.5 %collective-permute-start.13 = (bf16[3,256,2048]{2,1,0:T(8,128)(2,1)}, bf16[3,256,2048]{2,1,0:T(8,128)(2,1)}, u32[]{:S(2)}, u32[]{:S(2)}) collective-permute-start(bf16[3,256,2048]{2,1,0:T(8,128)(2,1)} %tie.13.za_ref), channel_id=1, source_target_pairs={{0,1},{1,0},{2,3},{3,2},{4,5},{5,4},{6,7},{7,6}} | collective-permute-start | bytes 9437192 | tf_op jit(solution)/shard_map/ppermute | solution.py:375
  318.5 101.8 %collective-permute-start.16 = (bf16[3,256,2048]{2,1,0:T(8,128)(2,1)S(1)}, bf16[3,256,2048]{2,1,0:T(8,128)(2,1)}, u32[]{:S(2)}, u32[]{:S(2)}) collective-permute-start(bf16[3,256,2048]{2,1,0:T(8,128)(2,1)S(1)} %copy-done.2), channel_id=1, source_target_pairs={{0,2},{2,0},{1,3},{3,1},{4,6},{6,4},{5,7},{7,5}} | collective-permute-start | bytes 9437192 | tf_op jit(solution)/shard_map/ppermute | solution.py:378
  320.5 135.8 %collective-permute-start.18 = (bf16[3,256,2048]{2,1,0:T(8,128)(2,1)}, bf16[3,256,2048]{2,1,0:T(8,128)(2,1)}, u32[]{:S(2)}, u32[]{:S(2)}) collective-permute-start(bf16[3,256,2048]{2,1,0:T(8,128)(2,1)} %tie.17), channel_id=1, source_target_pairs={{0,2},{2,0},{1,3},{3,1},{4,6},{6,4},{5,7},{7,5}} | collective-permute-start | bytes 9437192 | tf_op jit(solution)/shard_map/ppermute | solution.py:378
  420.3 220.0 %collective-permute-start.17 = (bf16[3,256,2048]{2,1,0:T(8,128)(2,1)}, bf16[3,256,2048]{2,1,0:T(8,128)(2,1)}, u32[]{:S(2)}, u32[]{:S(2)}) collective-permute-start(bf16[3,256,2048]{2,1,0:T(8,128)(2,1)} %tie.16.za_ref), channel_id=1, source_target_pairs={{0,1},{1,0},{2,3},{3,2},{4,5},{5,4},{6,7},{7,6}} | collective-permute-start | bytes 9437192 | tf_op jit(solution)/shard_map/ppermute | solution.py:375
  456.4 183.9 %collective-permute-start.19 = (bf16[3,256,2048]{2,1,0:T(8,128)(2,1)}, bf16[3,256,2048]{2,1,0:T(8,128)(2,1)}, u32[]{:S(2)}, u32[]{:S(2)}) collective-permute-start(bf16[3,256,2048]{2,1,0:T(8,128)(2,1)} %tie.18.ga_ref), channel_id=1, source_target_pairs={{0,1},{1,0},{2,3},{3,2},{4,5},{5,4},{6,7},{7,6}} | collective-permute-start | bytes 9437192 | tf_op jit(solution)/shard_map/ppermute | solution.py:375
  516.7 525.7 %reduce-scatter.20.cloned.1.call-start = ((), (), s32[]{:S(2)}) async-start(), calls=%async_computation.8 | async-start | bytes 15728640
  640.2 402.1 %reduce-scatter.22.cloned.1.call-start = ((), (), s32[]{:S(2)}) async-start(), calls=%async_computation.9 | async-start | bytes 15728640
  861.7 246.2 %reduce-scatter.18.cloned.1.call-start = ((), (), s32[]{:S(2)}) async-start(), calls=%async_computation.7 | async-start | bytes 15728640
  922.8 244.7 %reduce-scatter.24.cloned.1.call-start = ((), (), s32[]{:S(2)}) async-start(), calls=%async_computation.10 | async-start | bytes 7864320
  1107.9 349.2 %all-reduce.7.cloned.1.call-start = ((), (), s32[]{:S(2)}) async-start(), calls=%async_computation.5 | async-start | bytes 8421376 | tf_op jit(solution)/shard_map/psum | solution.py:609
  1120.4 22.9 %collective-permute-start.20 = (f32[2,512,2048]{2,1,0:T(8,128)}, f32[2,512,2048]{2,1,0:T(8,128)}, u32[]{:S(2)}, u32[]{:S(2)}) collective-permute-start(f32[2,512,2048]{2,1,0:T(8,128)} %shard_map.243.rest_0_), channel_id=1, source_target_pairs={{0,1},{1,0},{2,3},{3,2},{4,5},{5,4},{6,7},{7,6}} | collective-permute-start | bytes 25165832 | tf_op jit(solution)/shard_map/ppermute | solution.py:375
  1120.4 13.2 copy-start
  1133.0 22.4 %collective-permute-start.21 = (f32[2,2048,512]{2,1,0:T(8,128)}, f32[2,2048,512]{2,1,0:T(8,128)}, u32[]{:S(2)}, u32[]{:S(2)}) collective-permute-start(f32[2,2048,512]{2,1,0:T(8,128)} %shard_map.244.rest_1_), channel_id=1, source_target_pairs={{0,1},{1,0},{2,3},{3,2},{4,5},{5,4},{6,7},{7,6}} | collective-permute-start | bytes 25165832 | tf_op jit(solution)/shard_map/ppermute | solution.py:375
  1153.3 281.4 %collective-permute-start.23 = (f32[1,512,2048]{2,1,0:T(8,128)}, f32[1,512,2048]{2,1,0:T(8,128)}, u32[]{:S(2)}, u32[]{:S(2)}) collective-permute-start(f32[1,512,2048]{2,1,0:T(8,128)} %shard_map.245.rest_1_.token0_ref), channel_id=1, source_target_pairs={{0,2},{2,0},{1,3},{3,1},{4,6},{6,4},{5,7},{7,5}} | collective-permute-start | bytes 12582920 | tf_op jit(solution)/shard_map/ppermute | solution.py:378
  1165.4 280.6 %collective-permute-start.22 = (f32[1,2048,512]{2,1,0:T(8,128)}, f32[1,2048,512]{2,1,0:T(8,128)}, u32[]{:S(2)}, u32[]{:S(2)}) collective-permute-start(f32[1,2048,512]{2,1,0:T(8,128)} %shard_map.246.token1_ref), channel_id=1, source_target_pairs={{0,2},{2,0},{1,3},{3,1},{4,6},{6,4},{5,7},{7,5}} | collective-permute-start | bytes 12582920 | tf_op jit(solution)/shard_map/ppermute | solution.py:378
Sparse Core Ops, SparseCore 0:
  516.8 95.4 reduce-scatter.15
  640.4 95.5 reduce-scatter.19
  861.8 95.9 reduce-scatter.21
  960.2 94.0 reduce-scatter.17
  1108.1 59.4 reduce-scatter.23
  1202.6 148.4 all-reduce.6

commit v2 on v1

--- a/solution.py
+++ b/solution.py
@@ -261,8 +261,9 @@
     dx = inv * (dxn - xn * jnp.mean(dxn * xn, axis=-1, keepdims=True))
     dres = (go_ref[0].astype(F32) + dx).astype(BF)
     dres_ref[0] = dres
+    scale = hd**-0.5
     for r, kv_ref in enumerate((k0_ref, k1_ref, k2_ref, k3_ref)):
-        kt_ref[:, r * sl : (r + 1) * sl] = kv_ref[0, :, :hd].astype(F32).T.astype(BF)
+        kt_ref[:, r * sl : (r + 1) * sl] = (kv_ref[0, :, :hd].astype(F32) * scale).T.astype(BF)
         v_ref[r * sl : (r + 1) * sl, :] = kv_ref[0, :, hd:]
     for r, w_ref in enumerate((w0_ref, w1_ref, w2_ref, w3_ref)):
         dm = dot_nt(dres, w_ref[...]).astype(BF)
@@ -270,8 +271,7 @@
         for j in range(per):
             h = r * per + j
             do_ref[h * sl : (h + 1) * sl, :] = dm[:, j * hd : (j + 1) * hd]
-            qs_ref[h * sl : (h + 1) * sl, :] = q_ref[0, :, h * hd : (h + 1) * hd]
-    scale = hd**-0.5
+            qs_ref[h * sl : (h + 1) * sl, :] = (q_ref[0, :, h * hd : (h + 1) * hd].astype(F32) * scale).astype(BF)
     cos_t, sin_t = cos_ref[...], sin_ref[...]
 
     def dprobs(h):
@@ -283,7 +283,7 @@
             dp_ref[(h + 1) % 2] = dprobs(h + 1)
         p = pt_ref[0, :, h * sl : (h + 1) * sl].astype(F32)
         t = p * dp_ref[h % 2]
-        ds = ((t - p * jnp.sum(t, axis=0, keepdims=True)) * scale).astype(BF)
+        ds = (t - p * jnp.sum(t, axis=0, keepdims=True)).astype(BF)
         ds_ref[:, h * sl : (h + 1) * sl] = ds
         dq = dot_nn(kt_ref[...], ds).T
         first, second = rope_bwd(dq[:, : hd // 2], dq[:, hd // 2 :], cos_t, sin_t)
@@ -297,11 +297,13 @@
 
 
 def last_kernel(me_ref, dkv_ref, dq_ref, u_ref, h_ref, dres_ref, gain_ref, w0_ref, w1_ref, w2_ref, w3_ref, wk_ref, wv_ref, cos_ref, sin_ref, gm_ref,
-                token0_ref, token1_ref, gh_ref, gkv_ref, acc_ref, w_ref, d_ref, sems):
+                res_ref, p0_ref, p1_ref, token0_ref, gh_ref, gkv_ref, ho_ref, acc_ref, w_ref, d_ref, sems):
     b = pl.program_id(0)
     dim, hd = wk_ref.shape
     qd = dq_ref.shape[2]
     fetch_at_first((w0_ref, w1_ref, w2_ref, w3_ref, wk_ref, wv_ref), w_ref, 1, sems)
+    half = pl.num_programs(0) // 2
+    ho_ref[0] = (res_ref[0].astype(F32) + jnp.where(b < half, p0_ref[0], p1_ref[0]).astype(F32)).astype(BF)
     raw = dkv_ref[0]
     dk = raw[:, :hd].astype(F32)
     first, second = rope_bwd(dk[:, : hd // 2], dk[:, hd // 2 :], cos_ref[...], sin_ref[...])
@@ -338,15 +340,136 @@
             gkv_ref[dim + per + i : dim + per + i + 1, :] = acc_ref[:, i * width : (i + 1) * width]
 
 
-def block_grad_kernel(n_add, x_ref, y_ref, *rest):
-    out = dot_tn(x_ref[...], y_ref[...])
-    for ref in rest[:n_add]:
-        out = out + ref[...].reshape(out.shape)
-    rest[-1][...] = out.reshape(rest[-1].shape)
-
-
-def wgrad_kernel(x0_ref, x1_ref, y0_ref, y1_ref, *rest):
-    rest[-1][...] = dot_tn(x0_ref[...], y0_ref[...]) + dot_tn(x1_ref[...], y1_ref[...])
+def block_grad_kernel(*refs):
+    x_ref, y_ref, o_ref = refs[-4], refs[-3], refs[-1]
+    o_ref[...] = dot_tn(x_ref[...], y_ref[...]).reshape(o_ref.shape)
+
+
+def pair_grad_kernel(x_ref, y_ref, add_ref, token_ref, far_ref, own_ref):
+    out = dot_tn(x_ref[...], y_ref[...]) + add_ref[0]
+
+    @pl.when(pl.program_id(0) == 0)
+    def _():
+        far_ref[0] = out
+
+    @pl.when(pl.program_id(0) == 1)
+    def _():
+        own_ref[0] = out
+
+
+class Flow:
+    def __init__(self, bufs, sems, inward, sides):
+        self.bufs, self.sems, self.inward, self.sides = bufs, sems, inward, sides
+
+    def copies(self, t, slot):
+        out = []
+        for i, (hbm, buf) in enumerate(zip(self.sides(t), self.bufs)):
+            pair = (hbm, buf.at[slot]) if self.inward else (buf.at[slot], hbm)
+            out.append(pltpu.make_async_copy(*pair, self.sems.at[slot, i]))
+        return out
+
+    def start(self, t, slot):
+        for c in self.copies(t, slot):
+            c.start()
+
+    def wait(self, t, slot):
+        for c in self.copies(t, slot):
+            c.wait()
+
+
+def gated_grad_kernel(dg_ref, du_ref, wg_ref, wu_ref, *rest):
+    o_ref, a1, a2, b1, b2, ob, a_sem, b_sem, o_sem = rest[-9:]
+    ni = dg_ref.shape[0] * dg_ref.shape[1]
+    bn = b1.shape[1]
+    nj = wg_ref.shape[0] // bn
+    steps = ni * nj
+    cols = lambda t: pl.ds(pl.multiple_of(lax.rem(t, nj) * bn, bn), bn)
+    a_flow = Flow((a1, a2), a_sem, True, lambda i: (dg_ref.at[i // 2, i % 2], du_ref.at[i // 2, i % 2]))
+    b_flow = Flow((b1, b2), b_sem, True, lambda t: (wg_ref.at[cols(t)], wu_ref.at[cols(t)]))
+    o_flow = Flow((ob,), o_sem, False, lambda t: (o_ref.at[t // nj, :, cols(t)],))
+    a_flow.start(0, 0)
+    b_flow.start(0, 0)
+
+    @pl.loop(0, steps)
+    def _(t):
+        i, slot = t // nj, lax.rem(t, 2)
+        a_slot = lax.rem(i, 2)
+
+        @pl.when(t + 1 < steps)
+        def _():
+            b_flow.start(t + 1, 1 - slot)
+
+        @pl.when(lax.rem(t, nj) == 0)
+        def _():
+            a_flow.wait(i, a_slot)
+
+            @pl.when(i + 1 < ni)
+            def _():
+                a_flow.start(i + 1, 1 - a_slot)
+
+        @pl.when(t >= 2)
+        def _():
+            o_flow.wait(t - 2, slot)
+
+        b_flow.wait(t, slot)
+        ob[slot] = (dot_nt(a1[a_slot], b1[slot]) + dot_nt(a2[a_slot], b2[slot])).astype(BF)
+        o_flow.start(t, slot)
+
+    for t in (steps - 2, steps - 1):
+        o_flow.wait(t, t % 2)
+
+
+def weight_grads_kernel(count, first, ni, *refs):
+    x_refs, y_refs = refs[:2], refs[2 : 2 + 2 * count]
+    o_refs, (x0, x1, y0, y1, ob, x_sem, y_sem, o_sem) = refs[-8 - count : -8], refs[-8:]
+    bm, bn = ob.shape[1:]
+    nj = y_refs[0].shape[1] // bn
+    steps = ni * count * nj
+    per = count * nj
+    rows = lambda i: pl.ds(pl.multiple_of((first + i) * bm, bm), bm)
+    cols = lambda t: pl.ds(pl.multiple_of(lax.rem(t, nj) * bn, bn), bn)
+    x_flow = Flow((x0, x1), x_sem, True, lambda i: [r.at[:, rows(i)] for r in x_refs])
+    y_flows = [Flow((y0, y1), y_sem, True, lambda t, k=k: [r.at[:, cols(t)] for r in y_refs[2 * k : 2 * k + 2]]) for k in range(count)]
+    o_flows = [Flow((ob,), o_sem, False, lambda t, k=k: (o_refs[k].at[rows(t // per), cols(t)],)) for k in range(count)]
+
+    def each(flows, t, act):
+        if count == 1:
+            act(flows[0])
+        else:
+            which = lax.rem(t // nj, count)
+            for k in range(count):
+                pl.when(which == k)(functools.partial(act, flows[k]))
+
+    x_flow.start(0, 0)
+    y_flows[0].start(0, 0)
+
+    @pl.loop(0, steps)
+    def _(t):
+        i, slot = t // per, lax.rem(t, 2)
+        x_slot = lax.rem(i, 2)
+
+        @pl.when(t + 1 < steps)
+        def _():
+            each(y_flows, t + 1, lambda f: f.start(t + 1, 1 - slot))
+
+        @pl.when(lax.rem(t, per) == 0)
+        def _():
+            x_flow.wait(i, x_slot)
+
+            @pl.when(i + 1 < ni)
+            def _():
+                x_flow.start(i + 1, 1 - x_slot)
+
+        @pl.when(t >= 2)
+        def _():
+            o_flows[0].wait(t - 2, slot)
+
+        y_flows[0].wait(t, slot)
+        ob[slot] = dot_tn(x0[x_slot], y0[slot]) + dot_tn(x1[x_slot], y1[slot])
+        each(o_flows, t, lambda f: f.start(t, slot))
+
+    for t in (steps - 2, steps - 1):
+        o_flows[0].wait(t, t % 2)
 
 
 def tie_kernel(x_ref, *rest):
@@ -518,8 +641,12 @@
         full0 = mlp(1, 0, za, zb, da_far, db_far, near0, da_far)
 
         def gated_grad(full):
-            flat = (4 * rows, ffn)
-            return (dot_nt(full[1].reshape(flat), w_gate) + dot_nt(full[2].reshape(flat), w_up)).astype(BF)
+            bj = 512
+            return run(
+                gated_grad_kernel, (), [ANY] * 5, ANY, sds((4, rows, dim)), (full[1], full[2], w_gate, w_up, full[0]),
+                scratch=[pltpu.VMEM((2, rows, ffn), BF)] * 2 + [pltpu.VMEM((2, bj, ffn), BF)] * 2 + [pltpu.VMEM((2, rows, bj), BF)]
+                + [pltpu.SemaphoreType.DMA((2, 2))] * 2 + [pltpu.SemaphoreType.DMA((2, 1))],
+                flops=16 * rows * dim * ffn, nbytes=16 * rows * ffn)
 
         def mlp_out(full):
             return dot_nn(full[0].reshape(4 * rows, ffn), w_down).astype(BF)
@@ -549,20 +676,23 @@
         dz1 = scatter(dz_part1)
         mlp_part1 = mlp_out(full1)
         part1 = scatter(mlp_part1)
-        hidden_out = (resid.astype(F32) + jnp.concatenate([part0, part1]).astype(F32)).astype(BF)
-
-        def weight_grad(x, y, token):
-            x0, x1 = (a.reshape(4 * rows, -1) for a in x)
-            y0, y1 = (a.reshape(4 * rows, -1) for a in y)
-            m, n = x0.shape[1], y0.shape[1]
+
+        def weight_grads(x, ys, tokens, first=0, ni=None, prev=None):
+            flat = lambda pair: [a.reshape(4 * rows, -1) for a in pair]
+            xs, yf = flat(x), [a for y in ys for a in flat(y)]
+            m, n = xs[0].shape[1], yf[0].shape[1]
             bm, by = 1024, 512
-            x_spec = block((4 * rows, bm), lambda i, j: (0, i))
-            y_spec = block((4 * rows, by), lambda i, j: (0, j))
+            extra = [prev] if prev is not None else []
             return run(
-                wgrad_kernel, (m // bm, n // by), [x_spec, x_spec, y_spec, y_spec, ANY], block((bm, by), lambda i, j: (i, j)),
-                sds((m, n), F32), (x0, x1, y0, y1, token), flops=16 * rows * m * n, nbytes=4 * m * n)
-
-        g_down = weight_grad((full0[0], full1[0]), (gcat0, gcat1), mlp_part1)
+                functools.partial(weight_grads_kernel, len(ys), first, ni or m // bm), (),
+                [ANY] * (2 + len(yf) + len(extra) + len(tokens)), [ANY] * len(ys), [sds((m, n), F32)] * len(ys),
+                (*xs, *yf, *extra, *tokens), aliases={2 + len(yf): 0} if extra else None,
+                scratch=[pltpu.VMEM((2, 4 * rows, bm), BF)] * 2 + [pltpu.VMEM((2, 4 * rows, by), BF)] * 2 + [pltpu.VMEM((2, bm, by), F32)]
+                + [pltpu.SemaphoreType.DMA((2, 2))] * 2 + [pltpu.SemaphoreType.DMA((2, 1))],
+                flops=16 * rows * (ni or m // bm) * bm * n * len(ys), nbytes=4 * m * n)
+
+        down_args = (full0[0], full1[0]), ((gcat0, gcat1),)
+        g_down = weight_grads(*down_args, (mlp_part1,), 0, 1)[0]
 
         d_resid, d_q, dkv_part, gn2 = run(
             attn_bwd_kernel, (batch,),
@@ -573,37 +703,36 @@
             (me, dz0, dz1, resid, grad_out, gain2, *wos, *kvs, q, pt, cos_t, sin_t, mlp_part1, g_down, part0), prefetch=1,
             scratch=[pltpu.VMEM((hd, seq), BF), pltpu.VMEM((seq, hd), BF), pltpu.VMEM((heads * sl, hd), BF), pltpu.VMEM((heads * sl, hd), BF), pltpu.VMEM((seq, heads * sl), BF), pltpu.VMEM((2, seq, sl), F32)],
             flops=2 * own * dim * qd + 8 * own * seq * qd, nbytes=2 * own * heads * seq)
-        dkv = lax.psum_scatter(tie(dkv_part, part1), "tp", scatter_dimension=0)
+        dkv = lax.psum_scatter(dkv_part, "tp", scatter_dimension=0)
 
         mixed2, dres2, u2, dq2 = mixed.reshape(own, qd), d_resid.reshape(own, dim), u.reshape(own, dim), d_q.reshape(own, qd)
-
-        def block_grad(of_query, count, first, stride, adds, token):
-            pick = lambda j: (0, first + stride * j)
-            full, part = block((own, dim), lambda j: (0, 0), True), block((own, cols), pick)
-            o_dims = (dim, cols) if of_query else (cols, dim)
-            o_spec = block((1,) + o_dims, lambda j: (j, 0, 0))
-            return run(
-                functools.partial(block_grad_kernel, len(adds)), (count,),
-                ([full, part] if of_query else [part, full]) + [block((1,) + o_dims, lambda j, k=k: (k, 0, 0), True) for _, k in adds] + [ANY],
-                o_spec, sds((count,) + o_dims, F32), ((u2, dq2) if of_query else (mixed2, dres2)) + tuple(a for a, _ in adds) + (token,),
-                flops=2 * count * own * dim * cols, nbytes=4 * count * dim * cols)
-
-        to_mate = [block_grad(False, 2, 1, 2, (), d_resid)]
-        to_mate.append(block_grad(True, 2, 1, 2, (), to_mate[0]))
-        from_mate = [to_core(x) for x in to_mate]
-        far_sum = [block_grad(False, 1, 2, 1, ((from_mate[0], 1),), to_mate[1])]
-        far_sum.append(block_grad(True, 1, 2, 1, ((from_mate[1], 1),), far_sum[0]))
-        go_arrived = to_chip(far_sum[0])
-        gq_arrived = to_chip(far_sum[1])
+        x_spec, y_spec = block((own, dim), lambda j, *_: (0, 0), True), lambda pick: block((own, cols), lambda j, *_: (0, pick(j)))
+        g_out = run(
+            block_grad_kernel, (tp_n,), [y_spec(lambda j: j), x_spec, ANY],
+            block((1, cols, dim), lambda j, m: (m[0] ^ j, 0, 0)), sds((tp_n, cols, dim), F32), (me, mixed2, dres2, dkv_part),
+            prefetch=1, flops=2 * own * dim * qd, nbytes=4 * dim * qd)
+        g_out_sum = lax.psum_scatter(g_out, "tp", scatter_dimension=0)
+        to_mate = run(
+            block_grad_kernel, (2,), [x_spec, y_spec(lambda j: 1 + 2 * j), ANY],
+            block((1, dim, cols), lambda j: (j, 0, 0)), sds((2, dim, cols), F32), (u2, dq2, g_out),
+            flops=own * dim * qd, nbytes=2 * dim * qd)
+        from_mate = to_core(to_mate)
+        g_down = weight_grads(*down_args, (to_mate,), 1, ffn // 1024 - 1, g_down)[0]
+        far_sum, own_sum = run(
+            pair_grad_kernel, (2,), [x_spec, y_spec(lambda j: 2 - 2 * j), block((1, dim, cols), lambda j: (1 - j, 0, 0)), ANY],
+            [block((1, dim, cols), lambda j: (0, 0, 0))] * 2, [sds((1, dim, cols), F32)] * 2, (u2, dq2, from_mate, g_down),
+            flops=own * dim * qd, nbytes=2 * dim * qd)
+        arrived = to_chip(far_sum)
 
         extra = dim // hd
-        grad_hidden, gkv = run(
+        half_at = [block((1, sl, dim), lambda b, *_: (jnp.minimum(b, half - 1), 0, 0)), block((1, sl, dim), lambda b, *_: (jnp.maximum(b - half, 0), 0, 0))]
+        grad_hidden, gkv, hidden_out = run(
             last_kernel, (batch,),
             [kv_spec, q_spec, tok_spec, tok_spec, tok_spec, gain_spec,
-             ] + [ANY] * 6 + [rope_spec, rope_spec, const_spec((1, dim)), ANY, ANY],
-            [tok_spec, block((dim + extra, 2 * hd), lambda b, *_: (0, 0))],
-            [sds((batch, sl, dim)), sds((dim + extra, 2 * hd), F32)],
-            (me, dkv, d_q, u, hidden, d_resid, gain1, *wqs, w_key, w_value, cos_t, sin_t, gn2, *far_sum), prefetch=1,
+             ] + [ANY] * 6 + [rope_spec, rope_spec, const_spec((1, dim)), tok_spec, *half_at, ANY],
+            [tok_spec, block((dim + extra, 2 * hd), lambda b, *_: (0, 0)), tok_spec],
+            [sds((batch, sl, dim)), sds((dim + extra, 2 * hd), F32), sds((batch, sl, dim))],
+            (me, dkv, d_q, u, hidden, d_resid, gain1, *wqs, w_key, w_value, cos_t, sin_t, gn2, resid, part0, part1, far_sum), prefetch=1,
             scratch=[pltpu.VMEM((1, dim), F32), pltpu.VMEM((dim, qd + 2 * hd), BF), pltpu.VMEM((sl, qd + 2 * hd), BF), dma(6)],
             flops=2 * own * dim * (qd + 4 * hd), nbytes=8 * own * dim)
         gkv = lax.psum(gkv, "tp")
@@ -611,10 +740,8 @@
         g_mlp_norm = gkv[dim : dim + extra // 2].reshape(dim)
         g_attn_norm = gkv[dim + extra // 2 :].reshape(dim)
 
-        g_gate = weight_grad((full0[3], full1[3]), (full0[1], full1[1]), grad_hidden)
-        g_up = weight_grad((full0[3], full1[3]), (full0[2], full1[2]), g_gate)
-        g_out_sum = block_grad(False, 1, 0, 1, ((from_mate[0], 0), (go_arrived, 0)), g_gate)[0]
-        g_query_sum = block_grad(True, 1, 0, 1, ((from_mate[1], 0), (gq_arrived, 0)), g_up)[0]
+        g_gate, g_up = weight_grads((full0[3], full1[3]), ((full0[1], full1[1]), (full0[2], full1[2])), (grad_hidden,))
+        g_query_sum = own_sum[0] + tie(arrived, g_up)[0]
         return (hidden_out, grad_hidden, g_attn_norm, g_query_sum, g_key, g_value, g_out_sum, g_mlp_norm, g_gate, g_up, g_down)
 
     return jax.shard_map(local_layer, mesh=mesh, in_specs=in_specs, out_specs=out_specs, check_vma=False)

time: 1480 us -> 1690 us (1.14)
  waiting for transfers between devices: 45.4 us -> 294 us
  matrix products: 367 us -> 122 us
  Pallas kernels: 1000 us -> 1210 us
    dot_general x4 -> x0, matrix products: 246 us -> none  [dot_nt(): lax.dot_general(a, b, (((1,), (1,)), ((), ())), preferred_element_type=F32)]
    ppermute x9 -> x8, waiting for transfers between devices: 38.5 us -> 248 us  [to_chip(): return lax.ppermute(x, 'tp', chip_flip)]
    pallas_call x22 -> x21, Pallas kernels: 1000 us -> 1210 us  [run(): pl.pallas_call(kernel, grid_spec=spec, out_shape=out_shape, input_output_...]
    unnamed x11 -> x13, waiting for transfers between devices: 2.31 us -> 35.1 us
  transfers between devices with their start and end apart: 30 -> 29, of which waited for: 5 -> 7; matrix products, arithmetic and copies ran while one was open for 26% -> 5% of each run, Pallas kernels for 67% -> 65%
where the time goes in v2:
time: 1690 us; the launch traced here: 1680 us
  Pallas kernels  1210 us (72%)
  waiting for transfers between devices  294 us (17%)
  matrix products  122 us (7%)
    pallas_call x21, Pallas kernels, run(): pl.pallas_call(kernel, grid_spec=spec, out_shape=out_shape, input_output_...  1210 us
    ppermute x8, waiting for transfers between devices, to_chip(): return lax.ppermute(x, 'tp', chip_flip)  248 us
    dot_general x2, matrix products, dot_nn(): lax.dot_general(a, b, (((1,), (0,)), ((), ())), preferred_element_type=F32)  122 us
    unnamed x13, waiting for transfers between devices  35.1 us
  transfers between devices with their start and end apart: 29, of which 7 were waited for; matrix products, arithmetic and copies ran while one was open for 5% of the time, Pallas kernels for 65%

profile of v2, /device:TPU:0, one launch (start us, length us, event | category | flops | bytes accessed | tf_op | source)
XLA Modules:
  0.0 1679.9 jit_solution(3014870656782040929)
XLA Ops:
  7.2 0.9 collective-permute-start.5
  8.1 1.3 convert_add_fusion.1
  9.4 9.3 shard_map.230
  18.7 2.5 collective-permute-start.4
  21.7 33.6 %shard_map.231 = (bf16[2,768,4096]{2,1,0:T(8,128)(2,1)}, bf16[2,2,3,256,2048]{4,3,2,1,0:T(8,128)(2,1)}, bf16[2,2,3,256,2048]{4,3,2,1,0:T(8,128)(2,1)}, bf16[3,25...) custom-call(s32[1]{0:T(128)} %bitcast.me_ref.refs_0_, bf16[6,256,2048]{2,1,0:T(8,128)(2,1)} %go_ref.1, ...), custom_call_target="tpu_custom_call" | custom-call | flops 25769803776 | bytes 29360128 | tf_op jit(solution)/shard_map/pallas_call | solution.py:39
  55.3 46.0 %collective-permute-done.1.x_ref = bf16[2048,512]{1,0:T(8,128)(2,1)S(1)} collective-permute-done((bf16[2048,512]{1,0:T(8,128)(2,1)}, bf16[2048,512]{1,0:T(8,128)(2,1)S(1)}, u32[]{:S(2)}, u32[]{:S(2)}) %collective-permute-start.1) | collective-permute-done | bytes 2097184 | tf_op jit(solution)/shard_map/ppermute | solution.py:501
  101.4 1.3 copy-done.4
  102.7 32.6 %shard_map.232 = (bf16[2,768,4096]{2,1,0:T(8,128)(2,1)}, bf16[2,2,3,256,2048]{4,3,2,1,0:T(8,128)(2,1)}, bf16[2,2,3,256,2048]{4,3,2,1,0:T(8,128)(2,1)}) custom-call(s32[1]{0:T(128)} %bitcast.me_ref.refs_0_, bf16[6,256,2048]{2,1,0:T(8,128)(2,1)} %collective-permute-done.5.g_ref, ...), custom_call_target="tpu_custom_call", output_to_operand_aliasing={{1}: (4, {}), {2}: (5, {})} | custom-call | flops 25769803776 | bytes 29360128 | tf_op jit(solution)/shard_map/pallas_call | solution.py:39
  135.8 1.7 collective-permute-start.8
  137.6 1.6 collective-permute-done.6.k3_ref
  139.2 45.2 %shard_map.233 = (bf16[6,256,2048]{2,1,0:T(8,128)(2,1)}, bf16[6,1024,2048]{2,1,0:T(8,128)(2,1)}, bf16[6,256,2048]{2,1,0:T(8,128)(2,1)}) custom-call(s32[1]{0:T(128)} %bitcast.me_ref.refs_0_, s32[6]{0:T(128)} %pre_ref.1, s32[6]{0:T(128)} %val_ref.1, bf16[6,256,2048]{2,1,0:T(8,128)(2,1)} %get-tuple-element.59.u_ref, bf16[2048,512]{1,0:T(8,128)(2,1)} %w0_ref.9, ...), custom_call_target="tpu_custom_call" | custom-call | flops 25769803776 | bytes 25165824 | tf_op jit(solution)/shard_map/pallas_call | solution.py:39
  184.5 1.3 copy-done
  186.8 3.4 collective-permute-done.9.w3_ref
  190.2 1.3 copy-done.3
  191.5 14.3 shard_map.234
  206.2 1.7 collective-permute-start.14
  208.2 14.3 shard_map.235
  222.5 67.1 %shard_map.236 = (bf16[2,2,768,4096]{3,2,1,0:T(8,128)(2,1)}, bf16[2,2,768,4096]{3,2,1,0:T(8,128)(2,1)}, bf16[2,2,768,4096]{3,2,1,0:T(8,128)(2,1)}, bf16[2,2,3,256,2048]{4,3,2,1,0:T(8,128)(2,1)}) custom-call(s32[1]{0:T(128)} %bitcast.me_ref.refs_0_, bf16[3,256,2048]{2,1,0:T(8,128)(2,1)} %get-tuple-element.66.za_ref, ...), custom_call_target="tpu_custom_call" | custom-call | flops 51539607552 | bytes 83886080 | tf_op jit(solution)/shard_map/pallas_call | solution.py:39
  290.1 67.1 %shard_map.237 = (bf16[2,2,768,4096]{3,2,1,0:T(8,128)(2,1)}, bf16[2,2,768,4096]{3,2,1,0:T(8,128)(2,1)}, bf16[2,2,768,4096]{3,2,1,0:T(8,128)(2,1)}, bf16[2,2,3,256,2048]{4,3,2,1,0:T(8,128)(2,1)}) custom-call(s32[1]{0:T(128)} %bitcast.me_ref.refs_0_, bf16[3,256,2048]{2,1,0:T(8,128)(2,1)} %get-tuple-element.68.rest_0_.za_ref, ...), custom_call_target="tpu_custom_call" | custom-call | flops 51539607552 | bytes 83886080 | tf_op jit(solution)/shard_map/pallas_call | solution.py:39
  357.2 1.7 copy-done.2
  359.0 32.5 %shard_map.238 = (bf16[1,768,4096]{2,1,0:T(8,128)(2,1)}, bf16[1,768,4096]{2,1,0:T(8,128)(2,1)}, bf16[2,2,3,256,2048]{4,3,2,1,0:T(8,128)(2,1)}) custom-call(s32[1]{0:T(128)} %bitcast.me_ref.refs_0_, bf16[3,256,2048]{2,1,0:T(8,128)(2,1)} %tie.15.ga_ref, bf16[3,256,2048]{2,1,0:T(8,128)(2,1)} %collective-permute-done.15.gb_ref, ...), custom_call_target="tpu_custom_call", output_to_operand_aliasing={{2}: (4, {})} | custom-call | flops 25769803776 | bytes 29360128 | tf_op jit(solution)/shard_map/pallas_call | solution.py:39
  391.5 1.7 copy-done.6
  393.2 67.2 %shard_map.239 = (bf16[2,2,768,4096]{3,2,1,0:T(8,128)(2,1)}, bf16[2,2,768,4096]{3,2,1,0:T(8,128)(2,1)}, bf16[2,2,768,4096]{3,2,1,0:T(8,128)(2,1)}, bf16[2,2,3,256,2048]{4,3,2,1,0:T(8,128)(2,1)}) custom-call(s32[1]{0:T(128)} %bitcast.me_ref.refs_0_, ...), custom_call_target="tpu_custom_call", output_to_operand_aliasing={{0}: (7, {}), {1}: (8, {}), {2}: (9, {}), {3}: (10, {})} | custom-call | flops 51539607552 | bytes 83886080 | tf_op jit(solution)/shard_map/pallas_call | solution.py:39
  460.4 60.5 %convolution_convert_fusion.1.rest_6_ = bf16[3072,2048]{1,0:T(8,128)(2,1)} fusion(bf16[3072,4096]{1,0:T(8,128)(2,1)} %bitcast.38, bf16[4096,2048]{1,0:T(8,128)(2,1)} %wd_ref.7), kind=kOutput, calls=%fused_computation.1 | convolution fusion | flops 51545899008 | bytes 54525952 | tf_op jit(solution)/shard_map/dot_general | solution.py:21
  521.0 117.2 %shard_map.240.rest_5_ = bf16[4,768,2048]{2,1,0:T(8,128)(2,1)} custom-call(bf16[2,2,768,4096]{3,2,1,0:T(8,128)(2,1)} %get-tuple-element.78.dg_ref, bf16[2,2,768,4096]{3,2,1,0:T(8,128)(2,1)} %get-tuple-element.79.du_ref, bf16[2048,4096]{1,0:T(8,128)(2,1)} %wg_ref.11, bf16[2048,4096]{1,0:T(8,128)(2,1)} %wu_ref.11, ...), custom_call_target="tpu_custom_call" | custom-call | flops 103079215104 | bytes 50331648 | tf_op jit(solution)/shard_map/pallas_call | solution.py:39
  638.3 1.5 collective-permute-start.18
  640.1 1.5 collective-permute-start.16
  641.6 112.8 %collective-permute-done.18.x_ref = bf16[3,256,2048]{2,1,0:T(8,128)(2,1)} collective-permute-done((bf16[3,256,2048]{2,1,0:T(8,128)(2,1)}, bf16[3,256,2048]{2,1,0:T(8,128)(2,1)}, u32[]{:S(2)}, u32[]{:S(2)}) %collective-permute-start.18) | collective-permute-done | bytes 3145760 | tf_op jit(solution)/shard_map/ppermute | solution.py:501
  754.5 89.6 %collective-permute-done.16.x_ref = bf16[3,256,2048]{2,1,0:T(8,128)(2,1)} collective-permute-done((bf16[3,256,2048]{2,1,0:T(8,128)(2,1)S(1)}, bf16[3,256,2048]{2,1,0:T(8,128)(2,1)}, u32[]{:S(2)}, u32[]{:S(2)}) %collective-permute-start.16) | collective-permute-done | bytes 3145760 | tf_op jit(solution)/shard_map/ppermute | solution.py:501
  844.1 5.9 collective-permute-done.17.zb_ref
  849.9 1.7 copy-done.7
  851.6 95.4 %shard_map.241 = (bf16[2,2,768,4096]{3,2,1,0:T(8,128)(2,1)}, bf16[2,2,768,4096]{3,2,1,0:T(8,128)(2,1)}, bf16[2,2,768,4096]{3,2,1,0:T(8,128)(2,1)}, bf16[2,2,3,25...) custom-call(s32[1]{0:T(128)} %bitcast.me_ref.refs_0_, ...), custom_call_target="tpu_custom_call", output_to_operand_aliasing={{0}: (8, {}), {1}: (9, {}), {2}: (10, {}), {3}: (11, {}), {... | custom-call | flops 77309411328 | bytes 88080384 | tf_op jit(solution)/shard_map/pallas_call | solution.py:39
  947.0 115.2 %shard_map.242 = bf16[4,768,2048]{2,1,0:T(8,128)(2,1)} custom-call(bf16[2,2,768,4096]{3,2,1,0:T(8,128)(2,1)} %get-tuple-element.86.dg_ref, bf16[2,2,768,4096]{3,2,1,0:T(8,128)(2,1)} %get-tuple-element.87.du_ref, bf16[2048,4096]{1,0:T(8,128)(2,1)} %wg_ref.11, bf16[2048,4096]{1,0:T(8,128)(2,1)} %wu_ref.11, bf16[2,2,768,4096]{3,2,1,0:T(8,128)(2,1)} %get-tuple-element.88.rest_0_), custom_call_target="tpu_custom_call" | custom-call | flops 103079215104 | bytes 50331648 | tf_op jit(solution)/shard_map/pallas_call | solution.py:39
  1062.3 61.1 %convolution_convert_fusion.refs_4_.token0_ref = bf16[3072,2048]{1,0:T(8,128)(2,1)} fusion(bf16[3072,4096]{1,0:T(8,128)(2,1)} %bitcast.41, bf16[4096,2048]{1,0:T(8,128)(2,1)} %wd_ref.7), kind=kOutput, calls=%fused_computation | convolution fusion | flops 51545899008 | bytes 54525952 | tf_op jit(solution)/shard_map/dot_general | solution.py:21
  1123.5 35.0 %shard_map.243.token1_ref.refs_4_ = f32[4096,2048]{1,0:T(8,128)} custom-call(bf16[3072,4096]{1,0:T(8,128)(2,1)} %bitcast.39, bf16[3072,4096]{1,0:T(8,128)(2,1)} %bitcast.42, bf16[3072,2048]{1,0:T(8,128)(2,1)} %bitcast.50, bf16[3072,2048]{1,0:T(8,128)(2,1)} %bitcast.52, bf16[3072,2048]{1,0:T(8,128)(2,1)} %convolution_convert_fusion.refs_4_.token0_ref), custom_call_target="tpu_custom_call" | custom-call | flops 25769803776 | bytes 33554432 | tf_op jit(solution)/shard_map/pallas_call | solution.py:39
  1158.6 65.3 %shard_map.244 = (bf16[6,256,2048]{2,1,0:T(8,128)(2,1)}, bf16[6,256,2048]{2,1,0:T(8,128)(2,1)}, bf16[4,6,256,512]{3,2,1,0:T(8,128)(2,1)}, f32[1,2048]{1,0:T(1,128)}) custom-call(s32[1]{0:T(128)} %bitcast.me_ref.refs_0_, bf16[3,256,2048]{2,1,0:T(8,128)(2,1)} %bitcast.65, bf16[3,256,2048]{2,1,0:T(8,128)(2,1)} %bitcast.67, ...), custom_call_target="tpu_custom_call" | custom-call | flops 38654705664 | bytes 25165824 | tf_op jit(solution)/shard_map/pallas_call | solution.py:39
  1223.9 19.3 %shard_map.245.refs_2_ = f32[4,512,2048]{2,1,0:T(8,128)} custom-call(s32[1]{0:T(128)} %bitcast.me_ref.refs_0_, bf16[1536,2048]{1,0:T(8,128)(2,1)} %bitcast.44, bf16[1536,2048]{1,0:T(8,128)(2,1)} %bitcast.75, bf16[4,6,256,512]{3,2,1,0:T(8,128)(2,1)} %get-tuple-element.94.refs_3_), custom_call_target="tpu_custom_call" | custom-call | flops 12884901888 | bytes 16777216 | tf_op jit(solution)/shard_map/pallas_call | solution.py:39
  1243.2 12.3 shard_map.246.refs_5_
  1255.6 89.6 %shard_map.247.token_ref = f32[4096,2048]{1,0:T(8,128)} custom-call(bf16[3072,4096]{1,0:T(8,128)(2,1)} %bitcast.40, bf16[3072,4096]{1,0:T(8,128)(2,1)} %bitcast.43, bf16[3072,2048]{1,0:T(8,128)(2,1)} %bitcast.51, bf16[3072,2048]{1,0:T(8,128)(2,1)} %bitcast.53, f32[4096,2048]{1,0:T(8,128)} %shard_map.243.token1_ref.refs_4_, ...), custom_call_target="tpu_custom_call", output_to_operand_aliasing={{}: (4, {})} | custom-call | flops 77309411328 | bytes 33554432 | tf_op jit(solution)/shard_map/pallas_call | solution.py:39
  1345.2 15.6 shard_map.248
  1360.9 39.8 %shard_map.249 = (bf16[6,256,2048]{2,1,0:T(8,128)(2,1)}, f32[2056,512]{1,0:T(8,128)}, bf16[6,256,2048]{2,1,0:T(8,128)(2,1)}) custom-call(s32[1]{0:T(128)} %bitcast.me_ref.refs_0_, bf16[6,256,512]{2,1,0:T(8,128)(2,1)} %bitcast.68, bf16[6,256,2048]{2,1,0:T(8,128)(2,1)} %get-tuple-element.95.dq_ref, bf16[6,256,2048]{2,1,0:T(8,128)(2,1)} %get-tuple-element.59.u_ref, ...), custom_call_target="tpu_custom_call" | custom-call | flops 19327352832 | bytes 25165824 | tf_op jit(solution)/shard_map/pallas_call | solution.py:39
  1400.8 0.7 reduce-scatter.29.cloned.1.call-update
  1401.5 0.6 collective-permute-start.21
  1402.1 223.2 %shard_map.250 = (f32[2048,4096]{1,0:T(8,128)}, f32[2048,4096]{1,0:T(8,128)}) custom-call(bf16[3072,2048]{1,0:T(8,128)(2,1)} %bitcast.74, bf16[3072,2048]{1,0:T(8,128)(2,1)} %bitcast.73, bf16[3072,4096]{1,0:T(8,128)(2,1)} %bitcast.71, bf16[3072,4096]{1,0:T(8,128)(2,1)} %bitcast.69, bf16[3072,4096]{1,0:T(8,128)(2,1)} %bitcast.72, ...), custom_call_target="tpu_custom_call" | custom-call | flops 206158430208 | bytes 33554432 | tf_op jit(solution)/shard_map/pallas_call | solution.py:39
  1625.3 6.7 add_bitcast_fusion
  1632.0 0.8 slice_bitcast_fusion
  1634.0 4.5 fusion
  1638.5 34.2 %reduce-scatter.29.cloned.1.call-done = f32[1,512,2048]{2,1,0:T(8,128)} async-done(((f32[4,512,2048]{2,1,0:T(8,128)}), f32[1,512,2048]{2,1,0:T(8,128)}) %reduce-scatter.29.cloned.1.call-update) | async-done | bytes 4194320
  (73 shorter events, 5.3 us)
Async XLA Ops:
  7.2 1151.3 %reduce-scatter.23.cloned.1.call-start = ((), (), s32[]{:S(2)}) async-start(), calls=%async_computation.9 | async-start | bytes 15728640
  7.2 95.5 %collective-permute-start.5 = (bf16[6,256,2048]{2,1,0:T(8,128)(2,1)}, bf16[6,256,2048]{2,1,0:T(8,128)(2,1)}, u32[]{:S(2)}, u32[]{:S(2)}) collective-permute-start(bf16[6,256,2048]{2,1,0:T(8,128)(2,1)} %go_ref.1), channel_id=1, source_target_pairs={{0,1},{1,0},{2,3},{3,2},{4,5},{5,4},{6,7},{7,6}} | collective-permute-start | bytes 18874376 | tf_op jit(solution)/shard_map/ppermute | solution.py:498
  18.7 116.6 %collective-permute-start.4 = (bf16[6,256,512]{2,1,0:T(8,128)(2,1)}, bf16[6,256,512]{2,1,0:T(8,128)(2,1)}, u32[]{:S(2)}, u32[]{:S(2)}) collective-permute-start(bf16[6,256,512]{2,1,0:T(8,128)(2,1)} %get-tuple-element.60.rest_0_.k0_ref), channel_id=1, source_target_pairs={{0,2},{2,0},{1,3},{3,1},{4,6},{6,4},{5,7},{7,5}} | collective-permute-start | bytes 4718600 | tf_op jit(solution)/shard_map/ppermute | solution.py:501
  21.2 116.4 %collective-permute-start.3 = (bf16[6,256,512]{2,1,0:T(8,128)(2,1)}, bf16[6,256,512]{2,1,0:T(8,128)(2,1)}, u32[]{:S(2)}, u32[]{:S(2)}) collective-permute-start(bf16[6,256,512]{2,1,0:T(8,128)(2,1)} %get-tuple-element.60.rest_0_.k0_ref), channel_id=1, source_target_pairs={{0,1},{1,0},{2,3},{3,2},{4,5},{5,4},{6,7},{7,6}} | collective-permute-start | bytes 4718600 | tf_op jit(solution)/shard_map/ppermute | solution.py:498
  21.4 80.0 %collective-permute-start.1 = (bf16[2048,512]{1,0:T(8,128)(2,1)}, bf16[2048,512]{1,0:T(8,128)(2,1)S(1)}, u32[]{:S(2)}, u32[]{:S(2)}) collective-permute-start(bf16[2048,512]{1,0:T(8,128)(2,1)} %w0_ref.9), channel_id=1, source_target_pairs={{0,2},{2,0},{1,3},{3,1},{4,6},{6,4},{5,7},{7,5}} | collective-permute-start | bytes 6291464 | tf_op jit(solution)/shard_map/ppermute | solution.py:501
  21.7 115.9 %collective-permute-start = (bf16[2048,512]{1,0:T(8,128)(2,1)}, bf16[2048,512]{1,0:T(8,128)(2,1)}, u32[]{:S(2)}, u32[]{:S(2)}) collective-permute-start(bf16[2048,512]{1,0:T(8,128)(2,1)} %w0_ref.9), channel_id=1, source_target_pairs={{0,1},{1,0},{2,3},{3,2},{4,5},{5,4},{6,7},{7,6}} | collective-permute-start | bytes 6291464 | tf_op jit(solution)/shard_map/ppermute | solution.py:498
  101.4 1.3 copy-start.4
  102.7 34.9 %collective-permute-start.2 = (bf16[2048,512]{1,0:T(8,128)(2,1)}, bf16[2048,512]{1,0:T(8,128)(2,1)}, u32[]{:S(2)}, u32[]{:S(2)}) collective-permute-start(bf16[2048,512]{1,0:T(8,128)(2,1)} %tie.10.w2_ref), channel_id=1, source_target_pairs={{0,1},{1,0},{2,3},{3,2},{4,5},{5,4},{6,7},{7,6}} | collective-permute-start | bytes 6291464 | tf_op jit(solution)/shard_map/ppermute | solution.py:498
  135.3 3.9 collective-permute-start.6
  135.8 48.6 %collective-permute-start.8 = (bf16[512,2048]{1,0:T(8,128)(2,1)}, bf16[512,2048]{1,0:T(8,128)(2,1)S(1)}, u32[]{:S(2)}, u32[]{:S(2)}) collective-permute-start(bf16[512,2048]{1,0:T(8,128)(2,1)} %w0_ref.8), channel_id=1, source_target_pairs={{0,2},{2,0},{1,3},{3,1},{4,6},{6,4},{5,7},{7,5}} | collective-permute-start | bytes 6291464 | tf_op jit(solution)/shard_map/ppermute | solution.py:501
  137.6 49.2 %collective-permute-start.7 = (bf16[512,2048]{1,0:T(8,128)(2,1)}, bf16[512,2048]{1,0:T(8,128)(2,1)}, u32[]{:S(2)}, u32[]{:S(2)}) collective-permute-start(bf16[512,2048]{1,0:T(8,128)(2,1)} %w0_ref.8), channel_id=1, source_target_pairs={{0,1},{1,0},{2,3},{3,2},{4,5},{5,4},{6,7},{7,6}} | collective-permute-start | bytes 6291464 | tf_op jit(solution)/shard_map/ppermute | solution.py:498
  184.5 1.7 copy-start.5
  184.5 1.3 copy-start
  185.8 4.4 collective-permute-start.9
  190.2 1.3 copy-start.3
  205.8 16.7 collective-permute-start.12
  206.2 83.5 %collective-permute-start.14 = (bf16[3,256,2048]{2,1,0:T(8,128)(2,1)}, bf16[3,256,2048]{2,1,0:T(8,128)(2,1)}, u32[]{:S(2)}, u32[]{:S(2)}) collective-permute-start(bf16[3,256,2048]{2,1,0:T(8,128)(2,1)} %tie.14), channel_id=1, source_target_pairs={{0,2},{2,0},{1,3},{3,1},{4,6},{6,4},{5,7},{7,5}} | collective-permute-start | bytes 9437192 | tf_op jit(solution)/shard_map/ppermute | solution.py:501
  207.9 149.3 %collective-permute-start.10 = (bf16[3,256,2048]{2,1,0:T(8,128)(2,1)}, bf16[3,256,2048]{2,1,0:T(8,128)(2,1)S(1)}, u32[]{:S(2)}, u32[]{:S(2)}) collective-permute-start(bf16[3,256,2048]{2,1,0:T(8,128)(2,1)} %get-tuple-element.66.za_ref), channel_id=1, source_target_pairs={{0,2},{2,0},{1,3},{3,1},{4,6},{6,4},{5,7},{7,5}} | collective-permute-start | bytes 9437192 | tf_op jit(solution)/shard_map/ppermute | solution.py:501
  222.5 67.7 %collective-permute-start.11 = (bf16[3,256,2048]{2,1,0:T(8,128)(2,1)}, bf16[3,256,2048]{2,1,0:T(8,128)(2,1)}, u32[]{:S(2)}, u32[]{:S(2)}) collective-permute-start(bf16[3,256,2048]{2,1,0:T(8,128)(2,1)} %get-tuple-element.68.rest_0_.za_ref), channel_id=1, source_target_pairs={{0,1},{1,0},{2,3},{3,2},{4,5},{5,4},{6,7},{7,6}} | collective-permute-start | bytes 9437192 | tf_op jit(solution)/shard_map/ppermute | solution.py:498
  289.6 69.3 %collective-permute-start.15 = (bf16[3,256,2048]{2,1,0:T(8,128)(2,1)}, bf16[3,256,2048]{2,1,0:T(8,128)(2,1)}, u32[]{:S(2)}, u32[]{:S(2)}) collective-permute-start(bf16[3,256,2048]{2,1,0:T(8,128)(2,1)} %tie.15.ga_ref), channel_id=1, source_target_pairs={{0,1},{1,0},{2,3},{3,2},{4,5},{5,4},{6,7},{7,6}} | collective-permute-start | bytes 9437192 | tf_op jit(solution)/shard_map/ppermute | solution.py:498
  357.2 1.7 copy-start.2
  358.9 32.6 %collective-permute-start.13 = (bf16[3,256,2048]{2,1,0:T(8,128)(2,1)}, bf16[3,256,2048]{2,1,0:T(8,128)(2,1)S(1)}, u32[]{:S(2)}, u32[]{:S(2)}) collective-permute-start(bf16[3,256,2048]{2,1,0:T(8,128)(2,1)} %tie.13.za_ref), channel_id=1, source_target_pairs={{0,1},{1,0},{2,3},{3,2},{4,5},{5,4},{6,7},{7,6}} | collective-permute-start | bytes 9437192 | tf_op jit(solution)/shard_map/ppermute | solution.py:498
  391.5 1.7 copy-start.6
  521.0 637.5 %reduce-scatter.19.cloned.1.call-start = ((), (), s32[]{:S(2)}) async-start(), calls=%async_computation.7 | async-start | bytes 15728640
  638.2 1.9 copy-start.1
  638.3 520.3 %reduce-scatter.21.cloned.1.call-start = ((), (), s32[]{:S(2)}) async-start(), calls=%async_computation.8 | async-start | bytes 15728640
  638.3 116.2 %collective-permute-start.18 = (bf16[3,256,2048]{2,1,0:T(8,128)(2,1)}, bf16[3,256,2048]{2,1,0:T(8,128)(2,1)}, u32[]{:S(2)}, u32[]{:S(2)}) collective-permute-start(bf16[3,256,2048]{2,1,0:T(8,128)(2,1)} %tie.17), channel_id=1, source_target_pairs={{0,2},{2,0},{1,3},{3,1},{4,6},{6,4},{5,7},{7,5}} | collective-permute-start | bytes 9437192 | tf_op jit(solution)/shard_map/ppermute | solution.py:501
  640.1 203.9 %collective-permute-start.16 = (bf16[3,256,2048]{2,1,0:T(8,128)(2,1)S(1)}, bf16[3,256,2048]{2,1,0:T(8,128)(2,1)}, u32[]{:S(2)}, u32[]{:S(2)}) collective-permute-start(bf16[3,256,2048]{2,1,0:T(8,128)(2,1)S(1)} %copy-done.1), channel_id=1, source_target_pairs={{0,2},{2,0},{1,3},{3,1},{4,6},{6,4},{5,7},{7,5}} | collective-permute-start | bytes 9437192 | tf_op jit(solution)/shard_map/ppermute | solution.py:501
  754.5 89.6 %collective-permute-start.19 = (bf16[3,256,2048]{2,1,0:T(8,128)(2,1)}, bf16[3,256,2048]{2,1,0:T(8,128)(2,1)}, u32[]{:S(2)}, u32[]{:S(2)}) collective-permute-start(bf16[3,256,2048]{2,1,0:T(8,128)(2,1)} %tie.18.ga_ref), channel_id=1, source_target_pairs={{0,1},{1,0},{2,3},{3,2},{4,5},{5,4},{6,7},{7,6}} | collective-permute-start | bytes 9437192 | tf_op jit(solution)/shard_map/ppermute | solution.py:498
  844.0 5.9 collective-permute-start.17
  849.9 1.7 copy-start.7
  1062.2 298.6 %reduce-scatter.27.cloned.1.call-start = ((), (), s32[]{:S(2)}) async-start(), calls=%async_computation.11 | async-start | bytes 15728640
  1123.5 237.4 %reduce-scatter.25.cloned.1.call-start = ((), (), s32[]{:S(2)}) async-start(), calls=%async_computation.10 | async-start | bytes 7864320
  1223.8 408.2 %all-reduce.8.cloned.1.call-start = ((), (), s32[]{:S(2)}) async-start(), calls=%async_computation.6 | async-start | bytes 8421376 | tf_op jit(solution)/shard_map/psum | solution.py:738
  1255.5 89.7 %collective-permute-start.20 = (f32[2,2048,512]{2,1,0:T(8,128)}, f32[2,2048,512]{2,1,0:T(8,128)}, u32[]{:S(2)}, u32[]{:S(2)}) collective-permute-start(f32[2,2048,512]{2,1,0:T(8,128)} %shard_map.246.refs_5_), channel_id=1, source_target_pairs={{0,1},{1,0},{2,3},{3,2},{4,5},{5,4},{6,7},{7,6}} | collective-permute-start | bytes 25165832 | tf_op jit(solution)/shard_map/ppermute | solution.py:498
  1400.7 272.0 %reduce-scatter.29.cloned.1.call-start = ((), (), s32[]{:S(2)}) async-start(), calls=%async_computation.12 | async-start | bytes 20971520
  1401.5 223.8 %collective-permute-start.21 = (f32[1,2048,512]{2,1,0:T(8,128)}, f32[1,2048,512]{2,1,0:T(8,128)}, u32[]{:S(2)}, u32[]{:S(2)}) collective-permute-start(f32[1,2048,512]{2,1,0:T(8,128)} %get-tuple-element.98.token0_ref), channel_id=1, source_target_pairs={{0,2},{2,0},{1,3},{3,1},{4,6},{6,4},{5,7},{7,5}} | collective-permute-start | bytes 12582920 | tf_op jit(solution)/shard_map/ppermute | solution.py:501
Sparse Core Ops, SparseCore 0:
  521.1 95.3 reduce-scatter.22
  638.4 163.1 reduce-scatter.18
  1062.4 95.4 reduce-scatter.20
  1160.3 94.0 reduce-scatter.26
  1256.7 55.0 reduce-scatter.24
  1400.8 149.2 all-reduce.7
  1553.2 119.4 reduce-scatter.28

commit v3 on v2

--- a/solution.py
+++ b/solution.py
@@ -135,54 +135,93 @@
     z_ref[0] = (x * inv * gain_ref[...]).astype(BF)
 
 
-def place_copies(pieces, cats, sems):
-    return [pltpu.make_async_copy(src, dst, sems.at[i]) for i, (src, dst) in enumerate(zip(pieces, cats))]
-
-
-def start_at_first(copies):
-    @pl.when(pl.program_id(0) == 0)
-    def _():
-        for c in copies:
+class Flow:
+    def __init__(self, bufs, sems, inward, sides):
+        self.bufs, self.sems, self.inward, self.sides = bufs, sems, inward, sides
+
+    def copies(self, t, slot, only):
+        out = []
+        for i, (hbm, buf) in enumerate(zip(self.sides(t), self.bufs)):
+            if only is None or i == only:
+                pair = (hbm, buf.at[slot]) if self.inward else (buf.at[slot], hbm)
+                out.append(pltpu.make_async_copy(*pair, self.sems.at[slot, i]))
+        return out
+
+    def start(self, t, slot, only=None):
+        for c in self.copies(t, slot, only):
             c.start()
 
-
-def wait_at_last(copies):
-    @pl.when(pl.program_id(0) == pl.num_programs(0) - 1)
-    def _():
-        for c in copies:
+    def wait(self, t, slot, only=None):
+        for c in self.copies(t, slot, only):
             c.wait()
 
 
-def dact_near_kernel(rel, me_ref, g_ref, wd_ref, *rest):
-    outs, sems = rest[-4 if rel else -6 : -1], rest[-1]
-    da_ref, cats, owns = outs[0], outs[1:3], outs[3:]
-    half = g_ref.shape[0] // 2
-    rows, dim = half * g_ref.shape[1], g_ref.shape[2]
-    chip = me_ref[0] // 2
-    core = abs(rel - me_ref[0] % 2)
-    src, dst = [], []
-    for c in range(2):
-        piece = g_ref.at[pl.ds(c * half, half)]
-        src.append(piece)
-        dst.append(cats[c].at[chip, core])
-        if owns:
-            src.append(piece)
-            dst.append(owns[c])
-    copies = place_copies(src, dst, sems)
-    start_at_first(copies)
-    da_ref[...] = dot_nt(g_ref[...].reshape(2 * rows, dim), wd_ref[...]).astype(BF).reshape(da_ref.shape)
-    wait_at_last(copies)
-
-
-def dact_far_kernel(me_ref, ga_ref, gb_ref, wd_ref, *rest):
-    da_ref, db_ref, cat_ref, sems = rest[-4:]
-    rows, dim = ga_ref.shape[0] * ga_ref.shape[1], ga_ref.shape[2]
-    chip, core = 1 - me_ref[0] // 2, me_ref[0] % 2
-    copies = place_copies([ga_ref, gb_ref], [cat_ref.at[chip, core], cat_ref.at[chip, 1 - core]], sems)
-    start_at_first(copies)
-    for ref, o_ref in ((ga_ref, da_ref), (gb_ref, db_ref)):
-        o_ref[0] = dot_nt(ref[...].reshape(rows, dim), wd_ref[...]).astype(BF)
-    wait_at_last(copies)
+def local_copies(pairs, sems):
+    return [pltpu.make_async_copy(src, dst, sems.at[i]) for i, (src, dst) in enumerate(pairs)]
+
+
+def start_all(copies):
+    for c in copies:
+        c.start()
+
+
+def wait_all(copies):
+    for c in copies:
+        c.wait()
+
+
+def span(t, n):
+    return pl.ds(pl.multiple_of(t * n, n), n)
+
+
+OWN, MATE, FAR = 0, 1, 2
+
+
+def dact_kernel(kind, me_ref, *refs):
+    n_in, n_out = (2, 2) if kind == FAR else (1, 5 if kind == OWN else 3)
+    gs, wd_ref = refs[:n_in], refs[n_in]
+    outs, (wb, ob, gv, w_sem, o_sem, g_sem, c_sem) = refs[-7 - n_out : -7], refs[-7:]
+    da_ref, homes = outs[0], outs[1:]
+    half = gv.shape[0] // 2
+    chip, core = me_ref[0] // 2, me_ref[0] % 2
+    halves = [gv.at[pl.ds(c * half, half)] for c in range(2)]
+    if kind == FAR:
+        loads = local_copies(zip(gs, halves), g_sem)
+        puts = [(halves[0], homes[0].at[1 - chip, core]), (halves[1], homes[0].at[1 - chip, 1 - core])]
+    else:
+        loads = local_copies([(gs[0], gv)], g_sem)
+        puts = [(halves[c], homes[c].at[chip, core if kind == OWN else 1 - core]) for c in range(2)]
+        puts += list(zip(halves, homes[2:]))
+    puts = local_copies(puts, c_sem)
+    bn = ob.shape[-1]
+    steps = wd_ref.shape[0] // bn
+    w_flow = Flow((wb,), w_sem, True, lambda t: (wd_ref.at[span(t, bn)],))
+    o_flow = Flow((ob,), o_sem, False, lambda t: (da_ref.at[:, :, span(t, bn)],))
+    start_all(loads)
+    w_flow.start(0, 0)
+    wait_all(loads)
+    start_all(puts)
+
+    @pl.loop(0, steps)
+    def _(t):
+        slot = lax.rem(t, 2)
+
+        @pl.when(t + 1 < steps)
+        def _():
+            w_flow.start(t + 1, 1 - slot)
+
+        @pl.when(t >= 2)
+        def _():
+            o_flow.wait(t - 2, slot)
+
+        w_flow.wait(t, slot)
+        g = gv[...].reshape(2 * half * gv.shape[1], gv.shape[2])
+        ob[slot] = dot_nt(g, wb[slot]).astype(BF).reshape(ob.shape[1:])
+        o_flow.start(t, slot)
+
+    for t in (steps - 2, steps - 1):
+        o_flow.wait(t, t % 2)
+    wait_all(puts)
 
 
 def gated(gate, up, da):
@@ -195,48 +234,72 @@
     return (gelu * up).astype(BF), (da * up * slope).astype(BF), (da * gelu).astype(BF)
 
 
-def mlp_kernel(other, me_ref, za_ref, zb_ref, da_ref, db_ref, wg_ref, wu_ref, *rest):
-    act_ref, dg_ref, du_ref, cat_ref, sems = rest[-5:]
-    rows, dim = za_ref.shape[0] * za_ref.shape[1], za_ref.shape[2]
+def mlp_kernel(other, at, fused, me_ref, *refs):
+    za, zb, da, db, wg_ref, wu_ref = refs[:6]
+    n_out, n_scr = (5, 13) if fused else (4, 11)
+    outs, scr = refs[-n_scr - n_out : -n_scr], refs[-n_scr:]
+    zv, wgb, wub, act_b, dg_b, du_b, in_sem, o_sem, z_sem, c_sem = scr[:10]
+    chip = abs(other - me_ref[0] // 2)
     core = me_ref[0] % 2
-    chip = abs(other - me_ref[0] // 2)
-    copies = place_copies([za_ref, zb_ref], [cat_ref.at[chip, core], cat_ref.at[chip, 1 - core]], sems)
-    start_at_first(copies)
-    step = rows // 2
-    for rel, (ref, d_ref) in enumerate(((za_ref, da_ref), (zb_ref, db_ref))):
-        place = core if rel == 0 else 1 - core
-        z = ref[...].reshape(rows, dim)
-        for r in range(0, rows, step):
-            zr = z[r : r + step]
-            out = gated(dot_nn(zr, wg_ref[...]), dot_nn(zr, wu_ref[...]), d_ref[0, r : r + step, :].astype(F32))
-            for o_ref, o in zip((act_ref, dg_ref, du_ref), out):
-                o_ref[0, place, r : r + step, :] = o
-    wait_at_last(copies)
-
-
-def mlp_fused_kernel(other, me_ref, za_ref, zb_ref, ga_ref, gb_ref, wg_ref, wu_ref, wd_ref, *rest):
-    act_ref, dg_ref, du_ref, zcat_ref, gcat_ref, sems = rest[-6:]
-    rows, dim = za_ref.shape[0] * za_ref.shape[1], za_ref.shape[2]
-    core = me_ref[0] % 2
-    chip = abs(other - me_ref[0] // 2)
-    here, there = (chip, core), (chip, 1 - core)
-    copies = place_copies([za_ref, zb_ref, ga_ref, gb_ref], [zcat_ref.at[here], zcat_ref.at[there], gcat_ref.at[here], gcat_ref.at[there]], sems)
-    start_at_first(copies)
-    step = rows // 3
-    for rel, (z_ref, g_ref) in enumerate(((za_ref, ga_ref), (zb_ref, gb_ref))):
-        place = core if rel == 0 else 1 - core
-        z, g = z_ref[...].reshape(rows, dim), g_ref[...].reshape(rows, dim)
-        for r in range(0, rows, step):
-            zr = z[r : r + step]
-            out = gated(dot_nn(zr, wg_ref[...]), dot_nn(zr, wu_ref[...]), dot_nt(g[r : r + step], wd_ref[...]))
-            for o_ref, o in zip((act_ref, dg_ref, du_ref), out):
-                o_ref[0, place, r : r + step, :] = o
-    wait_at_last(copies)
+    rows, bn = act_b.shape[2:]
+    dim = zv.shape[-1]
+    steps = wg_ref.shape[1] // bn
+    if fused:
+        wdb, gv, g_sem = scr[10:]
+        wd_ref = refs[6]
+        in_flow = Flow((wgb, wub, wdb), in_sem, True, lambda t: (wg_ref.at[:, span(t, bn)], wu_ref.at[:, span(t, bn)], wd_ref.at[span(t, bn)]))
+    else:
+        dv = scr[10]
+        in_flow = Flow((wgb, wub, dv.at[:, 0], dv.at[:, 1]), in_sem, True,
+                       lambda t: (wg_ref.at[:, span(t, bn)], wu_ref.at[:, span(t, bn)], da.at[at[0], :, span(t, bn)], db.at[at[1], :, span(t, bn)]))
+    bufs = (act_b, dg_b, du_b)
+    o_flow = Flow([b.at[:, rel] for rel in range(2) for b in bufs], o_sem, False,
+                  lambda t: [o.at[chip, abs(rel - core), :, span(t, bn)] for rel in range(2) for o in outs[:3]])
+    loads = local_copies([(za, zv.at[0]), (zb, zv.at[1])], z_sem)
+    puts = [(zv.at[0], outs[3].at[chip, core]), (zv.at[1], outs[3].at[chip, 1 - core])]
+    if fused:
+        loads += local_copies([(da, gv.at[0]), (db, gv.at[1])], g_sem)
+        puts += [(gv.at[0], outs[4].at[chip, core]), (gv.at[1], outs[4].at[chip, 1 - core])]
+    puts = local_copies(puts, c_sem)
+    in_flow.start(0, 0)
+    start_all(loads)
+    wait_all(loads)
+    start_all(puts)
+    n = rows // (3 if fused else 2)
+
+    @pl.loop(0, steps)
+    def _(t):
+        slot = lax.rem(t, 2)
+
+        @pl.when(t + 1 < steps)
+        def _():
+            in_flow.start(t + 1, 1 - slot)
+
+        @pl.when(t >= 2)
+        def _():
+            o_flow.wait(t - 2, slot)
+
+        in_flow.wait(t, slot)
+        for rel in range(2):
+            z = zv[rel].reshape(rows, dim)
+            for r in range(0, rows, n):
+                gate, up = dot_nn(z[r : r + n], wgb[slot]), dot_nn(z[r : r + n], wub[slot])
+                if fused:
+                    d = dot_nt(gv[rel].reshape(rows, dim)[r : r + n], wdb[slot])
+                else:
+                    d = dv[slot, rel, r : r + n, :].astype(F32)
+                for buf, o in zip(bufs, gated(gate, up, d)):
+                    buf[slot, rel, r : r + n, :] = o
+        o_flow.start(t, slot)
+
+    for t in (steps - 2, steps - 1):
+        o_flow.wait(t, t % 2)
+    wait_all(puts)
 
 
 def attn_bwd_kernel(me_ref, dz0_ref, dz1_ref, res_ref, go_ref, gain_ref, w0_ref, w1_ref, w2_ref, w3_ref, k0_ref, k1_ref, k2_ref, k3_ref,
                     q_ref, pt_ref, cos_ref, sin_ref, token0_ref, token1_ref, token2_ref,
-                    dres_ref, dq_ref, dkv_ref, gn_ref, kt_ref, v_ref, do_ref, qs_ref, ds_ref, dp_ref):
+                    dres_ref, dq_ref, dkv_ref, gn_ref, kt_ref, v_ref, do_ref, qs_ref, ds_ref, dp_ref, dk_ref, dv_ref):
     b = pl.program_id(0)
     half = pl.num_programs(0) // 2
     seq, hd = v_ref.shape
@@ -265,20 +328,38 @@
     for r, kv_ref in enumerate((k0_ref, k1_ref, k2_ref, k3_ref)):
         kt_ref[:, r * sl : (r + 1) * sl] = (kv_ref[0, :, :hd].astype(F32) * scale).T.astype(BF)
         v_ref[r * sl : (r + 1) * sl, :] = kv_ref[0, :, hd:]
-    for r, w_ref in enumerate((w0_ref, w1_ref, w2_ref, w3_ref)):
-        dm = dot_nt(dres, w_ref[...]).astype(BF)
-        per = w_ref.shape[0] // hd
+    w_refs = (w0_ref, w1_ref, w2_ref, w3_ref)
+    per = w0_ref.shape[0] // hd
+
+    def d_mixed(r):
+        dm = dot_nt(dres, w_refs[r][...]).astype(BF)
         for j in range(per):
             h = r * per + j
             do_ref[h * sl : (h + 1) * sl, :] = dm[:, j * hd : (j + 1) * hd]
             qs_ref[h * sl : (h + 1) * sl, :] = (q_ref[0, :, h * hd : (h + 1) * hd].astype(F32) * scale).astype(BF)
+
     cos_t, sin_t = cos_ref[...], sin_ref[...]
 
     def dprobs(h):
         return dot_nt(v_ref[...], do_ref[h * sl : (h + 1) * sl, :])
 
+    def add_kv(r, first):
+        at = pl.ds(r * per * sl, per * sl)
+        dk, dv = dot_nn(ds_ref[:, at], qs_ref[at, :]), dot_nn(pt_ref[0, :, at], do_ref[at, :])
+        if first:
+            dk_ref[...], dv_ref[...] = dk, dv
+        else:
+            dk_ref[...] += dk
+            dv_ref[...] += dv
+
+    d_mixed(0)
     dp_ref[0] = dprobs(0)
     for h in range(heads):
+        if h % per == 0:
+            if h // per + 1 < len(w_refs):
+                d_mixed(h // per + 1)
+            if h:
+                add_kv(h // per - 1, h == per)
         if h + 1 < heads:
             dp_ref[(h + 1) % 2] = dprobs(h + 1)
         p = pt_ref[0, :, h * sl : (h + 1) * sl].astype(F32)
@@ -289,8 +370,9 @@
         first, second = rope_bwd(dq[:, : hd // 2], dq[:, hd // 2 :], cos_t, sin_t)
         dq_ref[0, :, h * hd : h * hd + hd // 2] = first.astype(BF)
         dq_ref[0, :, h * hd + hd // 2 : (h + 1) * hd] = second.astype(BF)
-    dk = dot_nn(ds_ref[...], qs_ref[...]).astype(BF)
-    dv = dot_nn(pt_ref[0], do_ref[...]).astype(BF)
+    at = pl.ds((heads - per) * sl, per * sl)
+    dk = (dk_ref[...] + dot_nn(ds_ref[:, at], qs_ref[at, :])).astype(BF)
+    dv = (dv_ref[...] + dot_nn(pt_ref[0, :, at], do_ref[at, :])).astype(BF)
     for r in range(seq // sl):
         dkv_ref[me ^ r, 0, :, :hd] = dk[r * sl : (r + 1) * sl]
         dkv_ref[me ^ r, 0, :, hd:] = dv[r * sl : (r + 1) * sl]
@@ -357,26 +439,6 @@
         own_ref[0] = out
 
 
-class Flow:
-    def __init__(self, bufs, sems, inward, sides):
-        self.bufs, self.sems, self.inward, self.sides = bufs, sems, inward, sides
-
-    def copies(self, t, slot):
-        out = []
-        for i, (hbm, buf) in enumerate(zip(self.sides(t), self.bufs)):
-            pair = (hbm, buf.at[slot]) if self.inward else (buf.at[slot], hbm)
-            out.append(pltpu.make_async_copy(*pair, self.sems.at[slot, i]))
-        return out
-
-    def start(self, t, slot):
-        for c in self.copies(t, slot):
-            c.start()
-
-    def wait(self, t, slot):
-        for c in self.copies(t, slot):
-            c.wait()
-
-
 def gated_grad_kernel(dg_ref, du_ref, wg_ref, wu_ref, *rest):
     o_ref, a1, a2, b1, b2, ob, a_sem, b_sem, o_sem = rest[-9:]
     ni = dg_ref.shape[0] * dg_ref.shape[1]
@@ -387,10 +449,20 @@
     a_flow = Flow((a1, a2), a_sem, True, lambda i: (dg_ref.at[i // 2, i % 2], du_ref.at[i // 2, i % 2]))
     b_flow = Flow((b1, b2), b_sem, True, lambda t: (wg_ref.at[cols(t)], wu_ref.at[cols(t)]))
     o_flow = Flow((ob,), o_sem, False, lambda t: (o_ref.at[t // nj, :, cols(t)],))
-    a_flow.start(0, 0)
-    b_flow.start(0, 0)
-
-    @pl.loop(0, steps)
+    for k in range(2):
+        a_flow.start(0, 0, k)
+        b_flow.start(0, 0, k)
+    b_flow.start(1, 1)
+    a_flow.start(1, 1)
+    for k in range(2):
+        a_flow.wait(0, 0, k)
+        b_flow.wait(0, 0, k)
+        if k == 0:
+            first = dot_nt(a1[0], b1[0])
+    ob[0] = (first + dot_nt(a2[0], b2[0])).astype(BF)
+    o_flow.start(0, 0)
+
+    @pl.loop(1, steps)
     def _(t):
         i, slot = t // nj, lax.rem(t, 2)
         a_slot = lax.rem(i, 2)
@@ -440,10 +512,21 @@
             for k in range(count):
                 pl.when(which == k)(functools.partial(act, flows[k]))
 
-    x_flow.start(0, 0)
-    y_flows[0].start(0, 0)
-
-    @pl.loop(0, steps)
+    for k in range(2):
+        x_flow.start(0, 0, k)
+        y_flows[0].start(0, 0, k)
+    y_flows[0].start(1, 1)
+    if ni > 1:
+        x_flow.start(1, 1)
+    for k in range(2):
+        x_flow.wait(0, 0, k)
+        y_flows[0].wait(0, 0, k)
+        if k == 0:
+            part = dot_tn(x0[0], y0[0])
+    ob[0] = part + dot_tn(x1[0], y1[0])
+    o_flows[0].start(0, 0)
+
+    @pl.loop(1, steps)
     def _(t):
         i, slot = t // per, lax.rem(t, 2)
         x_slot = lax.rem(i, 2)
@@ -550,24 +633,23 @@
         wo_mate = to_core(w_out)
 
         bn = 512
-        whole_spec = block((batch, sl, dim), lambda n, *_: (0, 0, 0), True)
-        half_spec = block((half, sl, dim), lambda n, *_: (0, 0, 0), True)
         cat_shape = (2, 2, half, sl, dim)
-        da_shape = (2, rows, ffn)
-
-        def dact_near(rel, g, token, cats):
+        SMEM = pl.BlockSpec(memory_space=pltpu.SMEM)
+        pair = (2, rows, bn)
+
+        def dact(kind, gs, homes, tokens, n_out):
             return run(
-                functools.partial(dact_near_kernel, rel), (ffn // bn,),
-                [whole_spec, block((bn, dim), lambda n, *_: (n, 0))] + [ANY] * (1 + len(cats)),
-                [block((2, rows, bn), lambda n, *_: (0, 0, n))] + [ANY] * (2 if rel else 4),
-                [sds(da_shape)] + [sds(cat_shape)] * 2 + ([] if rel else [sds((half, sl, dim))] * 2),
-                (me, g, w_down, token, *cats), prefetch=1, scratch=[dma(2 if rel else 4)], aliases={4: 1, 5: 2} if rel else None,
+                functools.partial(dact_kernel, kind), (), [SMEM] + [ANY] * (len(gs) + 1 + len(homes) + len(tokens)), [ANY] * n_out,
+                ([sds((2, rows, ffn))] + [sds(cat_shape)] * 2 + [sds((half, sl, dim))] * 2)[: n_out],
+                (me, *gs, w_down, *homes, *tokens), aliases={2 + len(gs) + i: 1 + i for i in range(len(homes))},
+                scratch=[pltpu.VMEM((2, bn, dim), BF), pltpu.VMEM((2,) + pair, BF), pltpu.VMEM((batch, sl, dim), BF),
+                         pltpu.SemaphoreType.DMA((2, 1)), pltpu.SemaphoreType.DMA((2, 1)), dma(2), dma(4)],
                 flops=4 * rows * dim * ffn, nbytes=2 * ffn * dim + 4 * rows * ffn)
 
-        da_own, gcat0, gcat1, go0, go1 = dact_near(0, grad_out, kv, ())
+        da_own, gcat0, gcat1, go0, go1 = dact(OWN, (grad_out,), (), (kv,), 5)
         wq_far = tie(wq_far, da_own)
         wq_far_mate = to_core(wq_far)
-        da_mate, gcat0, gcat1 = dact_near(1, g_mate, da_own, (gcat0, gcat1))
+        da_mate, gcat0, gcat1 = dact(MATE, (g_mate,), (gcat0, gcat1), (da_own,), 3)
         kv_far = tie(kv_far, da_mate)
         kv_far_mate = to_core(kv_far)
         wqs = (w_query, wq_mate, wq_far, wq_far_mate)
@@ -611,34 +693,30 @@
 
         o_shape = (2, 2, rows, ffn)
 
-        def mlp(other, c, za, zb, da, db, prev, token):
-            extra = list(prev) if prev is not None else []
-            o_spec = block((1, 2, rows, bn), lambda n, m: (abs(other - m[0] // 2), 0, 0, n))
-            w_spec = block((dim, bn), lambda n, *_: (0, n))
-            d_spec = block((1, rows, bn), lambda n, *_: (c, 0, n))
+        def mlp(other, at, fused, za, zb, da, db, prev, tokens):
+            n_out = 5 if fused else 4
+            weights = (w_gate, w_up, w_down) if fused else (w_gate, w_up)
+            sem = lambda k, n: pltpu.SemaphoreType.DMA((k, n))
+            scratch = [pltpu.VMEM((2, half, sl, dim), BF)] + [pltpu.VMEM((2, dim, bn), BF)] * 2 + [pltpu.VMEM((2, 2, rows, bn), BF)] * 3
+            scratch += [sem(2, 3 if fused else 4), sem(2, 6), dma(2), dma(4)]
+            scratch += [pltpu.VMEM((2, bn, dim), BF), pltpu.VMEM((2, half, sl, dim), BF), dma(2)] if fused else [pltpu.VMEM((2, 2, rows, bn), BF)]
             return run(
-                functools.partial(mlp_kernel, other), (ffn // bn,),
-                [half_spec, half_spec, d_spec, d_spec, w_spec, w_spec] + [ANY] * (len(extra) + 1),
-                [o_spec] * 3 + [ANY], [sds(o_shape)] * 3 + [sds(cat_shape)],
-                (me, za, zb, da, db, w_gate, w_up, *extra, token),
-                prefetch=1, scratch=[dma(2)], aliases={7 + i: i for i in range(4)} if extra else None,
-                flops=8 * rows * dim * ffn, nbytes=4 * ffn * dim + 16 * rows * ffn)
-
-        near0 = mlp(0, 0, zs[0], z_mate[0], da_own, da_mate, None, z1)
-        near1 = mlp(0, 1, zs[1], z_mate[1], da_own, da_mate, None, near0[0])
+                functools.partial(mlp_kernel, other, at, fused), (),
+                [SMEM] + [ANY] * (4 + len(weights) + len(prev) + len(tokens)), [ANY] * n_out,
+                [sds(o_shape)] * 3 + [sds(cat_shape)] * (n_out - 3),
+                (me, za, zb, da, db, *weights, *prev, *tokens), scratch=scratch,
+                aliases={5 + len(weights) + i: i for i in range(len(prev))},
+                flops=(12 if fused else 8) * rows * dim * ffn, nbytes=4 * ffn * dim + 16 * rows * ffn)
+
+        near0 = mlp(0, (0, 0), False, zs[0], z_mate[0], da_own, da_mate, (), (z1,))
+        near1 = mlp(0, (1, 1), False, zs[1], z_mate[1], da_own, da_mate, (), (near0[0],))
 
         ga = tie(g_far[0], near0[0])
         gb = to_core(ga)
-        da_far, db_far, gcat0 = run(
-            dact_far_kernel, (ffn // bn,),
-            [half_spec, half_spec, block((bn, dim), lambda n, *_: (n, 0)), ANY, ANY],
-            [block((1, rows, bn), lambda n, *_: (0, 0, n))] * 2 + [ANY],
-            [sds((1, rows, ffn))] * 2 + [sds(cat_shape)],
-            (me, ga, gb, w_down, gcat0, near1[0]), prefetch=1, scratch=[dma(2)], aliases={4: 2},
-            flops=4 * rows * dim * ffn, nbytes=2 * ffn * dim + 4 * rows * ffn)
+        da_far, gcat0 = dact(FAR, (ga, gb), (gcat0,), (near1[0],), 2)
         za = tie(z_far[0], near1[0])
         zb = to_core(za)
-        full0 = mlp(1, 0, za, zb, da_far, db_far, near0, da_far)
+        full0 = mlp(1, (0, 1), False, za, zb, da_far, da_far, near0, ())
 
         def gated_grad(full):
             bj = 512
@@ -660,17 +738,9 @@
         part0 = scatter(mlp_part0)
 
         ga, za = tie(g_far[1], full0[0]), tie(z_far[1], full0[0])
-        gb, zb = to_core(ga), to_core(za)
-        bf = 512
-        o_spec = block((1, 2, rows, bf), lambda n, m: (1 - m[0] // 2, 0, 0, n))
-        w_spec = block((dim, bf), lambda n, *_: (0, n))
-        full1 = run(
-            functools.partial(mlp_fused_kernel, 1), (ffn // bf,),
-            [half_spec] * 4 + [w_spec, w_spec, block((bf, dim), lambda n, *_: (n, 0))] + [ANY] * 7,
-            [o_spec] * 3 + [ANY] * 2, [sds(o_shape)] * 3 + [sds(cat_shape)] * 2,
-            (me, za, zb, ga, gb, w_gate, w_up, w_down, *near1, gcat1, dz_part0, mlp_part0),
-            prefetch=1, scratch=[dma(4)], aliases={8 + i: i for i in range(5)},
-            flops=12 * rows * dim * ffn, nbytes=6 * ffn * dim + 12 * rows * ffn)
+        gb = to_core(ga)
+        zb = to_core(za)
+        full1 = mlp(1, None, True, za, zb, ga, gb, (*near1, gcat1), (dz_part0, mlp_part0))
         gcat1 = full1[4]
         dz_part1 = gated_grad(full1)
         dz1 = scatter(dz_part1)
@@ -701,7 +771,7 @@
             [tok_spec, q_spec, kv4_spec, block((1, dim), lambda b, *_: (0, 0))],
             [sds((batch, sl, dim)), sds((batch, sl, qd)), sds((tp_n, batch, sl, 2 * hd)), sds((1, dim), F32)],
             (me, dz0, dz1, resid, grad_out, gain2, *wos, *kvs, q, pt, cos_t, sin_t, mlp_part1, g_down, part0), prefetch=1,
-            scratch=[pltpu.VMEM((hd, seq), BF), pltpu.VMEM((seq, hd), BF), pltpu.VMEM((heads * sl, hd), BF), pltpu.VMEM((heads * sl, hd), BF), pltpu.VMEM((seq, heads * sl), BF), pltpu.VMEM((2, seq, sl), F32)],
+            scratch=[pltpu.VMEM((hd, seq), BF), pltpu.VMEM((seq, hd), BF), pltpu.VMEM((heads * sl, hd), BF), pltpu.VMEM((heads * sl, hd), BF), pltpu.VMEM((seq, heads * sl), BF), pltpu.VMEM((2, seq, sl), F32)] + [pltpu.VMEM((seq, hd), F32)] * 2,
             flops=2 * own * dim * qd + 8 * own * seq * qd, nbytes=2 * own * heads * seq)
         dkv = lax.psum_scatter(dkv_part, "tp", scatter_dimension=0)
 
@@ -711,7 +781,7 @@
             block_grad_kernel, (tp_n,), [y_spec(lambda j: j), x_spec, ANY],
             block((1, cols, dim), lambda j, m: (m[0] ^ j, 0, 0)), sds((tp_n, cols, dim), F32), (me, mixed2, dres2, dkv_part),
             prefetch=1, flops=2 * own * dim * qd, nbytes=4 * dim * qd)
-        g_out_sum = lax.psum_scatter(g_out, "tp", scatter_dimension=0)
+        g_out_sum = lax.psum_scatter(g_out.reshape(qd, dim), "tp", scatter_dimension=0, tiled=True)
         to_mate = run(
             block_grad_kernel, (2,), [x_spec, y_spec(lambda j: 1 + 2 * j), ANY],
             block((1, dim, cols), lambda j: (j, 0, 0)), sds((2, dim, cols), F32), (u2, dq2, g_out),

time: 1690 us -> 1680 us (level)
    unnamed x13 -> x12, waiting for transfers between devices: 35.1 us -> 0.86 us
    reduce_scatter x0 -> x1, waiting for transfers between devices: none -> 33.3 us  [local_layer(): lax.psum_scatter(g_out.reshape(qd, dim), 'tp', scatter_dimension=0, tiled...]
where the time goes in v3:
time: 1680 us; the launch traced here: 1670 us
  Pallas kernels  1200 us (71%)
  waiting for transfers between devices  295 us (18%)
  matrix products  122 us (7%)
    pallas_call x21, Pallas kernels, run(): pl.pallas_call(kernel, grid_spec=spec, out_shape=out_shape, input_output_...  1200 us
    ppermute x8, waiting for transfers between devices, to_chip(): return lax.ppermute(x, 'tp', chip_flip)  250 us
    dot_general x2, matrix products, dot_nn(): lax.dot_general(a, b, (((1,), (0,)), ((), ())), preferred_element_type=F32)  122 us
  transfers between devices with their start and end apart: 29, of which 7 were waited for; matrix products, arithmetic and copies ran while one was open for 5% of the time, Pallas kernels for 65%

profile of v3, /device:TPU:0, one launch (start us, length us, event | category | flops | bytes accessed | tf_op | source)
XLA Modules:
  0.0 1671.7 jit_solution(1027444477386974357)
XLA Ops:
  7.2 0.9 collective-permute-start.5
  8.1 1.3 convert_add_fusion.1
  9.4 9.3 shard_map.230
  18.7 2.5 collective-permute-start.4
  21.7 32.5 %shard_map.231 = (bf16[2,768,4096]{2,1,0:T(8,128)(2,1)}, bf16[2,2,3,256,2048]{4,3,2,1,0:T(8,128)(2,1)}, bf16[2,2,3,256,2048]{4,3,2,1,0:T(8,128)(2,1)}, bf16[3,25...) custom-call(s32[1]{0:T(128)} %bitcast.me_ref.refs_0_, bf16[6,256,2048]{2,1,0:T(8,128)(2,1)} %go_ref.1, ...), custom_call_target="tpu_custom_call" | custom-call | flops 25769803776 | bytes 29360128 | tf_op jit(solution)/shard_map/pallas_call | solution.py:39
  54.2 47.2 %collective-permute-done.1.x_ref = bf16[2048,512]{1,0:T(8,128)(2,1)S(1)} collective-permute-done((bf16[2048,512]{1,0:T(8,128)(2,1)}, bf16[2048,512]{1,0:T(8,128)(2,1)S(1)}, u32[]{:S(2)}, u32[]{:S(2)}) %collective-permute-start.1) | collective-permute-done | bytes 2097184 | tf_op jit(solution)/shard_map/ppermute | solution.py:584
  101.4 1.3 copy-done.4
  102.7 32.5 %shard_map.232 = (bf16[2,768,4096]{2,1,0:T(8,128)(2,1)}, bf16[2,2,3,256,2048]{4,3,2,1,0:T(8,128)(2,1)}, bf16[2,2,3,256,2048]{4,3,2,1,0:T(8,128)(2,1)}) custom-call(s32[1]{0:T(128)} %bitcast.me_ref.refs_0_, bf16[6,256,2048]{2,1,0:T(8,128)(2,1)} %collective-permute-done.5.refs_0_, ...), custom_call_target="tpu_custom_call", output_to_operand_aliasing={{1}: (3, {}), {2}: (4, {})} | custom-call | flops 25769803776 | bytes 29360128 | tf_op jit(solution)/shard_map/pallas_call | solution.py:39
  135.8 1.7 collective-permute-start.8
  137.6 1.6 collective-permute-done.6.k3_ref
  139.2 45.0 %shard_map.233 = (bf16[6,256,2048]{2,1,0:T(8,128)(2,1)}, bf16[6,1024,2048]{2,1,0:T(8,128)(2,1)}, bf16[6,256,2048]{2,1,0:T(8,128)(2,1)}) custom-call(s32[1]{0:T(128)} %bitcast.me_ref.refs_0_, s32[6]{0:T(128)} %pre_ref.1, s32[6]{0:T(128)} %val_ref.1, bf16[6,256,2048]{2,1,0:T(8,128)(2,1)} %get-tuple-element.58.u_ref, bf16[2048,512]{1,0:T(8,128)(2,1)} %w0_ref.9, ...), custom_call_target="tpu_custom_call" | custom-call | flops 25769803776 | bytes 25165824 | tf_op jit(solution)/shard_map/pallas_call | solution.py:39
  184.2 1.3 copy-done
  186.5 3.4 collective-permute-done.9.w3_ref
  189.9 1.3 copy-done.3
  191.2 14.3 shard_map.234
  205.9 1.7 collective-permute-start.14
  207.9 14.3 shard_map.235
  222.3 64.4 %shard_map.236 = (bf16[2,2,768,4096]{3,2,1,0:T(8,128)(2,1)}, bf16[2,2,768,4096]{3,2,1,0:T(8,128)(2,1)}, bf16[2,2,768,4096]{3,2,1,0:T(8,128)(2,1)}, bf16[2,2,3,256,2048]{4,3,2,1,0:T(8,128)(2,1)}) custom-call(s32[1]{0:T(128)} %bitcast.me_ref.refs_0_, bf16[3,256,2048]{2,1,0:T(8,128)(2,1)} %get-tuple-element.65.refs_0_, ...), custom_call_target="tpu_custom_call" | custom-call | flops 51539607552 | bytes 83886080 | tf_op jit(solution)/shard_map/pallas_call | solution.py:39
  287.2 63.8 %shard_map.237 = (bf16[2,2,768,4096]{3,2,1,0:T(8,128)(2,1)}, bf16[2,2,768,4096]{3,2,1,0:T(8,128)(2,1)}, bf16[2,2,768,4096]{3,2,1,0:T(8,128)(2,1)}, bf16[2,2,3,256,2048]{4,3,2,1,0:T(8,128)(2,1)}) custom-call(s32[1]{0:T(128)} %bitcast.me_ref.refs_0_, bf16[3,256,2048]{2,1,0:T(8,128)(2,1)} %get-tuple-element.67.refs_6_.refs_0_.rest_0_, ...), custom_call_target="tpu_custom_call" | custom-call | flops 51539607552 | bytes 83886080 | tf_op jit(solution)/shard_map/pallas_call | solution.py:39
  351.0 1.7 copy-done.2
  352.8 32.5 %shard_map.238 = (bf16[2,768,4096]{2,1,0:T(8,128)(2,1)}, bf16[2,2,3,256,2048]{4,3,2,1,0:T(8,128)(2,1)}) custom-call(s32[1]{0:T(128)} %bitcast.me_ref.refs_0_, bf16[3,256,2048]{2,1,0:T(8,128)(2,1)} %tie.15.refs_0_, bf16[3,256,2048]{2,1,0:T(8,128)(2,1)} %collective-permute-done.15.refs_1_, ...), custom_call_target="tpu_custom_call", output_to_operand_aliasing={{1}: (4, {})} | custom-call | flops 25769803776 | bytes 29360128 | tf_op jit(solution)/shard_map/pallas_call | solution.py:39
  385.4 1.7 copy-done.6
  387.0 63.8 %shard_map.239 = (bf16[2,2,768,4096]{3,2,1,0:T(8,128)(2,1)}, bf16[2,2,768,4096]{3,2,1,0:T(8,128)(2,1)}, bf16[2,2,768,4096]{3,2,1,0:T(8,128)(2,1)}, bf16[2,2,3,256,2048]{4,3,2,1,0:T(8,128)(2,1)}) custom-call(s32[1]{0:T(128)} %bitcast.me_ref.refs_0_, ...), custom_call_target="tpu_custom_call", output_to_operand_aliasing={{0}: (7, {}), {1}: (8, {}), {2}: (9, {}), {3}: (10, {})} | custom-call | flops 51539607552 | bytes 83886080 | tf_op jit(solution)/shard_map/pallas_call | solution.py:39
  450.9 60.3 %convolution_convert_fusion.1.refs_13_ = bf16[3072,2048]{1,0:T(8,128)(2,1)} fusion(bf16[3072,4096]{1,0:T(8,128)(2,1)} %bitcast.38, bf16[4096,2048]{1,0:T(8,128)(2,1)} %refs_6_.1), kind=kOutput, calls=%fused_computation.1 | convolution fusion | flops 51545899008 | bytes 54525952 | tf_op jit(solution)/shard_map/dot_general | solution.py:21
  511.3 118.9 %shard_map.240.refs_12_ = bf16[4,768,2048]{2,1,0:T(8,128)(2,1)} custom-call(bf16[2,2,768,4096]{3,2,1,0:T(8,128)(2,1)} %get-tuple-element.76.dg_ref, bf16[2,2,768,4096]{3,2,1,0:T(8,128)(2,1)} %get-tuple-element.77.du_ref, bf16[2048,4096]{1,0:T(8,128)(2,1)} %wg_ref.3, bf16[2048,4096]{1,0:T(8,128)(2,1)} %wu_ref.3, ...), custom_call_target="tpu_custom_call" | custom-call | flops 103079215104 | bytes 50331648 | tf_op jit(solution)/shard_map/pallas_call | solution.py:39
  630.3 0.9 collective-permute-start.18
  631.2 0.9 copy-done.1
  632.1 0.9 collective-permute-start.16
  633.0 113.5 %collective-permute-done.18.x_ref = bf16[3,256,2048]{2,1,0:T(8,128)(2,1)} collective-permute-done((bf16[3,256,2048]{2,1,0:T(8,128)(2,1)}, bf16[3,256,2048]{2,1,0:T(8,128)(2,1)}, u32[]{:S(2)}, u32[]{:S(2)}) %collective-permute-start.18) | collective-permute-done | bytes 3145760 | tf_op jit(solution)/shard_map/ppermute | solution.py:584
  746.5 89.3 %collective-permute-done.16.x_ref = bf16[3,256,2048]{2,1,0:T(8,128)(2,1)} collective-permute-done((bf16[3,256,2048]{2,1,0:T(8,128)(2,1)S(1)}, bf16[3,256,2048]{2,1,0:T(8,128)(2,1)}, u32[]{:S(2)}, u32[]{:S(2)}) %collective-permute-start.16) | collective-permute-done | bytes 3145760 | tf_op jit(solution)/shard_map/ppermute | solution.py:584
  835.8 5.9 collective-permute-done.17.refs_1_
  841.7 1.7 copy-done.7
  843.4 92.8 %shard_map.241 = (bf16[2,2,768,4096]{3,2,1,0:T(8,128)(2,1)}, bf16[2,2,768,4096]{3,2,1,0:T(8,128)(2,1)}, bf16[2,2,768,4096]{3,2,1,0:T(8,128)(2,1)}, bf16[2,2,3,25...) custom-call(s32[1]{0:T(128)} %bitcast.me_ref.refs_0_, ...), custom_call_target="tpu_custom_call", output_to_operand_aliasing={{0}: (8, {}), {1}: (9, {}), {2}: (10, {}), {3}: (11, {}), {... | custom-call | flops 77309411328 | bytes 83886080 | tf_op jit(solution)/shard_map/pallas_call | solution.py:39
  936.2 115.2 %shard_map.242 = bf16[4,768,2048]{2,1,0:T(8,128)(2,1)} custom-call(bf16[2,2,768,4096]{3,2,1,0:T(8,128)(2,1)} %get-tuple-element.84.dg_ref, bf16[2,2,768,4096]{3,2,1,0:T(8,128)(2,1)} %get-tuple-element.85.du_ref, bf16[2048,4096]{1,0:T(8,128)(2,1)} %wg_ref.3, bf16[2048,4096]{1,0:T(8,128)(2,1)} %wu_ref.3, bf16[2,2,768,4096]{3,2,1,0:T(8,128)(2,1)} %get-tuple-element.86.rest_0_), custom_call_target="tpu_custom_call" | custom-call | flops 103079215104 | bytes 50331648 | tf_op jit(solution)/shard_map/pallas_call | solution.py:39
  1051.5 61.8 %convolution_convert_fusion.refs_4_.token0_ref = bf16[3072,2048]{1,0:T(8,128)(2,1)} fusion(bf16[3072,4096]{1,0:T(8,128)(2,1)} %bitcast.41, bf16[4096,2048]{1,0:T(8,128)(2,1)} %refs_6_.1), kind=kOutput, calls=%fused_computation | convolution fusion | flops 51545899008 | bytes 54525952 | tf_op jit(solution)/shard_map/dot_general | solution.py:21
  1113.6 35.6 %shard_map.243.token1_ref.refs_4_ = f32[4096,2048]{1,0:T(8,128)} custom-call(bf16[3072,4096]{1,0:T(8,128)(2,1)} %bitcast.39, bf16[3072,4096]{1,0:T(8,128)(2,1)} %bitcast.42, bf16[3072,2048]{1,0:T(8,128)(2,1)} %bitcast.51, bf16[3072,2048]{1,0:T(8,128)(2,1)} %bitcast.53, bf16[3072,2048]{1,0:T(8,128)(2,1)} %convolution_convert_fusion.refs_4_.token0_ref), custom_call_target="tpu_custom_call" | custom-call | flops 25769803776 | bytes 33554432 | tf_op jit(solution)/shard_map/pallas_call | solution.py:39
  1149.3 65.5 %shard_map.244 = (bf16[6,256,2048]{2,1,0:T(8,128)(2,1)}, bf16[6,256,2048]{2,1,0:T(8,128)(2,1)}, bf16[4,6,256,512]{3,2,1,0:T(8,128)(2,1)}, f32[1,2048]{1,0:T(1,128)}) custom-call(s32[1]{0:T(128)} %bitcast.me_ref.refs_0_, bf16[3,256,2048]{2,1,0:T(8,128)(2,1)} %bitcast.65, bf16[3,256,2048]{2,1,0:T(8,128)(2,1)} %bitcast.67, ...), custom_call_target="tpu_custom_call" | custom-call | flops 38654705664 | bytes 25165824 | tf_op jit(solution)/shard_map/pallas_call | solution.py:39
  1214.9 19.4 %shard_map.245.refs_2_ = f32[4,512,2048]{2,1,0:T(8,128)} custom-call(s32[1]{0:T(128)} %bitcast.me_ref.refs_0_, bf16[1536,2048]{1,0:T(8,128)(2,1)} %bitcast.45, bf16[1536,2048]{1,0:T(8,128)(2,1)} %bitcast.75, bf16[4,6,256,512]{3,2,1,0:T(8,128)(2,1)} %get-tuple-element.92.refs_3_), custom_call_target="tpu_custom_call" | custom-call | flops 12884901888 | bytes 16777216 | tf_op jit(solution)/shard_map/pallas_call | solution.py:39
  1234.3 12.3 shard_map.246.refs_5_
  1246.6 91.1 %shard_map.247.token_ref = f32[4096,2048]{1,0:T(8,128)} custom-call(bf16[3072,4096]{1,0:T(8,128)(2,1)} %bitcast.40, bf16[3072,4096]{1,0:T(8,128)(2,1)} %bitcast.43, bf16[3072,2048]{1,0:T(8,128)(2,1)} %bitcast.52, bf16[3072,2048]{1,0:T(8,128)(2,1)} %bitcast.54, f32[4096,2048]{1,0:T(8,128)} %shard_map.243.token1_ref.refs_4_, ...), custom_call_target="tpu_custom_call", output_to_operand_aliasing={{}: (4, {})} | custom-call | flops 77309411328 | bytes 33554432 | tf_op jit(solution)/shard_map/pallas_call | solution.py:39
  1337.7 15.4 shard_map.248
  1353.1 40.2 %shard_map.249 = (bf16[6,256,2048]{2,1,0:T(8,128)(2,1)}, f32[2056,512]{1,0:T(8,128)}, bf16[6,256,2048]{2,1,0:T(8,128)(2,1)}) custom-call(s32[1]{0:T(128)} %bitcast.me_ref.refs_0_, bf16[6,256,512]{2,1,0:T(8,128)(2,1)} %bitcast.68, bf16[6,256,2048]{2,1,0:T(8,128)(2,1)} %get-tuple-element.93.dq_ref, bf16[6,256,2048]{2,1,0:T(8,128)(2,1)} %get-tuple-element.58.u_ref, ...), custom_call_target="tpu_custom_call" | custom-call | flops 19327352832 | bytes 25165824 | tf_op jit(solution)/shard_map/pallas_call | solution.py:39
  1393.4 0.7 reduce-scatter.17.cloned.1.call-update
  1394.7 223.3 %shard_map.250 = (f32[2048,4096]{1,0:T(8,128)}, f32[2048,4096]{1,0:T(8,128)}) custom-call(bf16[3072,2048]{1,0:T(8,128)(2,1)} %bitcast.74, bf16[3072,2048]{1,0:T(8,128)(2,1)} %bitcast.73, bf16[3072,4096]{1,0:T(8,128)(2,1)} %bitcast.71, bf16[3072,4096]{1,0:T(8,128)(2,1)} %bitcast.69, bf16[3072,4096]{1,0:T(8,128)(2,1)} %bitcast.72, ...), custom_call_target="tpu_custom_call" | custom-call | flops 206158430208 | bytes 33554432 | tf_op jit(solution)/shard_map/pallas_call | solution.py:39
  1618.1 6.8 add_bitcast_fusion
  1624.9 0.8 slice_bitcast_fusion
  1626.9 4.5 fusion
  1631.4 33.3 %reduce-scatter.17.cloned.1.call-done = f32[512,2048]{1,0:T(8,128)} async-done(((f32[2048,2048]{1,0:T(8,128)}), f32[512,2048]{1,0:T(8,128)}) %reduce-scatter.17.cloned.1.call-update) | async-done | bytes 4194320 | tf_op jit(solution)/shard_map/reduce_scatter | solution.py:784
  (73 shorter events, 5.9 us)
Async XLA Ops:
  7.2 1142.0 %reduce-scatter.23.cloned.1.call-start = ((), (), s32[]{:S(2)}) async-start(), calls=%async_computation.10 | async-start | bytes 15728640
  7.2 95.5 %collective-permute-start.5 = (bf16[6,256,2048]{2,1,0:T(8,128)(2,1)}, bf16[6,256,2048]{2,1,0:T(8,128)(2,1)}, u32[]{:S(2)}, u32[]{:S(2)}) collective-permute-start(bf16[6,256,2048]{2,1,0:T(8,128)(2,1)} %go_ref.1), channel_id=1, source_target_pairs={{0,1},{1,0},{2,3},{3,2},{4,5},{5,4},{6,7},{7,6}} | collective-permute-start | bytes 18874376 | tf_op jit(solution)/shard_map/ppermute | solution.py:581
  18.7 116.6 %collective-permute-start.4 = (bf16[6,256,512]{2,1,0:T(8,128)(2,1)}, bf16[6,256,512]{2,1,0:T(8,128)(2,1)}, u32[]{:S(2)}, u32[]{:S(2)}) collective-permute-start(bf16[6,256,512]{2,1,0:T(8,128)(2,1)} %get-tuple-element.59.refs_2_.k0_ref), channel_id=1, source_target_pairs={{0,2},{2,0},{1,3},{3,1},{4,6},{6,4},{5,7},{7,5}} | collective-permute-start | bytes 4718600 | tf_op jit(solution)/shard_map/ppermute | solution.py:584
  21.2 116.4 %collective-permute-start.3 = (bf16[6,256,512]{2,1,0:T(8,128)(2,1)}, bf16[6,256,512]{2,1,0:T(8,128)(2,1)}, u32[]{:S(2)}, u32[]{:S(2)}) collective-permute-start(bf16[6,256,512]{2,1,0:T(8,128)(2,1)} %get-tuple-element.59.refs_2_.k0_ref), channel_id=1, source_target_pairs={{0,1},{1,0},{2,3},{3,2},{4,5},{5,4},{6,7},{7,6}} | collective-permute-start | bytes 4718600 | tf_op jit(solution)/shard_map/ppermute | solution.py:581
  21.4 80.0 %collective-permute-start.1 = (bf16[2048,512]{1,0:T(8,128)(2,1)}, bf16[2048,512]{1,0:T(8,128)(2,1)S(1)}, u32[]{:S(2)}, u32[]{:S(2)}) collective-permute-start(bf16[2048,512]{1,0:T(8,128)(2,1)} %w0_ref.9), channel_id=1, source_target_pairs={{0,2},{2,0},{1,3},{3,1},{4,6},{6,4},{5,7},{7,5}} | collective-permute-start | bytes 6291464 | tf_op jit(solution)/shard_map/ppermute | solution.py:584
  21.7 115.9 %collective-permute-start = (bf16[2048,512]{1,0:T(8,128)(2,1)}, bf16[2048,512]{1,0:T(8,128)(2,1)}, u32[]{:S(2)}, u32[]{:S(2)}) collective-permute-start(bf16[2048,512]{1,0:T(8,128)(2,1)} %w0_ref.9), channel_id=1, source_target_pairs={{0,1},{1,0},{2,3},{3,2},{4,5},{5,4},{6,7},{7,6}} | collective-permute-start | bytes 6291464 | tf_op jit(solution)/shard_map/ppermute | solution.py:581
  101.4 1.3 copy-start.4
  102.7 34.9 %collective-permute-start.2 = (bf16[2048,512]{1,0:T(8,128)(2,1)}, bf16[2048,512]{1,0:T(8,128)(2,1)}, u32[]{:S(2)}, u32[]{:S(2)}) collective-permute-start(bf16[2048,512]{1,0:T(8,128)(2,1)} %tie.10.w2_ref), channel_id=1, source_target_pairs={{0,1},{1,0},{2,3},{3,2},{4,5},{5,4},{6,7},{7,6}} | collective-permute-start | bytes 6291464 | tf_op jit(solution)/shard_map/ppermute | solution.py:581
  135.3 3.9 collective-permute-start.6
  135.8 48.4 %collective-permute-start.8 = (bf16[512,2048]{1,0:T(8,128)(2,1)}, bf16[512,2048]{1,0:T(8,128)(2,1)S(1)}, u32[]{:S(2)}, u32[]{:S(2)}) collective-permute-start(bf16[512,2048]{1,0:T(8,128)(2,1)} %w0_ref.8), channel_id=1, source_target_pairs={{0,2},{2,0},{1,3},{3,1},{4,6},{6,4},{5,7},{7,5}} | collective-permute-start | bytes 6291464 | tf_op jit(solution)/shard_map/ppermute | solution.py:584
  137.6 49.0 %collective-permute-start.7 = (bf16[512,2048]{1,0:T(8,128)(2,1)}, bf16[512,2048]{1,0:T(8,128)(2,1)}, u32[]{:S(2)}, u32[]{:S(2)}) collective-permute-start(bf16[512,2048]{1,0:T(8,128)(2,1)} %w0_ref.8), channel_id=1, source_target_pairs={{0,1},{1,0},{2,3},{3,2},{4,5},{5,4},{6,7},{7,6}} | collective-permute-start | bytes 6291464 | tf_op jit(solution)/shard_map/ppermute | solution.py:581
  184.2 1.7 copy-start.5
  184.2 1.3 copy-start
  185.6 4.4 collective-permute-start.9
  189.9 1.3 copy-start.3
  205.5 16.8 %collective-permute-start.12 = (bf16[3,256,2048]{2,1,0:T(8,128)(2,1)}, bf16[3,256,2048]{2,1,0:T(8,128)(2,1)}, u32[]{:S(2)}, u32[]{:S(2)}) collective-permute-start(bf16[3,256,2048]{2,1,0:T(8,128)(2,1)} %get-tuple-element.65.refs_0_), channel_id=1, source_target_pairs={{0,1},{1,0},{2,3},{3,2},{4,5},{5,4},{6,7},{7,6}} | collective-permute-start | bytes 9437192 | tf_op jit(solution)/shard_map/ppermute | solution.py:581
  205.9 80.8 %collective-permute-start.14 = (bf16[3,256,2048]{2,1,0:T(8,128)(2,1)}, bf16[3,256,2048]{2,1,0:T(8,128)(2,1)}, u32[]{:S(2)}, u32[]{:S(2)}) collective-permute-start(bf16[3,256,2048]{2,1,0:T(8,128)(2,1)} %tie.14), channel_id=1, source_target_pairs={{0,2},{2,0},{1,3},{3,1},{4,6},{6,4},{5,7},{7,5}} | collective-permute-start | bytes 9437192 | tf_op jit(solution)/shard_map/ppermute | solution.py:584
  207.6 143.3 %collective-permute-start.10 = (bf16[3,256,2048]{2,1,0:T(8,128)(2,1)}, bf16[3,256,2048]{2,1,0:T(8,128)(2,1)S(1)}, u32[]{:S(2)}, u32[]{:S(2)}) collective-permute-start(bf16[3,256,2048]{2,1,0:T(8,128)(2,1)} %get-tuple-element.65.refs_0_), channel_id=1, source_target_pairs={{0,2},{2,0},{1,3},{3,1},{4,6},{6,4},{5,7},{7,5}} | collective-permute-start | bytes 9437192 | tf_op jit(solution)/shard_map/ppermute | solution.py:584
  222.3 64.9 %collective-permute-start.11 = (bf16[3,256,2048]{2,1,0:T(8,128)(2,1)}, bf16[3,256,2048]{2,1,0:T(8,128)(2,1)}, u32[]{:S(2)}, u32[]{:S(2)}) collective-permute-start(bf16[3,256,2048]{2,1,0:T(8,128)(2,1)} %get-tuple-element.67.refs_6_.refs_0_.rest_0_), channel_id=1, source_target_pairs={{0,1},{1,0},{2,3},{3,2},{4,5},{5,4},{6,7},{7,6}} | collective-permute-start | bytes 9437192 | tf_op jit(solution)/shard_map/ppermute | solution.py:581
  286.7 66.1 %collective-permute-start.15 = (bf16[3,256,2048]{2,1,0:T(8,128)(2,1)}, bf16[3,256,2048]{2,1,0:T(8,128)(2,1)}, u32[]{:S(2)}, u32[]{:S(2)}) collective-permute-start(bf16[3,256,2048]{2,1,0:T(8,128)(2,1)} %tie.15.refs_0_), channel_id=1, source_target_pairs={{0,1},{1,0},{2,3},{3,2},{4,5},{5,4},{6,7},{7,6}} | collective-permute-start | bytes 9437192 | tf_op jit(solution)/shard_map/ppermute | solution.py:581
  351.0 1.7 copy-start.2
  352.7 32.7 %collective-permute-start.13 = (bf16[3,256,2048]{2,1,0:T(8,128)(2,1)}, bf16[3,256,2048]{2,1,0:T(8,128)(2,1)S(1)}, u32[]{:S(2)}, u32[]{:S(2)}) collective-permute-start(bf16[3,256,2048]{2,1,0:T(8,128)(2,1)} %tie.13.refs_0_), channel_id=1, source_target_pairs={{0,1},{1,0},{2,3},{3,2},{4,5},{5,4},{6,7},{7,6}} | collective-permute-start | bytes 9437192 | tf_op jit(solution)/shard_map/ppermute | solution.py:581
  385.4 1.7 copy-start.6
  511.2 638.0 %reduce-scatter.19.cloned.1.call-start = ((), (), s32[]{:S(2)}) async-start(), calls=%async_computation.8 | async-start | bytes 15728640
  630.2 1.9 copy-start.1
  630.2 519.1 %reduce-scatter.21.cloned.1.call-start = ((), (), s32[]{:S(2)}) async-start(), calls=%async_computation.9 | async-start | bytes 15728640
  630.3 116.2 %collective-permute-start.18 = (bf16[3,256,2048]{2,1,0:T(8,128)(2,1)}, bf16[3,256,2048]{2,1,0:T(8,128)(2,1)}, u32[]{:S(2)}, u32[]{:S(2)}) collective-permute-start(bf16[3,256,2048]{2,1,0:T(8,128)(2,1)} %tie.17), channel_id=1, source_target_pairs={{0,2},{2,0},{1,3},{3,1},{4,6},{6,4},{5,7},{7,5}} | collective-permute-start | bytes 9437192 | tf_op jit(solution)/shard_map/ppermute | solution.py:584
  632.1 203.7 %collective-permute-start.16 = (bf16[3,256,2048]{2,1,0:T(8,128)(2,1)S(1)}, bf16[3,256,2048]{2,1,0:T(8,128)(2,1)}, u32[]{:S(2)}, u32[]{:S(2)}) collective-permute-start(bf16[3,256,2048]{2,1,0:T(8,128)(2,1)S(1)} %copy-done.1), channel_id=1, source_target_pairs={{0,2},{2,0},{1,3},{3,1},{4,6},{6,4},{5,7},{7,5}} | collective-permute-start | bytes 9437192 | tf_op jit(solution)/shard_map/ppermute | solution.py:584
  746.5 89.3 %collective-permute-start.19 = (bf16[3,256,2048]{2,1,0:T(8,128)(2,1)}, bf16[3,256,2048]{2,1,0:T(8,128)(2,1)}, u32[]{:S(2)}, u32[]{:S(2)}) collective-permute-start(bf16[3,256,2048]{2,1,0:T(8,128)(2,1)} %tie.18.refs_2_), channel_id=1, source_target_pairs={{0,1},{1,0},{2,3},{3,2},{4,5},{5,4},{6,7},{7,6}} | collective-permute-start | bytes 9437192 | tf_op jit(solution)/shard_map/ppermute | solution.py:581
  835.8 5.9 collective-permute-start.17
  841.7 1.7 copy-start.7
  1051.4 301.7 %reduce-scatter.27.cloned.1.call-start = ((), (), s32[]{:S(2)}) async-start(), calls=%async_computation.12 | async-start | bytes 15728640
  1113.3 239.9 %reduce-scatter.25.cloned.1.call-start = ((), (), s32[]{:S(2)}) async-start(), calls=%async_computation.11 | async-start | bytes 7864320
  1214.8 410.1 %all-reduce.7.cloned.1.call-start = ((), (), s32[]{:S(2)}) async-start(), calls=%async_computation.6 | async-start | bytes 8421376 | tf_op jit(solution)/shard_map/psum | solution.py:808
  1246.6 91.1 %collective-permute-start.20 = (f32[2,2048,512]{2,1,0:T(8,128)}, f32[2,2048,512]{2,1,0:T(8,128)}, u32[]{:S(2)}, u32[]{:S(2)}) collective-permute-start(f32[2,2048,512]{2,1,0:T(8,128)} %shard_map.246.refs_5_), channel_id=1, source_target_pairs={{0,1},{1,0},{2,3},{3,2},{4,5},{5,4},{6,7},{7,6}} | collective-permute-start | bytes 25165832 | tf_op jit(solution)/shard_map/ppermute | solution.py:581
  1393.4 271.3 %reduce-scatter.17.cloned.1.call-start = ((), (), s32[]{:S(2)}) async-start(), calls=%async_computation.7 | async-start | bytes 20971520 | tf_op jit(solution)/shard_map/reduce_scatter | solution.py:784
  1394.1 223.9 %collective-permute-start.21 = (f32[1,2048,512]{2,1,0:T(8,128)}, f32[1,2048,512]{2,1,0:T(8,128)}, u32[]{:S(2)}, u32[]{:S(2)}) collective-permute-start(f32[1,2048,512]{2,1,0:T(8,128)} %get-tuple-element.96.token0_ref), channel_id=1, source_target_pairs={{0,2},{2,0},{1,3},{3,1},{4,6},{6,4},{5,7},{7,5}} | collective-permute-start | bytes 12582920 | tf_op jit(solution)/shard_map/ppermute | solution.py:584
Sparse Core Ops, SparseCore 0:
  511.3 95.2 reduce-scatter.22
  630.3 162.8 reduce-scatter.18
  1051.5 94.7 reduce-scatter.20
  1148.7 94.0 reduce-scatter.26
  1245.2 55.0 reduce-scatter.24
  1393.5 148.4 all-reduce.6
  1545.1 119.4 reduce-scatter.16

commit v4 on v3

--- a/solution.py
+++ b/solution.py
@@ -34,7 +34,7 @@
     return pl.BlockSpec(shape, lambda *_: zeros, pipeline_mode=pl.Buffered(1))
 
 
-def run(kernel, grid, in_specs, out_specs, out_shape, args, scratch=(), prefetch=0, aliases=None, flops=0, nbytes=0, limit=60):
+def run(kernel, grid, in_specs, out_specs, out_shape, args, scratch=(), prefetch=0, aliases=None, flops=0, nbytes=0, limit=63):
     spec = pltpu.PrefetchScalarGridSpec(num_scalar_prefetch=prefetch, grid=grid, in_specs=in_specs, out_specs=out_specs, scratch_shapes=scratch)
     return pl.pallas_call(
         kernel,
@@ -57,15 +57,18 @@
 
 
 def pre_kernel(me_ref, h_ref, gain_ref, wk_ref, wv_ref, cos_ref, sin_ref, u_ref, kv_ref):
-    x = h_ref[0].astype(F32)
+    n, sl, dim = h_ref.shape
+    x = h_ref[...].reshape(n * sl, dim).astype(F32)
     inv = lax.rsqrt(jnp.mean(x * x, axis=-1, keepdims=True) + EPS)
     u = (x * inv * gain_ref[...]).astype(BF)
-    u_ref[0] = u
+    u_ref[...] = u.reshape(n, sl, dim)
     hd = wk_ref.shape[1]
-    first, second = rope_fwd(dot_nn(u, wk_ref[...]), cos_ref[...], sin_ref[...])
-    kv_ref[0, :, : hd // 2] = first.astype(BF)
-    kv_ref[0, :, hd // 2 : hd] = second.astype(BF)
-    kv_ref[0, :, hd:] = dot_nn(u, wv_ref[...]).astype(BF)
+    k, v = dot_nn(u, wk_ref[...]), dot_nn(u, wv_ref[...])
+    for i in range(n):
+        first, second = rope_fwd(k[i * sl : (i + 1) * sl], cos_ref[...], sin_ref[...])
+        kv_ref[i, :, : hd // 2] = first.astype(BF)
+        kv_ref[i, :, hd // 2 : hd] = second.astype(BF)
+        kv_ref[i, :, hd:] = v[i * sl : (i + 1) * sl].astype(BF)
 
 
 def attn_fwd_kernel(me_ref, pre_ref, val_ref, u_ref, w0_ref, w1_ref, w2_ref, w3_ref, k0_ref, k1_ref, k2_ref, k3_ref, cos_ref, sin_ref, token_ref,
@@ -111,23 +114,34 @@
         mix_ref[0, :, h * hd : (h + 1) * hd] = dot_nn(vt_ref[...], p).T.astype(BF)
 
 
-def fetch_at_first(refs, dst, axis, sems):
+def weight_copies(refs, dst, axis, sems):
+    at, copies = 0, []
+    for i, ref in enumerate(refs):
+        n = ref.shape[axis]
+        copies.append(pltpu.make_async_copy(ref, dst.at[pl.ds(at, n), :] if axis == 0 else dst.at[:, pl.ds(at, n)], sems.at[i]))
+        at += n
+    return copies
+
+
+def start_first(*fetch):
     @pl.when(pl.program_id(0) == 0)
     def _():
-        at, copies = 0, []
-        for i, ref in enumerate(refs):
-            n = ref.shape[axis]
-            copies.append(pltpu.make_async_copy(ref, dst.at[pl.ds(at, n), :] if axis == 0 else dst.at[:, pl.ds(at, n)], sems.at[i]))
-            at += n
-        for c in copies:
+        for c in weight_copies(*fetch):
             c.start()
-        for c in copies:
+
+
+def wait_first(*fetch):
+    @pl.when(pl.program_id(0) == 0)
+    def _():
+        for c in weight_copies(*fetch):
             c.wait()
 
 
 def out_kernel(mix_ref, w0_ref, w1_ref, w2_ref, w3_ref, h_ref, gain_ref, *rest):
     resid_ref, z_ref, wo_ref, sems = rest[-4:]
-    fetch_at_first((w0_ref, w1_ref, w2_ref, w3_ref), wo_ref, 0, sems)
+    fetch = (w0_ref, w1_ref, w2_ref, w3_ref), wo_ref, 0, sems
+    start_first(*fetch)
+    wait_first(*fetch)
     x = (h_ref[0].astype(F32) + dot_nn(mix_ref[0], wo_ref[...])).astype(BF)
     resid_ref[0] = x
     x = x.astype(F32)
@@ -383,7 +397,8 @@
     b = pl.program_id(0)
     dim, hd = wk_ref.shape
     qd = dq_ref.shape[2]
-    fetch_at_first((w0_ref, w1_ref, w2_ref, w3_ref, wk_ref, wv_ref), w_ref, 1, sems)
+    fetch = (w0_ref, w1_ref, w2_ref, w3_ref, wk_ref, wv_ref), w_ref, 1, sems
+    start_first(*fetch)
     half = pl.num_programs(0) // 2
     ho_ref[0] = (res_ref[0].astype(F32) + jnp.where(b < half, p0_ref[0], p1_ref[0]).astype(F32)).astype(BF)
     raw = dkv_ref[0]
@@ -393,8 +408,9 @@
     d_ref[:, qd : qd + hd // 2] = first.astype(BF)
     d_ref[:, qd + hd // 2 : qd + hd] = second.astype(BF)
     d_ref[:, qd + hd :] = raw[:, hd:]
+    gk = dot_tn(u_ref[0], d_ref[:, qd:])
+    wait_first(*fetch)
     dn = dot_nt(d_ref[...], w_ref[...])
-    gk = dot_tn(u_ref[0], d_ref[:, qd:])
     x = h_ref[0].astype(F32)
     inv = lax.rsqrt(jnp.mean(x * x, axis=-1, keepdims=True) + EPS)
     xn = x * inv
@@ -425,18 +441,6 @@
 def block_grad_kernel(*refs):
     x_ref, y_ref, o_ref = refs[-4], refs[-3], refs[-1]
     o_ref[...] = dot_tn(x_ref[...], y_ref[...]).reshape(o_ref.shape)
-
-
-def pair_grad_kernel(x_ref, y_ref, add_ref, token_ref, far_ref, own_ref):
-    out = dot_tn(x_ref[...], y_ref[...]) + add_ref[0]
-
-    @pl.when(pl.program_id(0) == 0)
-    def _():
-        far_ref[0] = out
-
-    @pl.when(pl.program_id(0) == 1)
-    def _():
-        own_ref[0] = out
 
 
 def gated_grad_kernel(dg_ref, du_ref, wg_ref, wu_ref, *rest):
@@ -555,6 +559,15 @@
         o_flows[0].wait(t, t % 2)
 
 
+def split_kernel(x_ref, k_ref, v_ref, m_ref, a_ref):
+    dim, hd = k_ref.shape
+    k_ref[...], v_ref[...] = x_ref[:dim, :hd], x_ref[:dim, hd:]
+    for j, o_ref in enumerate((m_ref, a_ref)):
+        n = dim // (2 * hd)
+        for i in range(n):
+            o_ref[:, i * 2 * hd : (i + 1) * 2 * hd] = x_ref[dim + j * n + i : dim + j * n + i + 1, :]
+
+
 def tie_kernel(x_ref, *rest):
     del x_ref, rest
 
@@ -622,9 +635,10 @@
         wq_mate = to_core(w_query)
         g_mate = to_core(grad_out)
         u, kv = run(
-            pre_kernel, (batch,),
-            [tok_spec, gain_spec, const_spec((dim, hd)), const_spec((dim, hd)), rope_spec, rope_spec],
-            [tok_spec, kv_spec], [sds((batch, sl, dim)), sds((batch, sl, 2 * hd))],
+            pre_kernel, (batch // 2,),
+            [block((2, sl, dim), lambda b, *_: (b, 0, 0)), gain_spec, const_spec((dim, hd)), const_spec((dim, hd)), rope_spec, rope_spec],
+            [block((2, sl, dim), lambda b, *_: (b, 0, 0)), block((2, sl, 2 * hd), lambda b, *_: (b, 0, 0))],
+            [sds((batch, sl, dim)), sds((batch, sl, 2 * hd))],
             (me, hidden, gain1, w_key, w_value, cos_t, sin_t), prefetch=1,
             flops=4 * own * dim * hd, nbytes=6 * own * dim)
         kv_far = to_chip(kv)
@@ -747,11 +761,11 @@
         mlp_part1 = mlp_out(full1)
         part1 = scatter(mlp_part1)
 
-        def weight_grads(x, ys, tokens, first=0, ni=None, prev=None):
+        def weight_grads(x, ys, tokens, first=0, ni=None, prev=None, by=512):
             flat = lambda pair: [a.reshape(4 * rows, -1) for a in pair]
             xs, yf = flat(x), [a for y in ys for a in flat(y)]
             m, n = xs[0].shape[1], yf[0].shape[1]
-            bm, by = 1024, 512
+            bm = 1024
             extra = [prev] if prev is not None else []
             return run(
                 functools.partial(weight_grads_kernel, len(ys), first, ni or m // bm), (),
@@ -782,17 +796,12 @@
             block((1, cols, dim), lambda j, m: (m[0] ^ j, 0, 0)), sds((tp_n, cols, dim), F32), (me, mixed2, dres2, dkv_part),
             prefetch=1, flops=2 * own * dim * qd, nbytes=4 * dim * qd)
         g_out_sum = lax.psum_scatter(g_out.reshape(qd, dim), "tp", scatter_dimension=0, tiled=True)
-        to_mate = run(
-            block_grad_kernel, (2,), [x_spec, y_spec(lambda j: 1 + 2 * j), ANY],
-            block((1, dim, cols), lambda j: (j, 0, 0)), sds((2, dim, cols), F32), (u2, dq2, g_out),
-            flops=own * dim * qd, nbytes=2 * dim * qd)
-        from_mate = to_core(to_mate)
-        g_down = weight_grads(*down_args, (to_mate,), 1, ffn // 1024 - 1, g_down)[0]
-        far_sum, own_sum = run(
-            pair_grad_kernel, (2,), [x_spec, y_spec(lambda j: 2 - 2 * j), block((1, dim, cols), lambda j: (1 - j, 0, 0)), ANY],
-            [block((1, dim, cols), lambda j: (0, 0, 0))] * 2, [sds((1, dim, cols), F32)] * 2, (u2, dq2, from_mate, g_down),
-            flops=own * dim * qd, nbytes=2 * dim * qd)
-        arrived = to_chip(far_sum)
+        g_query = run(
+            block_grad_kernel, (tp_n,), [x_spec, y_spec(lambda j: j), ANY],
+            block((1, dim, cols), lambda j, m: (m[0] ^ j, 0, 0)), sds((tp_n, dim, cols), F32), (me, u2, dq2, g_out),
+            prefetch=1, flops=2 * own * dim * qd, nbytes=4 * dim * qd)
+        g_query_sum = lax.psum_scatter(g_query.reshape(tp_n * dim, cols), "tp", scatter_dimension=0, tiled=True)
+        g_down = weight_grads(*down_args, (g_query,), 1, ffn // 1024 - 1, g_down)[0]
 
         extra = dim // hd
         half_at = [block((1, sl, dim), lambda b, *_: (jnp.minimum(b, half - 1), 0, 0)), block((1, sl, dim), lambda b, *_: (jnp.maximum(b - half, 0), 0, 0))]
@@ -802,16 +811,17 @@
              ] + [ANY] * 6 + [rope_spec, rope_spec, const_spec((1, dim)), tok_spec, *half_at, ANY],
             [tok_spec, block((dim + extra, 2 * hd), lambda b, *_: (0, 0)), tok_spec],
             [sds((batch, sl, dim)), sds((dim + extra, 2 * hd), F32), sds((batch, sl, dim))],
-            (me, dkv, d_q, u, hidden, d_resid, gain1, *wqs, w_key, w_value, cos_t, sin_t, gn2, resid, part0, part1, far_sum), prefetch=1,
+            (me, dkv, d_q, u, hidden, d_resid, gain1, *wqs, w_key, w_value, cos_t, sin_t, gn2, resid, part0, part1, g_down), prefetch=1,
             scratch=[pltpu.VMEM((1, dim), F32), pltpu.VMEM((dim, qd + 2 * hd), BF), pltpu.VMEM((sl, qd + 2 * hd), BF), dma(6)],
             flops=2 * own * dim * (qd + 4 * hd), nbytes=8 * own * dim)
         gkv = lax.psum(gkv, "tp")
-        g_key, g_value = gkv[:dim, :hd], gkv[:dim, hd:]
-        g_mlp_norm = gkv[dim : dim + extra // 2].reshape(dim)
-        g_attn_norm = gkv[dim + extra // 2 :].reshape(dim)
-
-        g_gate, g_up = weight_grads((full0[3], full1[3]), ((full0[1], full1[1]), (full0[2], full1[2])), (grad_hidden,))
-        g_query_sum = own_sum[0] + tie(arrived, g_up)[0]
+        whole = lambda shape: block(shape, lambda b: (0,) * len(shape))
+        g_key, g_value, g_mlp_norm, g_attn_norm = run(
+            split_kernel, (1,), [whole((dim + extra, 2 * hd))], [whole((dim, hd))] * 2 + [whole((1, dim))] * 2,
+            [sds((dim, hd), F32)] * 2 + [sds((1, dim), F32)] * 2, (gkv,), nbytes=16 * dim * hd)
+        g_mlp_norm, g_attn_norm = g_mlp_norm.reshape(dim), g_attn_norm.reshape(dim)
+
+        g_gate, g_up = weight_grads((full0[3], full1[3]), ((full0[1], full1[1]), (full0[2], full1[2])), (grad_hidden,), by=512)
         return (hidden_out, grad_hidden, g_attn_norm, g_query_sum, g_key, g_value, g_out_sum, g_mlp_norm, g_gate, g_up, g_down)
 
     return jax.shard_map(local_layer, mesh=mesh, in_specs=in_specs, out_specs=out_specs, check_vma=False)

time: 1680 us -> 1710 us (1.018)
  waiting for transfers between devices: 295 us -> 358 us
    reduce_scatter x1, waiting for transfers between devices: 33.3 us -> 95.8 us  [local_layer(): lax.psum_scatter(g_out.reshape(qd, dim), 'tp', scatter_dimension=0, tiled...]
    ppermute x8 -> x7, waiting for transfers between devices: 250 us -> 250 us  [to_chip(): return lax.ppermute(x, 'tp', chip_flip)]
  transfers between devices with their start and end apart: 29 -> 28, of which waited for: 7 -> 7; matrix products, arithmetic and copies ran while one was open for 5% -> 4% of each run, Pallas kernels for 65% -> 63%
where the time goes in v4:
time: 1710 us
  Pallas kernels  1200 us (70%)
  waiting for transfers between devices  358 us (21%)
  matrix products  123 us (7%)
    pallas_call x21, Pallas kernels, run(): pl.pallas_call(kernel, grid_spec=spec, out_shape=out_shape, input_output_...  1200 us
    ppermute x7, waiting for transfers between devices, to_chip(): return lax.ppermute(x, 'tp', chip_flip)  250 us
    dot_general x2, matrix products, dot_nn(): lax.dot_general(a, b, (((1,), (0,)), ((), ())), preferred_element_type=F32)  123 us
    reduce_scatter x1, waiting for transfers between devices, local_layer(): lax.psum_scatter(g_out.reshape(qd, dim), 'tp', scatter_dimension=0, tiled...  95.8 us
  transfers between devices with their start and end apart: 28, of which 7 were waited for; matrix products, arithmetic and copies ran while one was open for 4% of the time, Pallas kernels for 63%

profile of v4, /device:TPU:0, one launch (start us, length us, event | category | flops | bytes accessed | tf_op | source)
XLA Modules:
  0.0 1708.5 jit_solution(806783158656613930)
XLA Ops:
  7.2 0.9 collective-permute-start.5
  8.1 1.3 convert_add_fusion.1
  9.4 8.2 shard_map.230
  17.6 2.5 collective-permute-start.4
  20.6 32.5 %shard_map.231 = (bf16[2,768,4096]{2,1,0:T(8,128)(2,1)}, bf16[2,2,3,256,2048]{4,3,2,1,0:T(8,128)(2,1)}, bf16[2,2,3,256,2048]{4,3,2,1,0:T(8,128)(2,1)}, bf16[3,25...) custom-call(s32[1]{0:T(128)} %bitcast.me_ref.refs_0_, bf16[6,256,2048]{2,1,0:T(8,128)(2,1)} %go_ref.1, ...), custom_call_target="tpu_custom_call" | custom-call | flops 25769803776 | bytes 29360128 | tf_op jit(solution)/shard_map/pallas_call | solution.py:39
  53.1 47.3 %collective-permute-done.1.x_ref = bf16[2048,512]{1,0:T(8,128)(2,1)} collective-permute-done((bf16[2048,512]{1,0:T(8,128)(2,1)}, bf16[2048,512]{1,0:T(8,128)(2,1)}, u32[]{:S(2)}, u32[]{:S(2)}) %collective-permute-start.1) | collective-permute-done | bytes 2097184 | tf_op jit(solution)/shard_map/ppermute | solution.py:597
  100.4 32.6 %shard_map.232 = (bf16[2,768,4096]{2,1,0:T(8,128)(2,1)}, bf16[2,2,3,256,2048]{4,3,2,1,0:T(8,128)(2,1)}, bf16[2,2,3,256,2048]{4,3,2,1,0:T(8,128)(2,1)}) custom-call(s32[1]{0:T(128)} %bitcast.me_ref.refs_0_, bf16[6,256,2048]{2,1,0:T(8,128)(2,1)} %collective-permute-done.5.refs_0_, ...), custom_call_target="tpu_custom_call", output_to_operand_aliasing={{1}: (3, {}), {2}: (4, {})} | custom-call | flops 25769803776 | bytes 29360128 | tf_op jit(solution)/shard_map/pallas_call | solution.py:39
  133.0 0.5 collective-permute-start.6
  133.5 1.8 collective-permute-start.8
  135.3 1.6 collective-permute-done.6.k3_ref
  136.9 44.9 %shard_map.233 = (bf16[6,256,2048]{2,1,0:T(8,128)(2,1)}, bf16[6,1024,2048]{2,1,0:T(8,128)(2,1)}, bf16[6,256,2048]{2,1,0:T(8,128)(2,1)}) custom-call(s32[1]{0:T(128)} %bitcast.me_ref.refs_0_, s32[6]{0:T(128)} %pre_ref.1, s32[6]{0:T(128)} %val_ref.1, bf16[6,256,2048]{2,1,0:T(8,128)(2,1)} %get-tuple-element.60.u_ref, bf16[2048,512]{1,0:T(8,128)(2,1)} %w0_ref.9, ...), custom_call_target="tpu_custom_call" | custom-call | flops 25769803776 | bytes 25165824 | tf_op jit(solution)/shard_map/pallas_call | solution.py:39
  181.9 0.4 collective-permute-start.9
  182.5 0.6 convert_add_fusion
  183.1 3.3 collective-permute-done.9.w3_ref
  186.4 14.3 shard_map.234
  200.7 0.4 collective-permute-start.12
  201.1 1.8 collective-permute-start.14
  203.1 14.3 shard_map.235
  217.5 64.3 %shard_map.236 = (bf16[2,2,768,4096]{3,2,1,0:T(8,128)(2,1)}, bf16[2,2,768,4096]{3,2,1,0:T(8,128)(2,1)}, bf16[2,2,768,4096]{3,2,1,0:T(8,128)(2,1)}, bf16[2,2,3,256,2048]{4,3,2,1,0:T(8,128)(2,1)}) custom-call(s32[1]{0:T(128)} %bitcast.me_ref.refs_0_, bf16[3,256,2048]{2,1,0:T(8,128)(2,1)} %get-tuple-element.67.refs_0_, ...), custom_call_target="tpu_custom_call" | custom-call | flops 51539607552 | bytes 83886080 | tf_op jit(solution)/shard_map/pallas_call | solution.py:39
  281.8 0.5 collective-permute-start.15
  282.3 63.8 %shard_map.237 = (bf16[2,2,768,4096]{3,2,1,0:T(8,128)(2,1)}, bf16[2,2,768,4096]{3,2,1,0:T(8,128)(2,1)}, bf16[2,2,768,4096]{3,2,1,0:T(8,128)(2,1)}, bf16[2,2,3,256,2048]{4,3,2,1,0:T(8,128)(2,1)}) custom-call(s32[1]{0:T(128)} %bitcast.me_ref.refs_0_, bf16[3,256,2048]{2,1,0:T(8,128)(2,1)} %get-tuple-element.69.refs_6_.refs_0_.rest_0_, ...), custom_call_target="tpu_custom_call" | custom-call | flops 51539607552 | bytes 83886080 | tf_op jit(solution)/shard_map/pallas_call | solution.py:39
  346.3 32.5 %shard_map.238 = (bf16[2,768,4096]{2,1,0:T(8,128)(2,1)}, bf16[2,2,3,256,2048]{4,3,2,1,0:T(8,128)(2,1)}) custom-call(s32[1]{0:T(128)} %bitcast.me_ref.refs_0_, bf16[3,256,2048]{2,1,0:T(8,128)(2,1)} %tie.14.refs_0_, bf16[3,256,2048]{2,1,0:T(8,128)(2,1)} %collective-permute-done.15.refs_1_, ...), custom_call_target="tpu_custom_call", output_to_operand_aliasing={{1}: (4, {})} | custom-call | flops 25769803776 | bytes 29360128 | tf_op jit(solution)/shard_map/pallas_call | solution.py:39
  378.8 63.9 %shard_map.239 = (bf16[2,2,768,4096]{3,2,1,0:T(8,128)(2,1)}, bf16[2,2,768,4096]{3,2,1,0:T(8,128)(2,1)}, bf16[2,2,768,4096]{3,2,1,0:T(8,128)(2,1)}, bf16[2,2,3,256,2048]{4,3,2,1,0:T(8,128)(2,1)}) custom-call(s32[1]{0:T(128)} %bitcast.me_ref.refs_0_, ...), custom_call_target="tpu_custom_call", output_to_operand_aliasing={{0}: (7, {}), {1}: (8, {}), {2}: (9, {}), {3}: (10, {})} | custom-call | flops 51539607552 | bytes 83886080 | tf_op jit(solution)/shard_map/pallas_call | solution.py:39
  442.7 60.3 %convolution_convert_fusion.1.refs_13_ = bf16[3072,2048]{1,0:T(8,128)(2,1)} fusion(bf16[3072,4096]{1,0:T(8,128)(2,1)} %bitcast.33, bf16[4096,2048]{1,0:T(8,128)(2,1)} %refs_6_.1), kind=kOutput, calls=%fused_computation.1 | convolution fusion | flops 51545899008 | bytes 54525952 | tf_op jit(solution)/shard_map/dot_general | solution.py:21
  503.0 118.8 %shard_map.240.refs_12_ = bf16[4,768,2048]{2,1,0:T(8,128)(2,1)} custom-call(bf16[2,2,768,4096]{3,2,1,0:T(8,128)(2,1)} %get-tuple-element.78.dg_ref, bf16[2,2,768,4096]{3,2,1,0:T(8,128)(2,1)} %get-tuple-element.79.du_ref, bf16[2048,4096]{1,0:T(8,128)(2,1)} %wg_ref.3, bf16[2048,4096]{1,0:T(8,128)(2,1)} %wu_ref.3, ...), custom_call_target="tpu_custom_call" | custom-call | flops 103079215104 | bytes 50331648 | tf_op jit(solution)/shard_map/pallas_call | solution.py:39
  621.9 1.0 collective-permute-start.18
  622.9 0.8 copy-done
  623.7 1.0 collective-permute-start.16
  624.7 113.2 %collective-permute-done.18.x_ref = bf16[3,256,2048]{2,1,0:T(8,128)(2,1)} collective-permute-done((bf16[3,256,2048]{2,1,0:T(8,128)(2,1)}, bf16[3,256,2048]{2,1,0:T(8,128)(2,1)}, u32[]{:S(2)}, u32[]{:S(2)}) %collective-permute-start.18) | collective-permute-done | bytes 3145760 | tf_op jit(solution)/shard_map/ppermute | solution.py:597
  737.9 0.3 collective-permute-start.19
  738.1 89.6 %collective-permute-done.16.x_ref = bf16[3,256,2048]{2,1,0:T(8,128)(2,1)} collective-permute-done((bf16[3,256,2048]{2,1,0:T(8,128)(2,1)S(1)}, bf16[3,256,2048]{2,1,0:T(8,128)(2,1)}, u32[]{:S(2)}, u32[]{:S(2)}) %collective-permute-start.16) | collective-permute-done | bytes 3145760 | tf_op jit(solution)/shard_map/ppermute | solution.py:597
  827.8 6.0 collective-permute-done.17.refs_1_
  833.8 93.0 %shard_map.241 = (bf16[2,2,768,4096]{3,2,1,0:T(8,128)(2,1)}, bf16[2,2,768,4096]{3,2,1,0:T(8,128)(2,1)}, bf16[2,2,768,4096]{3,2,1,0:T(8,128)(2,1)}, bf16[2,2,3,25...) custom-call(s32[1]{0:T(128)} %bitcast.me_ref.refs_0_, ...), custom_call_target="tpu_custom_call", output_to_operand_aliasing={{0}: (8, {}), {1}: (9, {}), {2}: (10, {}), {3}: (11, {}), {... | custom-call | flops 77309411328 | bytes 83886080 | tf_op jit(solution)/shard_map/pallas_call | solution.py:39
  926.8 115.2 %shard_map.242 = bf16[4,768,2048]{2,1,0:T(8,128)(2,1)} custom-call(bf16[2,2,768,4096]{3,2,1,0:T(8,128)(2,1)} %get-tuple-element.86.dg_ref, bf16[2,2,768,4096]{3,2,1,0:T(8,128)(2,1)} %get-tuple-element.87.du_ref, bf16[2048,4096]{1,0:T(8,128)(2,1)} %wg_ref.3, bf16[2048,4096]{1,0:T(8,128)(2,1)} %wu_ref.3, bf16[2,2,768,4096]{3,2,1,0:T(8,128)(2,1)} %get-tuple-element.88.rest_0_), custom_call_target="tpu_custom_call" | custom-call | flops 103079215104 | bytes 50331648 | tf_op jit(solution)/shard_map/pallas_call | solution.py:39
  1042.1 62.5 %convolution_convert_fusion.refs_4_.token0_ref = bf16[3072,2048]{1,0:T(8,128)(2,1)} fusion(bf16[3072,4096]{1,0:T(8,128)(2,1)} %bitcast.36, bf16[4096,2048]{1,0:T(8,128)(2,1)} %refs_6_.1), kind=kOutput, calls=%fused_computation | convolution fusion | flops 51545899008 | bytes 54525952 | tf_op jit(solution)/shard_map/dot_general | solution.py:21
  1104.7 0.3 reduce-scatter.28.cloned.1.call-start
  1105.0 35.7 %shard_map.243.token1_ref.refs_4_ = f32[4096,2048]{1,0:T(8,128)} custom-call(bf16[3072,4096]{1,0:T(8,128)(2,1)} %bitcast.34, bf16[3072,4096]{1,0:T(8,128)(2,1)} %bitcast.37, bf16[3072,2048]{1,0:T(8,128)(2,1)} %bitcast.43, bf16[3072,2048]{1,0:T(8,128)(2,1)} %bitcast.45, bf16[3072,2048]{1,0:T(8,128)(2,1)} %convolution_convert_fusion.refs_4_.token0_ref), custom_call_target="tpu_custom_call" | custom-call | flops 25769803776 | bytes 33554432 | tf_op jit(solution)/shard_map/pallas_call | solution.py:39
  1140.8 65.7 %shard_map.244 = (bf16[6,256,2048]{2,1,0:T(8,128)(2,1)}, bf16[6,256,2048]{2,1,0:T(8,128)(2,1)}, bf16[4,6,256,512]{3,2,1,0:T(8,128)(2,1)}, f32[1,2048]{1,0:T(1,128)}) custom-call(s32[1]{0:T(128)} %bitcast.me_ref.refs_0_, bf16[3,256,2048]{2,1,0:T(8,128)(2,1)} %bitcast.60, bf16[3,256,2048]{2,1,0:T(8,128)(2,1)} %bitcast.61, ...), custom_call_target="tpu_custom_call" | custom-call | flops 38654705664 | bytes 25165824 | tf_op jit(solution)/shard_map/pallas_call | solution.py:39
  1206.5 19.5 %shard_map.245.refs_3_ = f32[4,512,2048]{2,1,0:T(8,128)} custom-call(s32[1]{0:T(128)} %bitcast.me_ref.refs_0_, bf16[1536,2048]{1,0:T(8,128)(2,1)} %bitcast.39, bf16[1536,2048]{1,0:T(8,128)(2,1)} %bitcast.49, bf16[4,6,256,512]{3,2,1,0:T(8,128)(2,1)} %get-tuple-element.94.refs_3_), custom_call_target="tpu_custom_call" | custom-call | flops 12884901888 | bytes 16777216 | tf_op jit(solution)/shard_map/pallas_call | solution.py:39
  1226.0 19.3 %shard_map.246.refs_5_ = f32[4,2048,512]{2,1,0:T(8,128)} custom-call(s32[1]{0:T(128)} %bitcast.me_ref.refs_0_, bf16[1536,2048]{1,0:T(8,128)(2,1)} %bitcast.48, bf16[1536,2048]{1,0:T(8,128)(2,1)} %bitcast.50, f32[4,512,2048]{2,1,0:T(8,128)} %shard_map.245.refs_3_), custom_call_target="tpu_custom_call" | custom-call | flops 12884901888 | bytes 16777216 | tf_op jit(solution)/shard_map/pallas_call | solution.py:39
  1245.2 89.2 %shard_map.247.token0_ref = f32[4096,2048]{1,0:T(8,128)} custom-call(bf16[3072,4096]{1,0:T(8,128)(2,1)} %bitcast.35, bf16[3072,4096]{1,0:T(8,128)(2,1)} %bitcast.38, bf16[3072,2048]{1,0:T(8,128)(2,1)} %bitcast.44, bf16[3072,2048]{1,0:T(8,128)(2,1)} %bitcast.46, f32[4096,2048]{1,0:T(8,128)} %shard_map.243.token1_ref.refs_4_, ...), custom_call_target="tpu_custom_call", output_to_operand_aliasing={{}: (4, {})} | custom-call | flops 77309411328 | bytes 33554432 | tf_op jit(solution)/shard_map/pallas_call | solution.py:39
  1334.5 42.0 %shard_map.248 = (bf16[6,256,2048]{2,1,0:T(8,128)(2,1)}, f32[2056,512]{1,0:T(8,128)}, bf16[6,256,2048]{2,1,0:T(8,128)(2,1)}) custom-call(s32[1]{0:T(128)} %bitcast.me_ref.refs_0_, bf16[6,256,512]{2,1,0:T(8,128)(2,1)} %bitcast.54, bf16[6,256,2048]{2,1,0:T(8,128)(2,1)} %get-tuple-element.95.dq_ref, bf16[6,256,2048]{2,1,0:T(8,128)(2,1)} %get-tuple-element.60.u_ref, ...), custom_call_target="tpu_custom_call" | custom-call | flops 19327352832 | bytes 25165824 | tf_op jit(solution)/shard_map/pallas_call | solution.py:39
  1376.5 0.7 reduce-scatter.18.cloned.1.call-update
  1377.2 0.3 reduce-scatter.20.cloned.1.call-start
  1377.5 0.4 reduce-scatter.20.cloned.1.call-update
  1378.0 222.6 %shard_map.250 = (f32[2048,4096]{1,0:T(8,128)}, f32[2048,4096]{1,0:T(8,128)}) custom-call(bf16[3072,2048]{1,0:T(8,128)(2,1)} %bitcast.69, bf16[3072,2048]{1,0:T(8,128)(2,1)} %bitcast.68, bf16[3072,4096]{1,0:T(8,128)(2,1)} %bitcast.66, bf16[3072,4096]{1,0:T(8,128)(2,1)} %bitcast.64, bf16[3072,4096]{1,0:T(8,128)(2,1)} %bitcast.67, ...), custom_call_target="tpu_custom_call" | custom-call | flops 206158430208 | bytes 33554432 | tf_op jit(solution)/shard_map/pallas_call | solution.py:39
  1600.6 4.8 shard_map.249
  1605.4 95.8 %reduce-scatter.20.cloned.1.call-done = f32[512,2048]{1,0:T(8,128)} async-done(((f32[2048,2048]{1,0:T(8,128)}), f32[512,2048]{1,0:T(8,128)}) %reduce-scatter.20.cloned.1.call-update) | async-done | bytes 4194320 | tf_op jit(solution)/shard_map/reduce_scatter | solution.py:798
  (54 shorter events, 1.7 us)
Async XLA Ops:
  7.2 1133.5 %reduce-scatter.26.cloned.1.call-start = ((), (), s32[]{:S(2)}) async-start(), calls=%async_computation.12 | async-start | bytes 15728640
  7.2 93.2 %collective-permute-start.5 = (bf16[6,256,2048]{2,1,0:T(8,128)(2,1)}, bf16[6,256,2048]{2,1,0:T(8,128)(2,1)}, u32[]{:S(2)}, u32[]{:S(2)}) collective-permute-start(bf16[6,256,2048]{2,1,0:T(8,128)(2,1)} %go_ref.1), channel_id=1, source_target_pairs={{0,1},{1,0},{2,3},{3,2},{4,5},{5,4},{6,7},{7,6}} | collective-permute-start | bytes 18874376 | tf_op jit(solution)/shard_map/ppermute | solution.py:594
  17.6 115.4 %collective-permute-start.4 = (bf16[6,256,512]{2,1,0:T(8,128)(2,1)}, bf16[6,256,512]{2,1,0:T(8,128)(2,1)}, u32[]{:S(2)}, u32[]{:S(2)}) collective-permute-start(bf16[6,256,512]{2,1,0:T(8,128)(2,1)} %get-tuple-element.61.refs_2_.k0_ref), channel_id=1, source_target_pairs={{0,2},{2,0},{1,3},{3,1},{4,6},{6,4},{5,7},{7,5}} | collective-permute-start | bytes 4718600 | tf_op jit(solution)/shard_map/ppermute | solution.py:597
  20.1 115.2 %collective-permute-start.3 = (bf16[6,256,512]{2,1,0:T(8,128)(2,1)}, bf16[6,256,512]{2,1,0:T(8,128)(2,1)}, u32[]{:S(2)}, u32[]{:S(2)}) collective-permute-start(bf16[6,256,512]{2,1,0:T(8,128)(2,1)} %get-tuple-element.61.refs_2_.k0_ref), channel_id=1, source_target_pairs={{0,1},{1,0},{2,3},{3,2},{4,5},{5,4},{6,7},{7,6}} | collective-permute-start | bytes 4718600 | tf_op jit(solution)/shard_map/ppermute | solution.py:594
  20.3 80.1 %collective-permute-start.1 = (bf16[2048,512]{1,0:T(8,128)(2,1)}, bf16[2048,512]{1,0:T(8,128)(2,1)}, u32[]{:S(2)}, u32[]{:S(2)}) collective-permute-start(bf16[2048,512]{1,0:T(8,128)(2,1)} %w0_ref.9), channel_id=1, source_target_pairs={{0,2},{2,0},{1,3},{3,1},{4,6},{6,4},{5,7},{7,5}} | collective-permute-start | bytes 6291464 | tf_op jit(solution)/shard_map/ppermute | solution.py:597
  20.6 114.7 %collective-permute-start = (bf16[2048,512]{1,0:T(8,128)(2,1)}, bf16[2048,512]{1,0:T(8,128)(2,1)}, u32[]{:S(2)}, u32[]{:S(2)}) collective-permute-start(bf16[2048,512]{1,0:T(8,128)(2,1)} %w0_ref.9), channel_id=1, source_target_pairs={{0,1},{1,0},{2,3},{3,2},{4,5},{5,4},{6,7},{7,6}} | collective-permute-start | bytes 6291464 | tf_op jit(solution)/shard_map/ppermute | solution.py:594
  100.4 34.9 %collective-permute-start.2 = (bf16[2048,512]{1,0:T(8,128)(2,1)}, bf16[2048,512]{1,0:T(8,128)(2,1)}, u32[]{:S(2)}, u32[]{:S(2)}) collective-permute-start(bf16[2048,512]{1,0:T(8,128)(2,1)} %tie.9.w2_ref), channel_id=1, source_target_pairs={{0,1},{1,0},{2,3},{3,2},{4,5},{5,4},{6,7},{7,6}} | collective-permute-start | bytes 6291464 | tf_op jit(solution)/shard_map/ppermute | solution.py:594
  133.0 3.9 collective-permute-start.6
  133.5 48.3 %collective-permute-start.8 = (bf16[512,2048]{1,0:T(8,128)(2,1)}, bf16[512,2048]{1,0:T(8,128)(2,1)}, u32[]{:S(2)}, u32[]{:S(2)}) collective-permute-start(bf16[512,2048]{1,0:T(8,128)(2,1)} %w0_ref.8), channel_id=1, source_target_pairs={{0,2},{2,0},{1,3},{3,1},{4,6},{6,4},{5,7},{7,5}} | collective-permute-start | bytes 6291464 | tf_op jit(solution)/shard_map/ppermute | solution.py:597
  135.3 47.9 %collective-permute-start.7 = (bf16[512,2048]{1,0:T(8,128)(2,1)}, bf16[512,2048]{1,0:T(8,128)(2,1)}, u32[]{:S(2)}, u32[]{:S(2)}) collective-permute-start(bf16[512,2048]{1,0:T(8,128)(2,1)} %w0_ref.8), channel_id=1, source_target_pairs={{0,1},{1,0},{2,3},{3,2},{4,5},{5,4},{6,7},{7,6}} | collective-permute-start | bytes 6291464 | tf_op jit(solution)/shard_map/ppermute | solution.py:594
  181.8 0.7 copy-start.1
  181.9 4.5 collective-permute-start.9
  200.7 16.8 collective-permute-start.12
  201.1 80.7 %collective-permute-start.14 = (bf16[3,256,2048]{2,1,0:T(8,128)(2,1)}, bf16[3,256,2048]{2,1,0:T(8,128)(2,1)}, u32[]{:S(2)}, u32[]{:S(2)}) collective-permute-start(bf16[3,256,2048]{2,1,0:T(8,128)(2,1)} %tie.13), channel_id=1, source_target_pairs={{0,2},{2,0},{1,3},{3,1},{4,6},{6,4},{5,7},{7,5}} | collective-permute-start | bytes 9437192 | tf_op jit(solution)/shard_map/ppermute | solution.py:597
  202.8 143.3 %collective-permute-start.10 = (bf16[3,256,2048]{2,1,0:T(8,128)(2,1)}, bf16[3,256,2048]{2,1,0:T(8,128)(2,1)}, u32[]{:S(2)}, u32[]{:S(2)}) collective-permute-start(bf16[3,256,2048]{2,1,0:T(8,128)(2,1)} %get-tuple-element.67.refs_0_), channel_id=1, source_target_pairs={{0,2},{2,0},{1,3},{3,1},{4,6},{6,4},{5,7},{7,5}} | collective-permute-start | bytes 9437192 | tf_op jit(solution)/shard_map/ppermute | solution.py:597
  217.4 64.9 %collective-permute-start.11 = (bf16[3,256,2048]{2,1,0:T(8,128)(2,1)}, bf16[3,256,2048]{2,1,0:T(8,128)(2,1)}, u32[]{:S(2)}, u32[]{:S(2)}) collective-permute-start(bf16[3,256,2048]{2,1,0:T(8,128)(2,1)} %get-tuple-element.69.refs_6_.refs_0_.rest_0_), channel_id=1, source_target_pairs={{0,1},{1,0},{2,3},{3,2},{4,5},{5,4},{6,7},{7,6}} | collective-permute-start | bytes 9437192 | tf_op jit(solution)/shard_map/ppermute | solution.py:594
  281.8 64.5 %collective-permute-start.15 = (bf16[3,256,2048]{2,1,0:T(8,128)(2,1)}, bf16[3,256,2048]{2,1,0:T(8,128)(2,1)}, u32[]{:S(2)}, u32[]{:S(2)}) collective-permute-start(bf16[3,256,2048]{2,1,0:T(8,128)(2,1)} %tie.14.refs_0_), channel_id=1, source_target_pairs={{0,1},{1,0},{2,3},{3,2},{4,5},{5,4},{6,7},{7,6}} | collective-permute-start | bytes 9437192 | tf_op jit(solution)/shard_map/ppermute | solution.py:594
  346.2 32.6 %collective-permute-start.13 = (bf16[3,256,2048]{2,1,0:T(8,128)(2,1)}, bf16[3,256,2048]{2,1,0:T(8,128)(2,1)}, u32[]{:S(2)}, u32[]{:S(2)}) collective-permute-start(bf16[3,256,2048]{2,1,0:T(8,128)(2,1)} %tie.12.refs_0_), channel_id=1, source_target_pairs={{0,1},{1,0},{2,3},{3,2},{4,5},{5,4},{6,7},{7,6}} | collective-permute-start | bytes 9437192 | tf_op jit(solution)/shard_map/ppermute | solution.py:594
  503.0 637.8 %reduce-scatter.22.cloned.1.call-start = ((), (), s32[]{:S(2)}) async-start(), calls=%async_computation.10 | async-start | bytes 15728640
  621.8 1.9 copy-start
  621.8 518.9 %reduce-scatter.24.cloned.1.call-start = ((), (), s32[]{:S(2)}) async-start(), calls=%async_computation.11 | async-start | bytes 15728640
  621.9 115.9 %collective-permute-start.18 = (bf16[3,256,2048]{2,1,0:T(8,128)(2,1)}, bf16[3,256,2048]{2,1,0:T(8,128)(2,1)}, u32[]{:S(2)}, u32[]{:S(2)}) collective-permute-start(bf16[3,256,2048]{2,1,0:T(8,128)(2,1)} %tie.16), channel_id=1, source_target_pairs={{0,2},{2,0},{1,3},{3,1},{4,6},{6,4},{5,7},{7,5}} | collective-permute-start | bytes 9437192 | tf_op jit(solution)/shard_map/ppermute | solution.py:597
  623.7 204.1 %collective-permute-start.16 = (bf16[3,256,2048]{2,1,0:T(8,128)(2,1)S(1)}, bf16[3,256,2048]{2,1,0:T(8,128)(2,1)}, u32[]{:S(2)}, u32[]{:S(2)}) collective-permute-start(bf16[3,256,2048]{2,1,0:T(8,128)(2,1)S(1)} %copy-done), channel_id=1, source_target_pairs={{0,2},{2,0},{1,3},{3,1},{4,6},{6,4},{5,7},{7,5}} | collective-permute-start | bytes 9437192 | tf_op jit(solution)/shard_map/ppermute | solution.py:597
  737.9 89.9 %collective-permute-start.19 = (bf16[3,256,2048]{2,1,0:T(8,128)(2,1)}, bf16[3,256,2048]{2,1,0:T(8,128)(2,1)}, u32[]{:S(2)}, u32[]{:S(2)}) collective-permute-start(bf16[3,256,2048]{2,1,0:T(8,128)(2,1)} %tie.17.refs_2_), channel_id=1, source_target_pairs={{0,1},{1,0},{2,3},{3,2},{4,5},{5,4},{6,7},{7,6}} | collective-permute-start | bytes 9437192 | tf_op jit(solution)/shard_map/ppermute | solution.py:594
  827.8 6.0 collective-permute-start.17
  1042.1 292.4 %reduce-scatter.30.cloned.1.call-start = ((), (), s32[]{:S(2)}) async-start(), calls=%async_computation.14 | async-start | bytes 15728640
  1104.7 229.8 %reduce-scatter.28.cloned.1.call-start = ((), (), s32[]{:S(2)}) async-start(), calls=%async_computation.13 | async-start | bytes 7864320
  1206.5 394.2 %all-reduce.7.cloned.1.call-start = ((), (), s32[]{:S(2)}) async-start(), calls=%async_computation.7 | async-start | bytes 8421376 | tf_op jit(solution)/shard_map/psum | solution.py:817
  1376.5 228.9 %reduce-scatter.18.cloned.1.call-start = ((), (), s32[]{:S(2)}) async-start(), calls=%async_computation.8 | async-start | bytes 20971520 | tf_op jit(solution)/shard_map/reduce_scatter | solution.py:803
  1377.2 324.0 %reduce-scatter.20.cloned.1.call-start = ((), (), s32[]{:S(2)}) async-start(), calls=%async_computation.9 | async-start | bytes 20971520 | tf_op jit(solution)/shard_map/reduce_scatter | solution.py:798
Sparse Core Ops, SparseCore 0:
  503.1 95.5 reduce-scatter.25
  622.0 163.1 reduce-scatter.21
  1042.2 94.1 reduce-scatter.23
  1138.8 94.0 reduce-scatter.29
  1235.2 53.2 reduce-scatter.27
  1376.6 79.2 all-reduce.6
  1459.0 119.5 reduce-scatter.17
  1581.7 119.4 reduce-scatter.19

commit v5 on v4

--- a/solution.py
+++ b/solution.py
@@ -185,7 +185,7 @@
 
 
 def span(t, n):
-    return pl.ds(pl.multiple_of(t * n, n), n)
+    return pl.ds(t * n if isinstance(t, int) else pl.multiple_of(t * n, n), n)
 
 
 OWN, MATE, FAR = 0, 1, 2
@@ -393,14 +393,13 @@
 
 
 def last_kernel(me_ref, dkv_ref, dq_ref, u_ref, h_ref, dres_ref, gain_ref, w0_ref, w1_ref, w2_ref, w3_ref, wk_ref, wv_ref, cos_ref, sin_ref, gm_ref,
-                res_ref, p0_ref, p1_ref, token0_ref, gh_ref, gkv_ref, ho_ref, acc_ref, w_ref, d_ref, sems):
+                token0_ref, gh_ref, gkv_ref, acc_ref, w_ref, d_ref, sems):
     b = pl.program_id(0)
     dim, hd = wk_ref.shape
     qd = dq_ref.shape[2]
     fetch = (w0_ref, w1_ref, w2_ref, w3_ref, wk_ref, wv_ref), w_ref, 1, sems
     start_first(*fetch)
-    half = pl.num_programs(0) // 2
-    ho_ref[0] = (res_ref[0].astype(F32) + jnp.where(b < half, p0_ref[0], p1_ref[0]).astype(F32)).astype(BF)
+    wait_first(*fetch)
     raw = dkv_ref[0]
     dk = raw[:, :hd].astype(F32)
     first, second = rope_bwd(dk[:, : hd // 2], dk[:, hd // 2 :], cos_ref[...], sin_ref[...])
@@ -409,7 +408,6 @@
     d_ref[:, qd + hd // 2 : qd + hd] = second.astype(BF)
     d_ref[:, qd + hd :] = raw[:, hd:]
     gk = dot_tn(u_ref[0], d_ref[:, qd:])
-    wait_first(*fetch)
     dn = dot_nt(d_ref[...], w_ref[...])
     x = h_ref[0].astype(F32)
     inv = lax.rsqrt(jnp.mean(x * x, axis=-1, keepdims=True) + EPS)
@@ -495,8 +493,52 @@
         o_flow.wait(t, t % 2)
 
 
-def weight_grads_kernel(count, first, ni, *refs):
+def mlp_out_kernel(mine, me_ref, act_ref, wd_ref, *refs):
+    outs, (ab, wb, ob, pb, a_sem, w_sem, o_sem, p_sem) = refs[-9 - mine : -8], refs[-8:]
+    chip, core = me_ref[0] // 2, me_ref[0] % 2
+    core = core if mine else 1 - core
+    bn = wb.shape[2]
+    nj = wd_ref.shape[1] // bn
+    a_flow = Flow((ab,), a_sem, True, lambda i: (act_ref.at[abs(1 - i - chip), core],))
+    w_flow = Flow((wb,), w_sem, True, lambda t: (wd_ref.at[:, span(t % nj, bn)],))
+    p_flow = Flow((pb,), p_sem, True, lambda t: (refs[0].at[1 - t // nj, :, span(t % nj, bn)],))
+    if mine:
+        o_flow = Flow((ob,), o_sem, False, lambda t: (outs[t // nj].at[:, span(t % nj, bn)],))
+    else:
+        o_flow = Flow((ob,), o_sem, False, lambda t: (outs[0].at[1 - t // nj, :, span(t % nj, bn)],))
+    steps = 2 * nj
+    for i in range(2):
+        a_flow.start(i, i)
+        w_flow.start(i, i)
+        if mine:
+            p_flow.start(i, i)
+    for t in range(steps):
+        slot = t % 2
+        if t % nj == 0:
+            a_flow.wait(t // nj, t // nj)
+        w_flow.wait(t, slot)
+        if t >= 2:
+            o_flow.wait(t - 2, slot)
+        out = dot_nn(ab[t // nj], wb[slot])
+        if mine:
+            p_flow.wait(t, slot)
+            out = out + pb[slot].astype(F32)
+        ob[slot] = out.astype(BF)
+        o_flow.start(t, slot)
+        if t + 2 < steps:
+            w_flow.start(t + 2, slot)
+            if mine:
+                p_flow.start(t + 2, slot)
+    for t in (steps - 2, steps - 1):
+        o_flow.wait(t, t % 2)
+
+
+def weight_grads_kernel(count, first, ni, side, *refs):
     x_refs, y_refs = refs[:2], refs[2 : 2 + 2 * count]
+    if side:
+        res_ref, p0_ref, p1_ref, q1_ref = refs[2 + 2 * count : 6 + 2 * count]
+        ho_ref, (rb, sb, tb, hb, s_sem, h_sem) = refs[-15], refs[-6:]
+        refs = refs[:-15] + refs[-14:-6]
     o_refs, (x0, x1, y0, y1, ob, x_sem, y_sem, o_sem) = refs[-8 - count : -8], refs[-8:]
     bm, bn = ob.shape[1:]
     nj = y_refs[0].shape[1] // bn
@@ -504,6 +546,23 @@
     per = count * nj
     rows = lambda i: pl.ds(pl.multiple_of((first + i) * bm, bm), bm)
     cols = lambda t: pl.ds(pl.multiple_of(lax.rem(t, nj) * bn, bn), bn)
+    if side:
+        n = rb.shape[1]
+        turn = p0_ref.shape[0] // n
+        at = lambda t: pl.ds(pl.multiple_of(t * n, n), n)
+        later = lambda t: at(jnp.maximum(t - turn, 0))
+        side_in = [Flow((rb, sb, tb), s_sem, True, lambda t: (res_ref.at[at(t)], p0_ref.at[at(jnp.minimum(t, turn - 1))], q1_ref.at[later(t)])),
+                   Flow((rb, sb, tb), s_sem, True, lambda t: (res_ref.at[at(t)], p1_ref.at[later(t)], q1_ref.at[later(t)]))]
+        side_out = Flow((hb,), h_sem, False, lambda t: (ho_ref.at[at(t)],))
+
+        def side_start(t, slot):
+            pl.when(t < turn)(lambda: side_in[0].start(t, slot))
+            pl.when(t >= turn)(lambda: side_in[1].start(t, slot))
+
+        def side_work(t, slot):
+            extra = tb[slot].astype(F32) * jnp.where(t < turn, 0.0, 1.0)
+            hb[slot] = (rb[slot].astype(F32) + sb[slot].astype(F32) + extra).astype(BF)
+
     x_flow = Flow((x0, x1), x_sem, True, lambda i: [r.at[:, rows(i)] for r in x_refs])
     y_flows = [Flow((y0, y1), y_sem, True, lambda t, k=k: [r.at[:, cols(t)] for r in y_refs[2 * k : 2 * k + 2]]) for k in range(count)]
     o_flows = [Flow((ob,), o_sem, False, lambda t, k=k: (o_refs[k].at[rows(t // per), cols(t)],)) for k in range(count)]
@@ -520,6 +579,12 @@
         x_flow.start(0, 0, k)
         y_flows[0].start(0, 0, k)
     y_flows[0].start(1, 1)
+    if side:
+        side_in[0].start(0, 0)
+        side_in[0].start(1, 1)
+        side_in[0].wait(0, 0)
+        side_work(0, 0)
+        side_out.start(0, 0)
     if ni > 1:
         x_flow.start(1, 1)
     for k in range(2):
@@ -538,6 +603,8 @@
         @pl.when(t + 1 < steps)
         def _():
             each(y_flows, t + 1, lambda f: f.start(t + 1, 1 - slot))
+            if side:
+                pl.when(t > 0)(lambda: side_start(t + 1, 1 - slot))
 
         @pl.when(lax.rem(t, per) == 0)
         def _():
@@ -550,13 +617,22 @@
         @pl.when(t >= 2)
         def _():
             o_flows[0].wait(t - 2, slot)
+            if side:
+                side_out.wait(t - 2, slot)
 
         y_flows[0].wait(t, slot)
+        if side:
+            side_in[0].wait(t, slot)
+            side_work(t, slot)
         ob[slot] = dot_tn(x0[x_slot], y0[slot]) + dot_tn(x1[x_slot], y1[slot])
+        if side:
+            side_out.start(t, slot)
         each(o_flows, t, lambda f: f.start(t, slot))
 
     for t in (steps - 2, steps - 1):
         o_flows[0].wait(t, t % 2)
+        if side:
+            side_out.wait(t, t % 2)
 
 
 def split_kernel(x_ref, k_ref, v_ref, m_ref, a_ref):
@@ -649,14 +725,14 @@
         bn = 512
         cat_shape = (2, 2, half, sl, dim)
         SMEM = pl.BlockSpec(memory_space=pltpu.SMEM)
-        pair = (2, rows, bn)
+        bd = 1024
 
         def dact(kind, gs, homes, tokens, n_out):
             return run(
                 functools.partial(dact_kernel, kind), (), [SMEM] + [ANY] * (len(gs) + 1 + len(homes) + len(tokens)), [ANY] * n_out,
                 ([sds((2, rows, ffn))] + [sds(cat_shape)] * 2 + [sds((half, sl, dim))] * 2)[: n_out],
                 (me, *gs, w_down, *homes, *tokens), aliases={2 + len(gs) + i: 1 + i for i in range(len(homes))},
-                scratch=[pltpu.VMEM((2, bn, dim), BF), pltpu.VMEM((2,) + pair, BF), pltpu.VMEM((batch, sl, dim), BF),
+                scratch=[pltpu.VMEM((2, bd, dim), BF), pltpu.VMEM((2, 2, rows, bd), BF), pltpu.VMEM((batch, sl, dim), BF),
                          pltpu.SemaphoreType.DMA((2, 1)), pltpu.SemaphoreType.DMA((2, 1)), dma(2), dma(4)],
                 flops=4 * rows * dim * ffn, nbytes=2 * ffn * dim + 4 * rows * ffn)
 
@@ -758,25 +834,40 @@
         gcat1 = full1[4]
         dz_part1 = gated_grad(full1)
         dz1 = scatter(dz_part1)
-        mlp_part1 = mlp_out(full1)
-        part1 = scatter(mlp_part1)
-
-        def weight_grads(x, ys, tokens, first=0, ni=None, prev=None, by=512):
+
+        def mlp_out_half(mine, adds, token):
+            bo = 1024
+            dims = [(rows, dim)] * 2 if mine else [(2, rows, dim)]
+            dma2 = pltpu.SemaphoreType.DMA((2, 1))
+            return run(
+                functools.partial(mlp_out_kernel, mine), (), [SMEM] + [ANY] * (3 + len(adds)), [ANY] * len(dims), [sds(d) for d in dims],
+                (me, full1[0], w_down, *adds, token),
+                scratch=[pltpu.VMEM((2, rows, ffn), BF), pltpu.VMEM((2, ffn, bo), BF), pltpu.VMEM((2, rows, bo), BF), pltpu.VMEM((2, rows, bo), BF), dma2, dma2, dma2, dma2],
+                flops=4 * rows * dim * ffn, nbytes=2 * ffn * dim)
+
+        mlp_mate, = mlp_out_half(False, (), dz_part1)
+        mlp_from_mate = to_core(mlp_mate)
+
+        def weight_grads(x, ys, tokens, first=0, ni=None, prev=None, by=512, side=()):
             flat = lambda pair: [a.reshape(4 * rows, -1) for a in pair]
             xs, yf = flat(x), [a for y in ys for a in flat(y)]
             m, n = xs[0].shape[1], yf[0].shape[1]
             bm = 1024
             extra = [prev] if prev is not None else []
             return run(
-                functools.partial(weight_grads_kernel, len(ys), first, ni or m // bm), (),
-                [ANY] * (2 + len(yf) + len(extra) + len(tokens)), [ANY] * len(ys), [sds((m, n), F32)] * len(ys),
-                (*xs, *yf, *extra, *tokens), aliases={2 + len(yf): 0} if extra else None,
+                functools.partial(weight_grads_kernel, len(ys), first, ni or m // bm, bool(side)), (),
+                [ANY] * (2 + len(yf) + len(side) + len(extra) + len(tokens)), [ANY] * (len(ys) + bool(side)),
+                [sds((m, n), F32)] * len(ys) + [sds(a.shape) for a in side[:1]],
+                (*xs, *yf, *side, *extra, *tokens), aliases={2 + len(yf): 0} if extra else None,
                 scratch=[pltpu.VMEM((2, 4 * rows, bm), BF)] * 2 + [pltpu.VMEM((2, 4 * rows, by), BF)] * 2 + [pltpu.VMEM((2, bm, by), F32)]
-                + [pltpu.SemaphoreType.DMA((2, 2))] * 2 + [pltpu.SemaphoreType.DMA((2, 1))],
+                + [pltpu.SemaphoreType.DMA((2, 2))] * 2 + [pltpu.SemaphoreType.DMA((2, 1))]
+                + ([pltpu.VMEM((2, own // (m // bm * len(ys) * n // by), dim), BF)] * 4 + [pltpu.SemaphoreType.DMA((2, 3)), pltpu.SemaphoreType.DMA((2, 1))] if side else []),
                 flops=16 * rows * (ni or m // bm) * bm * n * len(ys), nbytes=4 * m * n)
 
         down_args = (full0[0], full1[0]), ((gcat0, gcat1),)
-        g_down = weight_grads(*down_args, (mlp_part1,), 0, 1)[0]
+        g_down = weight_grads(*down_args, (mlp_mate,), 0, 1)[0]
+        mlp_far, mlp_own = mlp_out_half(True, (mlp_from_mate,), g_down)
+        mlp_arrived = to_chip(mlp_far)
 
         d_resid, d_q, dkv_part, gn2 = run(
             attn_bwd_kernel, (batch,),
@@ -784,7 +875,7 @@
              tok_spec, tok_spec, gain_spec] + wo_specs + [kv_spec] * 4 + [q_spec, pt_spec, rope_spec, rope_spec, ANY, ANY, ANY],
             [tok_spec, q_spec, kv4_spec, block((1, dim), lambda b, *_: (0, 0))],
             [sds((batch, sl, dim)), sds((batch, sl, qd)), sds((tp_n, batch, sl, 2 * hd)), sds((1, dim), F32)],
-            (me, dz0, dz1, resid, grad_out, gain2, *wos, *kvs, q, pt, cos_t, sin_t, mlp_part1, g_down, part0), prefetch=1,
+            (me, dz0, dz1, resid, grad_out, gain2, *wos, *kvs, q, pt, cos_t, sin_t, mlp_own, g_down, part0), prefetch=1,
             scratch=[pltpu.VMEM((hd, seq), BF), pltpu.VMEM((seq, hd), BF), pltpu.VMEM((heads * sl, hd), BF), pltpu.VMEM((heads * sl, hd), BF), pltpu.VMEM((seq, heads * sl), BF), pltpu.VMEM((2, seq, sl), F32)] + [pltpu.VMEM((seq, hd), F32)] * 2,
             flops=2 * own * dim * qd + 8 * own * seq * qd, nbytes=2 * own * heads * seq)
         dkv = lax.psum_scatter(dkv_part, "tp", scatter_dimension=0)
@@ -804,14 +895,12 @@
         g_down = weight_grads(*down_args, (g_query,), 1, ffn // 1024 - 1, g_down)[0]
 
         extra = dim // hd
-        half_at = [block((1, sl, dim), lambda b, *_: (jnp.minimum(b, half - 1), 0, 0)), block((1, sl, dim), lambda b, *_: (jnp.maximum(b - half, 0), 0, 0))]
-        grad_hidden, gkv, hidden_out = run(
+        grad_hidden, gkv = run(
             last_kernel, (batch,),
-            [kv_spec, q_spec, tok_spec, tok_spec, tok_spec, gain_spec,
-             ] + [ANY] * 6 + [rope_spec, rope_spec, const_spec((1, dim)), tok_spec, *half_at, ANY],
-            [tok_spec, block((dim + extra, 2 * hd), lambda b, *_: (0, 0)), tok_spec],
-            [sds((batch, sl, dim)), sds((dim + extra, 2 * hd), F32), sds((batch, sl, dim))],
-            (me, dkv, d_q, u, hidden, d_resid, gain1, *wqs, w_key, w_value, cos_t, sin_t, gn2, resid, part0, part1, g_down), prefetch=1,
+            [kv_spec, q_spec, tok_spec, tok_spec, tok_spec, gain_spec] + [ANY] * 6 + [rope_spec, rope_spec, const_spec((1, dim)), ANY],
+            [tok_spec, block((dim + extra, 2 * hd), lambda b, *_: (0, 0))],
+            [sds((batch, sl, dim)), sds((dim + extra, 2 * hd), F32)],
+            (me, dkv, d_q, u, hidden, d_resid, gain1, *wqs, w_key, w_value, cos_t, sin_t, gn2, g_down), prefetch=1,
             scratch=[pltpu.VMEM((1, dim), F32), pltpu.VMEM((dim, qd + 2 * hd), BF), pltpu.VMEM((sl, qd + 2 * hd), BF), dma(6)],
             flops=2 * own * dim * (qd + 4 * hd), nbytes=8 * own * dim)
         gkv = lax.psum(gkv, "tp")
@@ -821,7 +910,9 @@
             [sds((dim, hd), F32)] * 2 + [sds((1, dim), F32)] * 2, (gkv,), nbytes=16 * dim * hd)
         g_mlp_norm, g_attn_norm = g_mlp_norm.reshape(dim), g_attn_norm.reshape(dim)
 
-        g_gate, g_up = weight_grads((full0[3], full1[3]), ((full0[1], full1[1]), (full0[2], full1[2])), (grad_hidden,), by=512)
+        g_gate, g_up, hidden_out = weight_grads((full0[3], full1[3]), ((full0[1], full1[1]), (full0[2], full1[2])), (grad_hidden,),
+                                                side=(resid.reshape(own, dim), part0.reshape(rows, dim), mlp_own, mlp_arrived))
+        hidden_out = hidden_out.reshape(batch, sl, dim)
         return (hidden_out, grad_hidden, g_attn_norm, g_query_sum, g_key, g_value, g_out_sum, g_mlp_norm, g_gate, g_up, g_down)
 
     return jax.shard_map(local_layer, mesh=mesh, in_specs=in_specs, out_specs=out_specs, check_vma=False)

time: 1710 us -> 1740 us (1.018)
  Pallas kernels: 1200 us -> 1270 us
  matrix products: 123 us -> 60.1 us
    ppermute x7 -> x8, waiting for transfers between devices: 250 us -> 336 us  [to_chip(): return lax.ppermute(x, 'tp', chip_flip)]
    reduce_scatter x1, waiting for transfers between devices: 95.8 us -> 19.5 us  [local_layer(): lax.psum_scatter(g_out.reshape(qd, dim), 'tp', scatter_dimension=0, tiled...]
    pallas_call x21 -> x23, Pallas kernels: 1200 us -> 1270 us  [run(): pl.pallas_call(kernel, grid_spec=spec, out_shape=out_shape, input_output_...]
    dot_general x2 -> x1, matrix products: 123 us -> 60.1 us  [dot_nn(): lax.dot_general(a, b, (((1,), (0,)), ((), ())), preferred_element_type=F32)]
  transfers between devices with their start and end apart: 28 -> 29, of which waited for: 7 -> 9; matrix products, arithmetic and copies ran while one was open for 4% -> 0% of each run, Pallas kernels for 63% -> 63%
where the time goes in v5:
time: 1740 us; the launch traced here: 1730 us
  Pallas kernels  1270 us (73%)
  waiting for transfers between devices  368 us (21%)
  matrix products  60.1 us (3%)
    pallas_call x23, Pallas kernels, run(): pl.pallas_call(kernel, grid_spec=spec, out_shape=out_shape, input_output_...  1270 us
    ppermute x8, waiting for transfers between devices, to_chip(): return lax.ppermute(x, 'tp', chip_flip)  336 us
    dot_general x1, matrix products, dot_nn(): lax.dot_general(a, b, (((1,), (0,)), ((), ())), preferred_element_type=F32)  60.1 us
  transfers between devices with their start and end apart: 29, of which 9 were waited for; matrix products, arithmetic and copies ran while one was open for 0% of the time, Pallas kernels for 63%

profile of v5, /device:TPU:0, one launch (start us, length us, event | category | flops | bytes accessed | tf_op | source)
XLA Modules:
  0.0 1730.0 jit_solution(16266655550218740290)
XLA Ops:
  7.2 0.9 collective-permute-start.5
  8.1 2.9 collective-permute-start.1
  11.1 1.3 convert_add_fusion.1
  12.4 8.2 shard_map.230
  20.6 33.3 %shard_map.231 = (bf16[2,768,4096]{2,1,0:T(8,128)(2,1)}, bf16[2,2,3,256,2048]{4,3,2,1,0:T(8,128)(2,1)}, bf16[2,2,3,256,2048]{4,3,2,1,0:T(8,128)(2,1)}, bf16[3,25...) custom-call(s32[1]{0:T(128)} %bitcast.me_ref.refs_0_, bf16[6,256,2048]{2,1,0:T(8,128)(2,1)} %go_ref.1, ...), custom_call_target="tpu_custom_call" | custom-call | flops 25769803776 | bytes 29360128 | tf_op jit(solution)/shard_map/pallas_call | solution.py:39
  53.9 3.9 collective-permute-done.1.x_ref
  57.9 33.3 %shard_map.232 = (bf16[2,768,4096]{2,1,0:T(8,128)(2,1)}, bf16[2,2,3,256,2048]{4,3,2,1,0:T(8,128)(2,1)}, bf16[2,2,3,256,2048]{4,3,2,1,0:T(8,128)(2,1)}) custom-call(s32[1]{0:T(128)} %bitcast.me_ref.refs_0_, bf16[6,256,2048]{2,1,0:T(8,128)(2,1)} %collective-permute-done.5.refs_0_, ...), custom_call_target="tpu_custom_call", output_to_operand_aliasing={{1}: (3, {}), {2}: (4, {})} | custom-call | flops 25769803776 | bytes 29360128 | tf_op jit(solution)/shard_map/pallas_call | solution.py:39
  91.2 0.5 collective-permute-start.6
  91.7 2.0 collective-permute-start.8
  93.8 1.3 collective-permute-done.6.k3_ref
  95.1 44.8 %shard_map.233 = (bf16[6,256,2048]{2,1,0:T(8,128)(2,1)}, bf16[6,1024,2048]{2,1,0:T(8,128)(2,1)}, bf16[6,256,2048]{2,1,0:T(8,128)(2,1)}) custom-call(s32[1]{0:T(128)} %bitcast.me_ref.refs_0_, s32[6]{0:T(128)} %pre_ref.1, s32[6]{0:T(128)} %val_ref.1, bf16[6,256,2048]{2,1,0:T(8,128)(2,1)} %get-tuple-element.62.u_ref, bf16[2048,512]{1,0:T(8,128)(2,1)} %w0_ref.9, ...), custom_call_target="tpu_custom_call" | custom-call | flops 25769803776 | bytes 25165824 | tf_op jit(solution)/shard_map/pallas_call | solution.py:39
  139.8 0.5 collective-permute-done.8.x_ref
  140.5 0.6 convert_add_fusion
  141.1 3.7 collective-permute-done.9.w3_ref
  144.9 14.4 shard_map.234
  159.4 1.8 collective-permute-start.14
  161.5 14.4 shard_map.235
  175.9 63.9 %shard_map.236 = (bf16[2,2,768,4096]{3,2,1,0:T(8,128)(2,1)}, bf16[2,2,768,4096]{3,2,1,0:T(8,128)(2,1)}, bf16[2,2,768,4096]{3,2,1,0:T(8,128)(2,1)}, bf16[2,2,3,256,2048]{4,3,2,1,0:T(8,128)(2,1)}) custom-call(s32[1]{0:T(128)} %bitcast.me_ref.refs_0_, bf16[3,256,2048]{2,1,0:T(8,128)(2,1)} %get-tuple-element.69.refs_0_, ...), custom_call_target="tpu_custom_call" | custom-call | flops 51539607552 | bytes 83886080 | tf_op jit(solution)/shard_map/pallas_call | solution.py:39
  239.8 0.5 collective-permute-start.15
  240.3 64.1 %shard_map.237 = (bf16[2,2,768,4096]{3,2,1,0:T(8,128)(2,1)}, bf16[2,2,768,4096]{3,2,1,0:T(8,128)(2,1)}, bf16[2,2,768,4096]{3,2,1,0:T(8,128)(2,1)}, bf16[2,2,3,256,2048]{4,3,2,1,0:T(8,128)(2,1)}) custom-call(s32[1]{0:T(128)} %bitcast.me_ref.refs_0_, bf16[3,256,2048]{2,1,0:T(8,128)(2,1)} %get-tuple-element.71.refs_6_.refs_0_.rest_0_, ...), custom_call_target="tpu_custom_call" | custom-call | flops 51539607552 | bytes 83886080 | tf_op jit(solution)/shard_map/pallas_call | solution.py:39
  304.4 33.3 %shard_map.238 = (bf16[2,768,4096]{2,1,0:T(8,128)(2,1)}, bf16[2,2,3,256,2048]{4,3,2,1,0:T(8,128)(2,1)}) custom-call(s32[1]{0:T(128)} %bitcast.me_ref.refs_0_, bf16[3,256,2048]{2,1,0:T(8,128)(2,1)} %tie.14.refs_0_, bf16[3,256,2048]{2,1,0:T(8,128)(2,1)} %collective-permute-done.15.refs_1_, bf16[4096,2048]{1,0:T(8,128)(2,1)} %wd_ref.3, ...), custom_call_target="tpu_custom_call", output_to_operand_aliasing={{1}: (4, {})} | custom-call | flops 25769803776 | bytes 29360128 | tf_op jit(solution)/shard_map/pallas_call | solution.py:39
  337.7 64.2 %shard_map.239 = (bf16[2,2,768,4096]{3,2,1,0:T(8,128)(2,1)}, bf16[2,2,768,4096]{3,2,1,0:T(8,128)(2,1)}, bf16[2,2,768,4096]{3,2,1,0:T(8,128)(2,1)}, bf16[2,2,3,256,2048]{4,3,2,1,0:T(8,128)(2,1)}) custom-call(s32[1]{0:T(128)} %bitcast.me_ref.refs_0_, ...), custom_call_target="tpu_custom_call", output_to_operand_aliasing={{0}: (7, {}), {1}: (8, {}), {2}: (9, {}), {3}: (10, {})} | custom-call | flops 51539607552 | bytes 83886080 | tf_op jit(solution)/shard_map/pallas_call | solution.py:39
  402.0 60.1 %convolution_convert_fusion.refs_13_ = bf16[3072,2048]{1,0:T(8,128)(2,1)} fusion(bf16[3072,4096]{1,0:T(8,128)(2,1)} %bitcast.32, bf16[4096,2048]{1,0:T(8,128)(2,1)} %wd_ref.3), kind=kOutput, calls=%fused_computation | convolution fusion | flops 51545899008 | bytes 54525952 | tf_op jit(solution)/shard_map/dot_general | solution.py:21
  462.3 118.8 %shard_map.240.refs_12_ = bf16[4,768,2048]{2,1,0:T(8,128)(2,1)} custom-call(bf16[2,2,768,4096]{3,2,1,0:T(8,128)(2,1)} %get-tuple-element.87.dg_ref, bf16[2,2,768,4096]{3,2,1,0:T(8,128)(2,1)} %get-tuple-element.88.du_ref, bf16[2048,4096]{1,0:T(8,128)(2,1)} %wg_ref.3, bf16[2048,4096]{1,0:T(8,128)(2,1)} %wu_ref.3, ...), custom_call_target="tpu_custom_call" | custom-call | flops 103079215104 | bytes 50331648 | tf_op jit(solution)/shard_map/pallas_call | solution.py:39
  581.4 1.6 copy-done
  583.0 1.1 collective-permute-start.16
  584.1 0.9 collective-permute-start.18
  585.1 115.4 %collective-permute-done.16.x_ref = bf16[3,256,2048]{2,1,0:T(8,128)(2,1)} collective-permute-done((bf16[3,256,2048]{2,1,0:T(8,128)(2,1)S(1)}, bf16[3,256,2048]{2,1,0:T(8,128)(2,1)}, u32[]{:S(2)}, u32[]{:S(2)}) %collective-permute-start.16) | collective-permute-done | bytes 3145760 | tf_op jit(solution)/shard_map/ppermute | solution.py:673
  700.5 88.1 %collective-permute-done.18.x_ref = bf16[3,256,2048]{2,1,0:T(8,128)(2,1)} collective-permute-done((bf16[3,256,2048]{2,1,0:T(8,128)(2,1)}, bf16[3,256,2048]{2,1,0:T(8,128)(2,1)}, u32[]{:S(2)}, u32[]{:S(2)}) %collective-permute-start.18) | collective-permute-done | bytes 3145760 | tf_op jit(solution)/shard_map/ppermute | solution.py:673
  788.6 6.0 collective-permute-done.19.refs_3_
  794.6 92.9 %shard_map.241 = (bf16[2,2,768,4096]{3,2,1,0:T(8,128)(2,1)}, bf16[2,2,768,4096]{3,2,1,0:T(8,128)(2,1)}, bf16[2,2,768,4096]{3,2,1,0:T(8,128)(2,1)}, bf16[2,2,3,25...) custom-call(s32[1]{0:T(128)} %bitcast.me_ref.refs_0_, ...), custom_call_target="tpu_custom_call", output_to_operand_aliasing={{0}: (8, {}), {1}: (9, {}), {2}: (10, {}), {3}: (11, {}), {... | custom-call | flops 77309411328 | bytes 83886080 | tf_op jit(solution)/shard_map/pallas_call | solution.py:39
  887.5 115.3 %shard_map.242.refs_0_ = bf16[4,768,2048]{2,1,0:T(8,128)(2,1)} custom-call(bf16[2,2,768,4096]{3,2,1,0:T(8,128)(2,1)} %get-tuple-element.90.dg_ref, bf16[2,2,768,4096]{3,2,1,0:T(8,128)(2,1)} %get-tuple-element.91.du_ref, bf16[2048,4096]{1,0:T(8,128)(2,1)} %wg_ref.3, bf16[2048,4096]{1,0:T(8,128)(2,1)} %wu_ref.3, ...), custom_call_target="tpu_custom_call" | custom-call | flops 103079215104 | bytes 50331648 | tf_op jit(solution)/shard_map/pallas_call | solution.py:39
  1003.0 36.6 %shard_map.243.refs_4_ = bf16[2,768,2048]{2,1,0:T(8,128)(2,1)} custom-call(s32[1]{0:T(128)} %bitcast.me_ref.refs_0_, bf16[2,2,768,4096]{3,2,1,0:T(8,128)(2,1)} %get-tuple-element.93.rest_0_.act_ref, bf16[4096,2048]{1,0:T(8,128)(2,1)} %wd_ref.3, bf16[4,768,2048]{2,1,0:T(8,128)(2,1)} %shard_map.242.refs_0_), custom_call_target="tpu_custom_call" | custom-call | flops 25769803776 | bytes 16777216 | tf_op jit(solution)/shard_map/pallas_call | solution.py:39
  1039.7 35.6 %shard_map.244.refs_1_.token1_ref.refs_4_ = f32[4096,2048]{1,0:T(8,128)} custom-call(bf16[3072,4096]{1,0:T(8,128)(2,1)} %bitcast.33, bf16[3072,4096]{1,0:T(8,128)(2,1)} %bitcast.35, bf16[3072,2048]{1,0:T(8,128)(2,1)} %bitcast.40, bf16[3072,2048]{1,0:T(8,128)(2,1)} %bitcast.42, bf16[2,768,2048]{2,1,0:T(8,128)(2,1)} %shard_map.243.refs_4_), custom_call_target="tpu_custom_call" | custom-call | flops 25769803776 | bytes 33554432 | tf_op jit(solution)/shard_map/pallas_call | solution.py:39
  1075.3 37.5 %shard_map.245 = (bf16[768,2048]{1,0:T(8,128)(2,1)}, bf16[768,2048]{1,0:T(8,128)(2,1)}) custom-call(s32[1]{0:T(128)} %bitcast.me_ref.refs_0_, bf16[2,2,768,4096]{3,2,1,0:T(8,128)(2,1)} %get-tuple-element.93.rest_0_.act_ref, bf16[4096,2048]{1,0:T(8,128)(2,1)} %wd_ref.3, bf16[2,768,2048]{2,1,0:T(8,128)(2,1)} %collective-permute-done.20.refs_0_, ...), custom_call_target="tpu_custom_call" | custom-call | flops 25769803776 | bytes 16777216 | tf_op jit(solution)/shard_map/pallas_call | solution.py:39
  1112.9 61.3 %shard_map.246 = (bf16[6,256,2048]{2,1,0:T(8,128)(2,1)}, bf16[6,256,2048]{2,1,0:T(8,128)(2,1)}, bf16[4,6,256,512]{3,2,1,0:T(8,128)(2,1)}, f32[1,2048]{1,0:T(1,128)}) custom-call(s32[1]{0:T(128)} %bitcast.me_ref.refs_0_, bf16[3,256,2048]{2,1,0:T(8,128)(2,1)} %bitcast.57, bf16[3,256,2048]{2,1,0:T(8,128)(2,1)} %bitcast.58, ...), custom_call_target="tpu_custom_call" | custom-call | flops 38654705664 | bytes 25165824 | tf_op jit(solution)/shard_map/pallas_call | solution.py:39
  1174.3 19.9 %shard_map.247.refs_3_ = f32[4,512,2048]{2,1,0:T(8,128)} custom-call(s32[1]{0:T(128)} %bitcast.me_ref.refs_0_, bf16[1536,2048]{1,0:T(8,128)(2,1)} %bitcast.37, bf16[1536,2048]{1,0:T(8,128)(2,1)} %bitcast.46, bf16[4,6,256,512]{3,2,1,0:T(8,128)(2,1)} %get-tuple-element.100.refs_3_), custom_call_target="tpu_custom_call" | custom-call | flops 12884901888 | bytes 16777216 | tf_op jit(solution)/shard_map/pallas_call | solution.py:39
  1194.2 19.3 %shard_map.248.refs_5_ = f32[4,2048,512]{2,1,0:T(8,128)} custom-call(s32[1]{0:T(128)} %bitcast.me_ref.refs_0_, bf16[1536,2048]{1,0:T(8,128)(2,1)} %bitcast.45, bf16[1536,2048]{1,0:T(8,128)(2,1)} %bitcast.47, f32[4,512,2048]{2,1,0:T(8,128)} %shard_map.247.refs_3_), custom_call_target="tpu_custom_call" | custom-call | flops 12884901888 | bytes 16777216 | tf_op jit(solution)/shard_map/pallas_call | solution.py:39
  1213.5 88.4 %shard_map.249.token0_ref = f32[4096,2048]{1,0:T(8,128)} custom-call(bf16[3072,4096]{1,0:T(8,128)(2,1)} %bitcast.34, bf16[3072,4096]{1,0:T(8,128)(2,1)} %bitcast.36, bf16[3072,2048]{1,0:T(8,128)(2,1)} %bitcast.41, bf16[3072,2048]{1,0:T(8,128)(2,1)} %bitcast.43, f32[4096,2048]{1,0:T(8,128)} %shard_map.244.refs_1_.token1_ref.refs_4_, ...), custom_call_target="tpu_custom_call", output_to_operand_aliasing={{}: (4, {})} | custom-call | flops 77309411328 | bytes 33554432 | tf_op jit(solution)/shard_map/pallas_call | solution.py:39
  1301.9 35.9 %shard_map.250 = (bf16[6,256,2048]{2,1,0:T(8,128)(2,1)}, f32[2056,512]{1,0:T(8,128)}) custom-call(s32[1]{0:T(128)} %bitcast.me_ref.refs_0_, bf16[6,256,512]{2,1,0:T(8,128)(2,1)} %bitcast.49, bf16[6,256,2048]{2,1,0:T(8,128)(2,1)} %get-tuple-element.101.dq_ref, bf16[6,256,2048]{2,1,0:T(8,128)(2,1)} %get-tuple-element.62.u_ref, bf16[6,256,2048]{2,1,0:T(8,128)(2,1)} %h_ref.7, ...), custom_call_target="tpu_custom_call" | custom-call | flops 19327352832 | bytes 25165824 | tf_op jit(solution)/shard_map/pallas_call | solution.py:39
  1337.9 0.5 reduce-scatter.15.cloned.1.call-update
  1338.7 0.4 reduce-scatter.17.cloned.1.call-update
  1339.2 2.0 copy-done.2
  1341.2 127.9 %collective-permute-done.21.refs_9_ = bf16[768,2048]{1,0:T(8,128)(2,1)S(1)} collective-permute-done((bf16[768,2048]{1,0:T(8,128)(2,1)S(1)}, bf16[768,2048]{1,0:T(8,128)(2,1)S(1)}, u32[]{:S(2)}, u32[]{:S(2)}) %collective-permute-start.21) | collective-permute-done | bytes 3145760 | tf_op jit(solution)/shard_map/ppermute | solution.py:673
  1469.1 1.7 copy-done.3
  1470.8 227.9 %shard_map.251 = (f32[2048,4096]{1,0:T(8,128)}, f32[2048,4096]{1,0:T(8,128)}, bf16[1536,2048]{1,0:T(8,128)(2,1)}) custom-call(bf16[3072,2048]{1,0:T(8,128)(2,1)} %bitcast.66, bf16[3072,2048]{1,0:T(8,128)(2,1)} %bitcast.65, bf16[3072,4096]{1,0:T(8,128)(2,1)} %bitcast.63, bf16[3072,4096]{1,0:T(8,128)(2,1)} %bitcast.61, bf16[3072,4096]{1,0:T(8,128)(2,1)} %bitcast.64, ...), custom_call_target="tpu_custom_call" | custom-call | flops 206158430208 | bytes 33554432 | tf_op jit(solution)/shard_map/pallas_call | solution.py:39
  1698.7 4.5 shard_map.252
  1703.2 19.5 %reduce-scatter.17.cloned.1.call-done = f32[512,2048]{1,0:T(8,128)} async-done(((f32[2048,2048]{1,0:T(8,128)}), f32[512,2048]{1,0:T(8,128)}) %reduce-scatter.17.cloned.1.call-update) | async-done | bytes 4194320 | tf_op jit(solution)/shard_map/reduce_scatter | solution.py:889
  (60 shorter events, 2.1 us)
Async XLA Ops:
  7.2 1105.7 %reduce-scatter.19.cloned.1.call-start = ((), (), s32[]{:S(2)}) async-start(), calls=%async_computation.9 | async-start | bytes 15728640
  7.2 50.6 %collective-permute-start.5 = (bf16[6,256,2048]{2,1,0:T(8,128)(2,1)}, bf16[6,256,2048]{2,1,0:T(8,128)(2,1)}, u32[]{:S(2)}, u32[]{:S(2)}) collective-permute-start(bf16[6,256,2048]{2,1,0:T(8,128)(2,1)} %go_ref.1), channel_id=1, source_target_pairs={{0,1},{1,0},{2,3},{3,2},{4,5},{5,4},{6,7},{7,6}} | collective-permute-start | bytes 18874376 | tf_op jit(solution)/shard_map/ppermute | solution.py:670
  8.1 85.7 %collective-permute-start = (bf16[2048,512]{1,0:T(8,128)(2,1)}, bf16[2048,512]{1,0:T(8,128)(2,1)}, u32[]{:S(2)}, u32[]{:S(2)}) collective-permute-start(bf16[2048,512]{1,0:T(8,128)(2,1)} %w0_ref.9), channel_id=1, source_target_pairs={{0,1},{1,0},{2,3},{3,2},{4,5},{5,4},{6,7},{7,6}} | collective-permute-start | bytes 6291464 | tf_op jit(solution)/shard_map/ppermute | solution.py:670
  8.1 49.7 %collective-permute-start.1 = (bf16[2048,512]{1,0:T(8,128)(2,1)}, bf16[2048,512]{1,0:T(8,128)(2,1)}, u32[]{:S(2)}, u32[]{:S(2)}) collective-permute-start(bf16[2048,512]{1,0:T(8,128)(2,1)} %w0_ref.9), channel_id=1, source_target_pairs={{0,2},{2,0},{1,3},{3,1},{4,6},{6,4},{5,7},{7,5}} | collective-permute-start | bytes 6291464 | tf_op jit(solution)/shard_map/ppermute | solution.py:673
  20.6 71.1 %collective-permute-start.3 = (bf16[6,256,512]{2,1,0:T(8,128)(2,1)}, bf16[6,256,512]{2,1,0:T(8,128)(2,1)}, u32[]{:S(2)}, u32[]{:S(2)}) collective-permute-start(bf16[6,256,512]{2,1,0:T(8,128)(2,1)} %get-tuple-element.63.refs_2_.k0_ref), channel_id=1, source_target_pairs={{0,1},{1,0},{2,3},{3,2},{4,5},{5,4},{6,7},{7,6}} | collective-permute-start | bytes 4718600 | tf_op jit(solution)/shard_map/ppermute | solution.py:670
  20.6 70.6 %collective-permute-start.4 = (bf16[6,256,512]{2,1,0:T(8,128)(2,1)}, bf16[6,256,512]{2,1,0:T(8,128)(2,1)}, u32[]{:S(2)}, u32[]{:S(2)}) collective-permute-start(bf16[6,256,512]{2,1,0:T(8,128)(2,1)} %get-tuple-element.63.refs_2_.k0_ref), channel_id=1, source_target_pairs={{0,2},{2,0},{1,3},{3,1},{4,6},{6,4},{5,7},{7,5}} | collective-permute-start | bytes 4718600 | tf_op jit(solution)/shard_map/ppermute | solution.py:673
  57.9 35.9 %collective-permute-start.2 = (bf16[2048,512]{1,0:T(8,128)(2,1)}, bf16[2048,512]{1,0:T(8,128)(2,1)}, u32[]{:S(2)}, u32[]{:S(2)}) collective-permute-start(bf16[2048,512]{1,0:T(8,128)(2,1)} %tie.9.w2_ref), channel_id=1, source_target_pairs={{0,1},{1,0},{2,3},{3,2},{4,5},{5,4},{6,7},{7,6}} | collective-permute-start | bytes 6291464 | tf_op jit(solution)/shard_map/ppermute | solution.py:670
  91.2 3.9 collective-permute-start.6
  91.7 49.4 %collective-permute-start.7 = (bf16[512,2048]{1,0:T(8,128)(2,1)}, bf16[512,2048]{1,0:T(8,128)(2,1)}, u32[]{:S(2)}, u32[]{:S(2)}) collective-permute-start(bf16[512,2048]{1,0:T(8,128)(2,1)} %w0_ref.8), channel_id=1, source_target_pairs={{0,1},{1,0},{2,3},{3,2},{4,5},{5,4},{6,7},{7,6}} | collective-permute-start | bytes 6291464 | tf_op jit(solution)/shard_map/ppermute | solution.py:670
  91.7 48.6 %collective-permute-start.8 = (bf16[512,2048]{1,0:T(8,128)(2,1)}, bf16[512,2048]{1,0:T(8,128)(2,1)}, u32[]{:S(2)}, u32[]{:S(2)}) collective-permute-start(bf16[512,2048]{1,0:T(8,128)(2,1)} %w0_ref.8), channel_id=1, source_target_pairs={{0,2},{2,0},{1,3},{3,1},{4,6},{6,4},{5,7},{7,5}} | collective-permute-start | bytes 6291464 | tf_op jit(solution)/shard_map/ppermute | solution.py:673
  139.8 0.7 copy-start.1
  140.4 4.5 collective-permute-start.9
  159.3 16.6 collective-permute-start.12
  159.4 80.4 %collective-permute-start.14 = (bf16[3,256,2048]{2,1,0:T(8,128)(2,1)}, bf16[3,256,2048]{2,1,0:T(8,128)(2,1)}, u32[]{:S(2)}, u32[]{:S(2)}) collective-permute-start(bf16[3,256,2048]{2,1,0:T(8,128)(2,1)} %tie.13), channel_id=1, source_target_pairs={{0,2},{2,0},{1,3},{3,1},{4,6},{6,4},{5,7},{7,5}} | collective-permute-start | bytes 9437192 | tf_op jit(solution)/shard_map/ppermute | solution.py:673
  161.2 143.1 %collective-permute-start.10 = (bf16[3,256,2048]{2,1,0:T(8,128)(2,1)}, bf16[3,256,2048]{2,1,0:T(8,128)(2,1)}, u32[]{:S(2)}, u32[]{:S(2)}) collective-permute-start(bf16[3,256,2048]{2,1,0:T(8,128)(2,1)} %get-tuple-element.69.refs_0_), channel_id=1, source_target_pairs={{0,2},{2,0},{1,3},{3,1},{4,6},{6,4},{5,7},{7,5}} | collective-permute-start | bytes 9437192 | tf_op jit(solution)/shard_map/ppermute | solution.py:673
  175.9 64.4 %collective-permute-start.11 = (bf16[3,256,2048]{2,1,0:T(8,128)(2,1)}, bf16[3,256,2048]{2,1,0:T(8,128)(2,1)}, u32[]{:S(2)}, u32[]{:S(2)}) collective-permute-start(bf16[3,256,2048]{2,1,0:T(8,128)(2,1)} %get-tuple-element.71.refs_6_.refs_0_.rest_0_), channel_id=1, source_target_pairs={{0,1},{1,0},{2,3},{3,2},{4,5},{5,4},{6,7},{7,6}} | collective-permute-start | bytes 9437192 | tf_op jit(solution)/shard_map/ppermute | solution.py:670
  239.8 64.6 %collective-permute-start.15 = (bf16[3,256,2048]{2,1,0:T(8,128)(2,1)}, bf16[3,256,2048]{2,1,0:T(8,128)(2,1)}, u32[]{:S(2)}, u32[]{:S(2)}) collective-permute-start(bf16[3,256,2048]{2,1,0:T(8,128)(2,1)} %tie.14.refs_0_), channel_id=1, source_target_pairs={{0,1},{1,0},{2,3},{3,2},{4,5},{5,4},{6,7},{7,6}} | collective-permute-start | bytes 9437192 | tf_op jit(solution)/shard_map/ppermute | solution.py:670
  304.4 33.3 %collective-permute-start.13 = (bf16[3,256,2048]{2,1,0:T(8,128)(2,1)}, bf16[3,256,2048]{2,1,0:T(8,128)(2,1)}, u32[]{:S(2)}, u32[]{:S(2)}) collective-permute-start(bf16[3,256,2048]{2,1,0:T(8,128)(2,1)} %tie.12.refs_0_), channel_id=1, source_target_pairs={{0,1},{1,0},{2,3},{3,2},{4,5},{5,4},{6,7},{7,6}} | collective-permute-start | bytes 9437192 | tf_op jit(solution)/shard_map/ppermute | solution.py:670
  462.1 650.8 %reduce-scatter.21.cloned.1.call-start = ((), (), s32[]{:S(2)}) async-start(), calls=%async_computation.10 | async-start | bytes 15728640
  581.1 1.9 copy-start
  581.2 531.7 %reduce-scatter.23.cloned.1.call-start = ((), (), s32[]{:S(2)}) async-start(), calls=%async_computation.11 | async-start | bytes 15728640
  583.0 117.4 %collective-permute-start.16 = (bf16[3,256,2048]{2,1,0:T(8,128)(2,1)S(1)}, bf16[3,256,2048]{2,1,0:T(8,128)(2,1)}, u32[]{:S(2)}, u32[]{:S(2)}) collective-permute-start(bf16[3,256,2048]{2,1,0:T(8,128)(2,1)S(1)} %copy-done), channel_id=1, source_target_pairs={{0,2},{2,0},{1,3},{3,1},{4,6},{6,4},{5,7},{7,5}} | collective-permute-start | bytes 9437192 | tf_op jit(solution)/shard_map/ppermute | solution.py:673
  584.1 204.5 %collective-permute-start.18 = (bf16[3,256,2048]{2,1,0:T(8,128)(2,1)}, bf16[3,256,2048]{2,1,0:T(8,128)(2,1)}, u32[]{:S(2)}, u32[]{:S(2)}) collective-permute-start(bf16[3,256,2048]{2,1,0:T(8,128)(2,1)} %tie.16), channel_id=1, source_target_pairs={{0,2},{2,0},{1,3},{3,1},{4,6},{6,4},{5,7},{7,5}} | collective-permute-start | bytes 9437192 | tf_op jit(solution)/shard_map/ppermute | solution.py:673
  700.5 88.1 %collective-permute-start.17 = (bf16[3,256,2048]{2,1,0:T(8,128)(2,1)}, bf16[3,256,2048]{2,1,0:T(8,128)(2,1)}, u32[]{:S(2)}, u32[]{:S(2)}) collective-permute-start(bf16[3,256,2048]{2,1,0:T(8,128)(2,1)} %tie.15.refs_0_), channel_id=1, source_target_pairs={{0,1},{1,0},{2,3},{3,2},{4,5},{5,4},{6,7},{7,6}} | collective-permute-start | bytes 9437192 | tf_op jit(solution)/shard_map/ppermute | solution.py:670
  788.6 6.0 collective-permute-start.19
  1002.8 299.1 %reduce-scatter.25.cloned.1.call-start = ((), (), s32[]{:S(2)}) async-start(), calls=%async_computation.12 | async-start | bytes 7864320
  1039.6 35.7 %collective-permute-start.20 = (bf16[2,768,2048]{2,1,0:T(8,128)(2,1)}, bf16[2,768,2048]{2,1,0:T(8,128)(2,1)}, u32[]{:S(2)}, u32[]{:S(2)}) collective-permute-start(bf16[2,768,2048]{2,1,0:T(8,128)(2,1)} %shard_map.243.refs_4_), channel_id=1, source_target_pairs={{0,1},{1,0},{2,3},{3,2},{4,5},{5,4},{6,7},{7,6}} | collective-permute-start | bytes 18874376 | tf_op jit(solution)/shard_map/ppermute | solution.py:670
  1174.2 524.5 %all-reduce.6.cloned.1.call-start = ((), (), s32[]{:S(2)}) async-start(), calls=%async_computation.6 | async-start | bytes 8421376 | tf_op jit(solution)/shard_map/psum | solution.py:906
  1337.8 365.4 %reduce-scatter.15.cloned.1.call-start = ((), (), s32[]{:S(2)}) async-start(), calls=%async_computation.7 | async-start | bytes 20971520 | tf_op jit(solution)/shard_map/reduce_scatter | solution.py:894
  1338.4 384.3 %reduce-scatter.17.cloned.1.call-start = ((), (), s32[]{:S(2)}) async-start(), calls=%async_computation.8 | async-start | bytes 20971520 | tf_op jit(solution)/shard_map/reduce_scatter | solution.py:889
  1338.7 2.5 copy-start.2
  1341.2 127.9 %collective-permute-start.21 = (bf16[768,2048]{1,0:T(8,128)(2,1)S(1)}, bf16[768,2048]{1,0:T(8,128)(2,1)S(1)}, u32[]{:S(2)}, u32[]{:S(2)}) collective-permute-start(bf16[768,2048]{1,0:T(8,128)(2,1)S(1)} %copy-done.2), channel_id=1, source_target_pairs={{0,2},{2,0},{1,3},{3,1},{4,6},{6,4},{5,7},{7,5}} | collective-permute-start | bytes 9437192 | tf_op jit(solution)/shard_map/ppermute | solution.py:673
  1469.1 1.7 copy-start.3
Sparse Core Ops, SparseCore 0:
  462.2 95.7 reduce-scatter.18
  581.3 162.9 reduce-scatter.20
  1002.9 95.1 reduce-scatter.22
  1174.4 53.6 reduce-scatter.24
  1338.0 139.7 all-reduce.5
  1480.7 119.3 reduce-scatter.14
  1603.2 119.4 reduce-scatter.16
